TPU v7x, 8 devices: a whole 2x2x1 slice. The times are simulated.
8 devices in a mesh: dp: 1 (over z), etp: 2 (over y), ep: 4 (over x, core).
Axes of the slice: x: 2, y: 2, z: 1, core: 2. Of those that a mesh axis runs over, the one named last changes fastest.
Arguments:
- x_in: bfloat16 [512, 1024], P(('dp', 'ep'))
- y_grad: bfloat16 [512, 1024], P(('dp', 'ep'))
- prim_exp: int32 [512], P(('dp', 'ep'))
- alt_exp: int32 [512], P(('dp', 'ep'))
- w_router: bfloat16 [1024, 32], replicated
- exp_gate: bfloat16 [32, 1024, 512], P('ep', None, 'etp')
- exp_up: bfloat16 [32, 1024, 512], P('ep', None, 'etp')
- exp_down: bfloat16 [32, 512, 1024], P('ep', 'etp')
- sh_gate: bfloat16 [1024, 512], P(None, 'etp')
- sh_up: bfloat16 [1024, 512], P(None, 'etp')
- sh_down: bfloat16 [512, 1024], P('etp')
Outputs:
- output 1: bfloat16 [512, 1024], P(('dp', 'ep'))
- output 2: bfloat16 [512, 1024], P(('dp', 'ep'))
- output 3: float32 [32, 1024, 512], P(('dp', 'ep'), None, 'etp')
- output 4: float32 [32, 1024, 512], P(('dp', 'ep'), None, 'etp')
- output 5: float32 [32, 512, 1024], P(('dp', 'ep'), 'etp')
- output 6: float32 [1024, 512], P('dp', 'etp')
- output 7: float32 [1024, 512], P('dp', 'etp')
- output 8: float32 [512, 1024], P(('dp', 'etp'))
- output 9: float32 [1024, 32], P('dp')
All inputs are finite; a program needn't handle non-finite values.
Results may differ from a plain program's by a relative error of at most 0.001.
Values are sent between devices in bfloat16 or wider.
A program may use at most 1 GiB of HBM per device.

v0:
```python
import jax
import jax.numpy as jnp
from jax import lax
from jax.sharding import PartitionSpec as P

EPS = 1e-5
F32 = jnp.float32
BF16 = jnp.bfloat16


def exclusive_rank(onehot):
    return jnp.sum((jnp.cumsum(onehot, axis=0) - onehot) * onehot, axis=1)


def glu_grads(d_hidden, act_gate, act_up):
    sig_gate = jax.nn.sigmoid(act_gate)
    d_gate = (d_hidden * act_up * sig_gate * (1.0 + act_gate * (1.0 - sig_gate))).astype(BF16)
    d_up = (d_hidden * act_gate * sig_gate).astype(BF16)
    return d_gate, d_up


def solution(mesh):
    ep_size = mesh.shape["ep"]
    tok_spec = P(("dp", "ep"), None)
    id_spec = P(("dp", "ep"))
    in_specs = (tok_spec, tok_spec, id_spec, id_spec, P(None, None), P("ep", None, "etp"), P("ep", None, "etp"), P("ep", "etp", None), P(None, "etp"), P(None, "etp"), P("etp", None))
    out_specs = (tok_spec, tok_spec, P(("dp", "ep"), None, "etp"), P(("dp", "ep"), None, "etp"), P(("dp", "ep"), "etp", None), P("dp", "etp"), P("dp", "etp"), P(("dp", "etp"), None), P("dp", None))

    def local_step(x_in, y_grad, prim_exp, alt_exp, w_router, exp_gate, exp_up, exp_down, sh_gate, sh_up, sh_down):
        tok_local, model_dim = x_in.shape
        num_exp = w_router.shape[1]
        local_exp = exp_gate.shape[0]
        capacity = 5 * tok_local * ep_size // (4 * num_exp)
        my_rank = lax.axis_index("ep")
        expert_ids = jnp.arange(num_exp)
        earlier = (jnp.arange(ep_size) < my_rank).astype(jnp.int32)[:, None]
        x_wide = x_in.astype(F32)
        inv_rms = lax.rsqrt(jnp.mean(x_wide * x_wide, axis=1, keepdims=True) + EPS)
        normed = (x_wide * inv_rms).astype(BF16)
        gate_probs = jax.nn.softmax(jnp.dot(normed, w_router, preferred_element_type=F32), axis=1)
        one_prim = (prim_exp[:, None] == expert_ids[None, :]).astype(jnp.int32)
        prim_counts = lax.all_gather(jnp.sum(one_prim, axis=0), "ep")
        rank_prim = exclusive_rank(one_prim) + jnp.sum(one_prim * jnp.sum(prim_counts * earlier, axis=0)[None, :], axis=1)
        keep_prim = rank_prim < capacity
        kept_count = jnp.minimum(jnp.sum(prim_counts, axis=0), capacity)
        overflow = jnp.logical_not(keep_prim).astype(jnp.int32)
        one_alt = (alt_exp[:, None] == expert_ids[None, :]).astype(jnp.int32) * overflow[:, None]
        alt_counts = lax.all_gather(jnp.sum(one_alt, axis=0), "ep")
        alt_base = kept_count + jnp.sum(alt_counts * earlier, axis=0)
        slot_alt = exclusive_rank(one_alt) + jnp.sum(one_alt * alt_base[None, :], axis=1)
        keep_alt = (overflow == 1) & (slot_alt < capacity)
        assign = jnp.where(keep_prim, prim_exp, jnp.where(keep_alt, alt_exp, -1))
        slot_idx = jnp.where(keep_prim, rank_prim, slot_alt)
        owner_rank = jnp.where(assign >= 0, assign // local_exp, -1)
        to_owner = (owner_rank[None, :] == jnp.arange(ep_size)[:, None])[:, :, None]
        total_rows = ep_size * tok_local
        all_assign = lax.all_gather(assign, "ep", tiled=True)
        all_slot = lax.all_gather(slot_idx, "ep", tiled=True)
        mine_rows = (all_assign >= 0) & (all_assign // local_exp == my_rank)
        target = jnp.where(mine_rows, (all_assign - my_rank * local_exp) * capacity + all_slot, local_exp * capacity)
        slot_table = jnp.full((local_exp * capacity + 1,), total_rows, jnp.int32).at[target].set(jnp.arange(total_rows, dtype=jnp.int32))[: local_exp * capacity]

        def send_out(tok_rows):
            sent_rows = jnp.where(to_owner, tok_rows[None], 0)
            recv_rows = lax.all_to_all(sent_rows, "ep", 0, 0, tiled=True).reshape(total_rows, model_dim)
            return jnp.take(recv_rows, slot_table, axis=0, mode="fill", fill_value=0).reshape(local_exp, capacity, model_dim)

        def send_back(slot_rows):
            flat_rows = jnp.take(slot_rows.reshape(local_exp * capacity, model_dim), target, axis=0, mode="fill", fill_value=0)
            back_rows = lax.all_to_all(flat_rows.reshape(ep_size, tok_local, model_dim), "ep", 0, 0, tiled=True)
            return jnp.sum(back_rows, axis=0).astype(F32)

        expert_rows = send_out(normed)
        act_gate = jnp.einsum("ecd,edf->ecf", expert_rows, exp_gate, preferred_element_type=F32)
        act_up = jnp.einsum("ecd,edf->ecf", expert_rows, exp_up, preferred_element_type=F32)
        hidden = (jax.nn.silu(act_gate) * act_up).astype(BF16)
        out_rows = lax.psum(jnp.einsum("ecf,efd->ecd", hidden, exp_down, preferred_element_type=F32), "etp").astype(BF16)
        tok_out = send_back(out_rows)
        one_assign = (assign[:, None] == expert_ids[None, :]).astype(F32)
        gate_val = jnp.sum(gate_probs * one_assign, axis=1, keepdims=True)
        sh_act_gate = jnp.dot(normed, sh_gate, preferred_element_type=F32)
        sh_act_up = jnp.dot(normed, sh_up, preferred_element_type=F32)
        sh_hidden = (jax.nn.silu(sh_act_gate) * sh_act_up).astype(BF16)
        sh_out = lax.psum(jnp.dot(sh_hidden, sh_down, preferred_element_type=F32), "etp")
        y_out = (x_wide + sh_out + gate_val * tok_out).astype(BF16)
        dy_wide = y_grad.astype(F32)
        d_route = (gate_val * dy_wide).astype(BF16)
        d_rows = send_out(d_route)
        d_hidden = jnp.einsum("ecd,efd->ecf", d_rows, exp_down, preferred_element_type=F32)
        g_exp_down = jnp.einsum("ecf,ecd->efd", hidden, d_rows, preferred_element_type=F32)
        d_gate, d_up = glu_grads(d_hidden, act_gate, act_up)
        g_exp_gate = jnp.einsum("ecd,ecf->edf", expert_rows, d_gate, preferred_element_type=F32)
        g_exp_up = jnp.einsum("ecd,ecf->edf", expert_rows, d_up, preferred_element_type=F32)
        d_rows_in = lax.psum(jnp.einsum("ecf,edf->ecd", d_gate, exp_gate, preferred_element_type=F32) + jnp.einsum("ecf,edf->ecd", d_up, exp_up, preferred_element_type=F32), "etp").astype(BF16)
        dn_routed = send_back(d_rows_in)
        d_gate_val = jnp.sum(dy_wide * tok_out, axis=1, keepdims=True)
        d_logits = (d_gate_val * gate_val * (one_assign - gate_probs)).astype(BF16)
        g_router = lax.psum(jnp.einsum("td,te->de", normed, d_logits, preferred_element_type=F32), "ep")
        dn_router = jnp.einsum("te,de->td", d_logits, w_router, preferred_element_type=F32)
        sh_d_hidden = jnp.einsum("td,fd->tf", y_grad, sh_down, preferred_element_type=F32)
        g_sh_down = lax.psum(jnp.einsum("tf,td->fd", sh_hidden, y_grad, preferred_element_type=F32), "ep")
        sh_d_gate, sh_d_up = glu_grads(sh_d_hidden, sh_act_gate, sh_act_up)
        g_sh_gate = lax.psum(jnp.einsum("td,tf->df", normed, sh_d_gate, preferred_element_type=F32), "ep")
        g_sh_up = lax.psum(jnp.einsum("td,tf->df", normed, sh_d_up, preferred_element_type=F32), "ep")
        dn_shared = lax.psum(jnp.einsum("tf,df->td", sh_d_gate, sh_gate, preferred_element_type=F32) + jnp.einsum("tf,df->td", sh_d_up, sh_up, preferred_element_type=F32), "etp")
        d_normed = dn_shared + dn_router + dn_routed
        norm_proj = jnp.mean(d_normed * x_wide, axis=1, keepdims=True)
        x_grad = (dy_wide + inv_rms * d_normed - x_wide * inv_rms ** 3 * norm_proj).astype(BF16)
        return (y_out, x_grad, g_exp_gate, g_exp_up, g_exp_down, g_sh_gate, g_sh_up, g_sh_down, g_router)

    return jax.shard_map(local_step, mesh=mesh, in_specs=in_specs, out_specs=out_specs, check_vma=False)
```

profile of v0, /device:TPU:0, one launch (start us, length us, event | category | flops | bytes accessed | tf_op | source)
XLA Modules:
  0.0 248.2 jit_solution(5509173108655415441)
XLA Ops:
  12.1 6.8 %all-reduce = s32[128]{0:T(128)S(1)} all-reduce(s32[128]{0:T(128)S(1)} %dynamic-update-slice), channel_id=2, replica_groups=mesh['dp'=1,'etp'=2,'ep'=4] {'ep'}, use_global_device_ids=true, to_apply=%add | all-reduce | flops 128 | bytes 1024
  21.7 4.3 %all-reduce.1 = s32[128]{0:T(128)S(1)} all-reduce(s32[128]{0:T(128)S(1)} %dynamic-update-slice.1), channel_id=3, replica_groups=mesh['dp'=1,'etp'=2,'ep'=4] {'ep'}, use_global_device_ids=true, to_apply=%add.1 | all-reduce | flops 128 | bytes 1024
  33.2 3.5 %all-to-all-start.2 = ((bf16[4,128,1024]{2,1,0:T(8,128)(2,1)}), bf16[4,128,1024]{2,1,0:T(8,128)(2,1)S(1)}, u32[]{:S(2)}, u32[]{:S(2)}) async-start(bf16[4,128,1024]{2,1,0:T(8,128)(2,1)} %get-tuple-element.50), calls=%async_computation.2 | async-start | bytes 2097152 | tf_op jit(solution)/shard_map/all_to_all | solution.py:65
  41.2 11.7 %all-gather.3 = s32[4,1,128]{2,1,0:T(1,128)S(1)} all-gather(s32[1,1,128]{2,1,0:T(1,128)S(1)} %get-tuple-element.41), channel_id=1, replica_groups=mesh['dp'=1,'etp'=2,'ep'=4] {'ep'}, dimensions={0}, use_global_device_ids=true | all-gather | bytes 2560 | tf_op jit(solution)/shard_map/all_gather | solution.py:58
  52.9 8.1 %all-gather.2 = s32[4,1,128]{2,1,0:T(1,128)S(1)} all-gather(s32[1,1,128]{2,1,0:T(1,128)S(1)} %bitcast.54), channel_id=1, replica_groups=mesh['dp'=1,'etp'=2,'ep'=4] {'ep'}, dimensions={0}, use_global_device_ids=true | all-gather | bytes 2560 | tf_op jit(solution)/shard_map/all_gather | solution.py:57
  61.0 2.4 scatter_custom_fusion
  63.5 3.5 %all-to-all-start = ((bf16[4,128,1024]{2,1,0:T(8,128)(2,1)}), bf16[4,128,1024]{2,1,0:T(8,128)(2,1)S(1)}, u32[]{:S(2)}, u32[]{:S(2)}) async-start(bf16[4,128,1024]{2,1,0:T(8,128)(2,1)} %get-tuple-element.51), calls=%async_computation | async-start | bytes 2097152 | tf_op jit(solution)/shard_map/all_to_all | solution.py:65
  69.4 11.9 %all-to-all-done = bf16[4,128,1024]{2,1,0:T(8,128)(2,1)S(1)} async-done(((bf16[4,128,1024]{2,1,0:T(8,128)(2,1)}), bf16[4,128,1024]{2,1,0:T(8,128)(2,1)S(1)}, u32[]{:S(2)}, u32[]{:S(2)}) %all-to-all-start) | async-done | bytes 1048608 | tf_op jit(solution)/shard_map/all_to_all | solution.py:65
  82.5 3.0 %fusion.31 = f32[8,20,256]{2,1,0:T(8,128)S(1)} fusion(bf16[8,20,1024]{2,1,0:T(8,128)(2,1)S(1)} %reshape.123, bf16[8,1024,256]{2,1,0:T(8,128)(2,1)} %param.21), kind=kOutput, calls=%fused_computation.102 | convolution fusion | flops 83886080 | bytes 4685824 | tf_op jit(solution)/shard_map/ecd,edf->ecf/dot_general | solution.py:75
  85.5 3.0 %fusion.30 = f32[8,20,256]{2,1,0:T(8,128)S(1)} fusion(bf16[8,20,1024]{2,1,0:T(8,128)(2,1)S(1)} %reshape.123, bf16[8,1024,256]{2,1,0:T(8,128)(2,1)} %param.20), kind=kOutput, calls=%fused_computation.101 | convolution fusion | flops 83886080 | bytes 4685824 | tf_op jit(solution)/shard_map/ecd,edf->ecf/dot_general | solution.py:74
  92.9 40.5 %all-reduce.12 = (bf16[8,20,1024]{2,1,0:T(8,128)(2,1)}, bf16[8,20,1024]{2,1,0:T(8,128)(2,1)S(1)}) all-reduce(f32[8,20,1024]{2,1,0:T(8,128)S(1)} %fusion.32, f32[8,20,1024]{2,1,0:T(8,128)S(1)} %convolution_add_fusion), channel_id=1, replica_groups=mesh['dp'=1,'etp'=2,'ep'=4] {'etp'}, use_global_device_ids=true, to_apply=%region_17.19 | all-reduce | flops 327680 | bytes 1966080 | tf_op jit(solution)/shard_map/psum | solution.py:77
  134.6 2.1 gather_fusion.3
  140.2 3.6 %all-to-all-start.1 = ((bf16[4,128,1024]{2,1,0:T(8,128)(2,1)}), bf16[4,128,1024]{2,1,0:T(8,128)(2,1)S(1)}, u32[]{:S(2)}, u32[]{:S(2)}) async-start(bf16[4,128,1024]{2,1,0:T(8,128)(2,1)} %bitcast.53), calls=%async_computation.1 | async-start | bytes 2097152 | tf_op jit(solution)/shard_map/all_to_all | solution.py:70
  143.9 2.2 fusion.39
  147.4 4.7 %fusion.37 = f32[8,256,1024]{2,1,0:T(8,128)} fusion(bf16[8,20,256]{2,1,0:T(8,128)(2,1)S(1)} %copy-done.14, bf16[8,20,1024]{2,1,0:T(8,128)(2,1)S(1)} %copy-done.8), kind=kOutput, calls=%fused_computation.108 | convolution fusion | flops 83886080 | bytes 8798208 | tf_op jit(solution)/shard_map/ecf,ecd->efd/dot_general | solution.py:90
  152.1 6.0 %all-to-all-done.1 = bf16[4,128,1024]{2,1,0:T(8,128)(2,1)S(1)} async-done(((bf16[4,128,1024]{2,1,0:T(8,128)(2,1)}), bf16[4,128,1024]{2,1,0:T(8,128)(2,1)S(1)}, u32[]{:S(2)}, u32[]{:S(2)}) %all-to-all-start.1) | async-done | bytes 1048608 | tf_op jit(solution)/shard_map/all_to_all | solution.py:70
  158.1 3.5 %all-to-all-start.3 = ((bf16[4,128,1024]{2,1,0:T(8,128)(2,1)}), bf16[4,128,1024]{2,1,0:T(8,128)(2,1)S(1)}, u32[]{:S(2)}, u32[]{:S(2)}) async-start(bf16[4,128,1024]{2,1,0:T(8,128)(2,1)} %bitcast.8), calls=%async_computation.3 | async-start | bytes 2097152 | tf_op jit(solution)/shard_map/all_to_all | solution.py:70
  162.9 5.6 %fusion.36 = f32[8,1024,256]{2,1,0:T(8,128)} fusion(bf16[8,20,1024]{2,1,0:T(8,128)(2,1)S(1)} %reshape.123, bf16[8,20,256]{2,1,0:T(8,128)(2,1)} %copy-done.12), kind=kOutput, calls=%fused_computation.107 | convolution fusion | flops 83886080 | bytes 8798208 | tf_op jit(solution)/shard_map/ecd,ecf->edf/dot_general | solution.py:93
  168.5 4.7 %fusion.35 = f32[8,1024,256]{2,1,0:T(8,128)} fusion(bf16[8,20,1024]{2,1,0:T(8,128)(2,1)S(1)} %reshape.123, bf16[8,20,256]{2,1,0:T(8,128)(2,1)S(1)} %get-tuple-element.32), kind=kOutput, calls=%fused_computation.106 | convolution fusion | flops 83886080 | bytes 8798208 | tf_op jit(solution)/shard_map/ecd,ecf->edf/dot_general | solution.py:92
  173.2 7.5 %all-to-all-done.3 = bf16[4,128,1024]{2,1,0:T(8,128)(2,1)S(1)} async-done(((bf16[4,128,1024]{2,1,0:T(8,128)(2,1)}), bf16[4,128,1024]{2,1,0:T(8,128)(2,1)S(1)}, u32[]{:S(2)}, u32[]{:S(2)}) %all-to-all-start.3) | async-done | bytes 1048608 | tf_op jit(solution)/shard_map/all_to_all | solution.py:70
  182.4 2.2 fusion.6
  184.6 50.5 %all-reduce.9.cloned.1.call-done = (f32[1024,256]{1,0:T(8,128)}, f32[1024,256]{1,0:T(8,128)}, f32[256,1024]{1,0:T(8,128)}, f32[1024,32]{0,1:T(8,128)}) async-done(((f32[1024,256]{1,0:T(8,128)}, f32[1024,256]{1,0:T(8,128)}, f32[256,1024]{1,0:T(8,128)}, f32[1024,32]{0,1:T(8,128)}), (f32[1024,256]{1,0:T(8,128)}, f32[1024,256]{1,0:T(8,128)}, f32[256,1024]{1,0:T(8,128)}, ...) | async-done | bytes 3276816 | tf_op jit(solution)/shard_map/psum | solution.py:103
  235.1 2.4 copy.34
  237.5 2.3 copy.35
  (130 shorter events, 37.0 us)
Async XLA Ops:
  7.2 30.1 %copy-start = (bf16[256,1024]{1,0:T(8,128)(2,1)S(1)}, bf16[256,1024]{1,0:T(8,128)(2,1)}, u32[]{:S(2)}) copy-start(bf16[256,1024]{1,0:T(8,128)(2,1)} %param.25) | copy-start | bytes 1572868
  7.2 29.6 %copy-start.9 = (bf16[1024,256]{1,0:T(8,128)(2,1)S(1)}, bf16[1024,256]{1,0:T(8,128)(2,1)}, u32[]{:S(2)}) copy-start(bf16[1024,256]{1,0:T(8,128)(2,1)} %param.24) | copy-start | bytes 1572868
  7.2 29.8 %copy-start.10 = (bf16[1024,256]{1,0:T(8,128)(2,1)S(1)}, bf16[1024,256]{1,0:T(8,128)(2,1)}, u32[]{:S(2)}) copy-start(bf16[1024,256]{1,0:T(8,128)(2,1)} %param.23) | copy-start | bytes 1572868
  19.4 17.8 %copy-start.26 = (f32[128]{0:T(128)}, f32[128]{0:T(128)S(1)}, u32[]{:S(2)}) copy-start(f32[128]{0:T(128)S(1)} %get-tuple-element.45) | copy-start | bytes 1540
  19.8 17.5 %copy-start.5 = (bf16[128,1024]{1,0:T(8,128)(2,1)S(1)}, bf16[128,1024]{1,0:T(8,128)(2,1)}, u32[]{:S(2)}) copy-start(bf16[128,1024]{1,0:T(8,128)(2,1)} %param.16) | copy-start | bytes 786436
  27.8 25.1 %copy-start.20 = (s32[128]{0:T(128)}, s32[128]{0:T(128)S(1)}, u32[]{:S(2)}) copy-start(s32[128]{0:T(128)S(1)} %get-tuple-element.28) | copy-start | bytes 1540
  30.0 7.6 %copy-start.22 = (f32[128]{0:T(128)}, f32[128]{0:T(128)S(1)}, u32[]{:S(2)}) copy-start(f32[128]{0:T(128)S(1)} %fusion.17) | copy-start | bytes 1540
  33.2 30.3 %all-to-all-start.2 = ((bf16[4,128,1024]{2,1,0:T(8,128)(2,1)}), bf16[4,128,1024]{2,1,0:T(8,128)(2,1)S(1)}, u32[]{:S(2)}, u32[]{:S(2)}) async-start(bf16[4,128,1024]{2,1,0:T(8,128)(2,1)} %get-tuple-element.50), calls=%async_computation.2 | async-start | bytes 2097152 | tf_op jit(solution)/shard_map/all_to_all | solution.py:65
  36.7 144.2 %all-reduce.11.cloned.1.call-start = ((), (), s32[]{:S(2)}) async-start(), calls=%async_computation.5 | async-start | bytes 2097152 | tf_op jit(solution)/shard_map/psum | solution.py:84
  37.6 30.8 %copy-start.16 = (bf16[128,256]{1,0:T(8,128)(2,1)}, bf16[128,256]{1,0:T(8,128)(2,1)S(1)}, u32[]{:S(2)}) copy-start(bf16[128,256]{1,0:T(8,128)(2,1)S(1)} %get-tuple-element.36) | copy-start | bytes 196612
  63.5 17.7 %all-to-all-start = ((bf16[4,128,1024]{2,1,0:T(8,128)(2,1)}), bf16[4,128,1024]{2,1,0:T(8,128)(2,1)S(1)}, u32[]{:S(2)}, u32[]{:S(2)}) async-start(bf16[4,128,1024]{2,1,0:T(8,128)(2,1)} %get-tuple-element.51), calls=%async_computation | async-start | bytes 2097152 | tf_op jit(solution)/shard_map/all_to_all | solution.py:65
  140.2 7.1 %copy-start.14 = (bf16[8,20,256]{2,1,0:T(8,128)(2,1)S(1)}, bf16[8,20,256]{2,1,0:T(8,128)(2,1)}, u32[]{:S(2)}) copy-start(bf16[8,20,256]{2,1,0:T(8,128)(2,1)} %copy-done.13) | copy-start | bytes 245764
  140.2 17.8 %all-to-all-start.1 = ((bf16[4,128,1024]{2,1,0:T(8,128)(2,1)}), bf16[4,128,1024]{2,1,0:T(8,128)(2,1)S(1)}, u32[]{:S(2)}, u32[]{:S(2)}) async-start(bf16[4,128,1024]{2,1,0:T(8,128)(2,1)} %bitcast.53), calls=%async_computation.1 | async-start | bytes 2097152 | tf_op jit(solution)/shard_map/all_to_all | solution.py:70
  147.3 14.7 %copy-start.25 = (f32[128]{0:T(128)S(1)}, f32[128]{0:T(128)}, u32[]{:S(2)}) copy-start(f32[128]{0:T(128)} %copy-done.24) | copy-start | bytes 1540
  147.3 14.7 %copy-start.19 = (f32[128]{0:T(128)S(1)}, f32[128]{0:T(128)}, u32[]{:S(2)}) copy-start(f32[128]{0:T(128)} %copy-done.18) | copy-start | bytes 1540
  147.4 14.7 %copy-start.21 = (s32[128]{0:T(128)S(1)}, s32[128]{0:T(128)}, u32[]{:S(2)}) copy-start(s32[128]{0:T(128)} %copy-done.20) | copy-start | bytes 1540
  147.4 14.7 %copy-start.23 = (f32[128]{0:T(128)S(1)}, f32[128]{0:T(128)}, u32[]{:S(2)}) copy-start(f32[128]{0:T(128)} %copy-done.22) | copy-start | bytes 1540
  158.1 22.6 %all-to-all-start.3 = ((bf16[4,128,1024]{2,1,0:T(8,128)(2,1)}), bf16[4,128,1024]{2,1,0:T(8,128)(2,1)S(1)}, u32[]{:S(2)}, u32[]{:S(2)}) async-start(bf16[4,128,1024]{2,1,0:T(8,128)(2,1)} %bitcast.8), calls=%async_computation.3 | async-start | bytes 2097152 | tf_op jit(solution)/shard_map/all_to_all | solution.py:70
  161.6 73.5 %all-reduce.9.cloned.1.call-start = ((), (), s32[]{:S(2)}) async-start(), calls=%async_computation.4 | async-start | bytes 6553600 | tf_op jit(solution)/shard_map/psum | solution.py:103
  168.5 12.4 %copy-start.6 = (bf16[128,1024]{1,0:T(8,128)(2,1)S(1)}, bf16[128,1024]{1,0:T(8,128)(2,1)}, u32[]{:S(2)}) copy-start(bf16[128,1024]{1,0:T(8,128)(2,1)} %param.15) | copy-start | bytes 786436
  168.5 12.4 %copy-start.15 = (bf16[1024,32]{0,1:T(8,128)(2,1)S(1)}, bf16[1024,32]{0,1:T(8,128)(2,1)}, u32[]{:S(2)}) copy-start(bf16[1024,32]{0,1:T(8,128)(2,1)} %param.19) | copy-start | bytes 196612
  168.5 13.9 %copy-start.27 = (f32[128]{0:T(128)S(1)}, f32[128]{0:T(128)}, u32[]{:S(2)}) copy-start(f32[128]{0:T(128)} %copy-done.26) | copy-start | bytes 1540
  168.5 13.9 %copy-start.28 = (f32[128]{0:T(128)S(1)}, f32[128]{0:T(128)}, u32[]{:S(2)}) copy-start(f32[128]{0:T(128)} %get-tuple-element.44) | copy-start | bytes 1540
  182.4 59.0 %copy-start.1 = (bf16[256,1024]{1,0:T(8,128)(2,1)S(1)}, bf16[256,1024]{1,0:T(8,128)(2,1)}, u32[]{:S(2)}) copy-start(bf16[256,1024]{1,0:T(8,128)(2,1)} %param.25) | copy-start | bytes 1572868
  (11 other events, 48.8 us)
Sparse Core Ops, SparseCore 0:
  41.3 35.6 all-reduce.10
  166.1 68.9 all-reduce.8
where the time goes:
time: 249 us; the launch traced here: 248 us
  waiting for transfers between devices  75.9 us (30%)
  blocking collectives  71.3 us (29%)
  matrix products  37.7 us (15%)
  local copies, waits for them, and re-layouts  18.5 us (7%)
  between operations  15.3 us (6%)
  other arithmetic  15.2 us (6%)
  starting transfers between devices  14.3 us (6%)
    psum x1, waiting for transfers between devices, local_step(): lax.psum(jnp.einsum('td,tf->df', normed, sh_d_gate, preferred_element_typ...  50.5 us
    psum x1, blocking collectives, local_step(): lax.psum(jnp.einsum('ecf,efd->ecd', hidden, exp_down, preferred_element_t...  40.5 us
    all_to_all x2, waiting for transfers between devices, send_back(): lax.all_to_all(flat_rows.reshape(ep_size, tok_local, model_dim), 'ep', 0,...  13.5 us
    all_to_all x2, waiting for transfers between devices, send_out(): lax.all_to_all(sent_rows, 'ep', 0, 0, tiled=True)  11.9 us
    all_gather x1, blocking collectives, local_step(): all_slot = lax.all_gather(slot_idx, 'ep', tiled=True)  11.7 us
    unnamed x2, blocking collectives  11 us
    unnamed x67, local copies, waits for them, and re-layouts  8.61 us
    all_gather x1, blocking collectives, local_step(): all_assign = lax.all_gather(assign, 'ep', tiled=True)  8.09 us
  transfers between devices with their start and end apart: 6, of which 4 were waited for; matrix products, arithmetic and copies ran while one was open for 20% of the time, Pallas kernels for 0%

commit v1 on v0

v1 whole, which is shorter than its diff:
```python
import functools

import jax
import jax.numpy as jnp
from jax import lax
from jax.experimental import pallas as pl
from jax.experimental.pallas import tpu as pltpu
from jax.sharding import PartitionSpec as P

EPS = 1e-5
F32 = jnp.float32
BF16 = jnp.bfloat16
MESH = pl.DeviceIdType.MESH
ANY = pl.BlockSpec(memory_space=pl.ANY)
VMEM = pl.BlockSpec(memory_space=pltpu.VMEM)
NN = (((1,), (0,)), ((), ()))
NT = (((1,), (1,)), ((), ()))
TN = (((0,), (0,)), ((), ()))

SHARDS = 4
TOK = 128
DIM = 1024
HALF = 512
EXPERTS = 32
OWN = 8
CAP = 20
PAD = 32
SLOTS = OWN * CAP


def mm(a, b, dims=NN):
    return lax.dot_general(a, b, dims, preferred_element_type=F32)


def inv_rms_of(x_wide):
    return lax.rsqrt(jnp.mean(x_wide * x_wide, axis=1, keepdims=True) + EPS)


def glu_grads(d_hidden, act_gate, act_up):
    sig_gate = jax.nn.sigmoid(act_gate)
    d_gate = (d_hidden * act_up * sig_gate * (1.0 + act_gate * (1.0 - sig_gate))).astype(BF16)
    d_up = (d_hidden * act_gate * sig_gate).astype(BF16)
    return d_gate, d_up


def to_row(col):
    return jnp.transpose(jnp.broadcast_to(col, (TOK, TOK)))[:8]


def to_col(row):
    return jnp.transpose(jnp.broadcast_to(row, (TOK, TOK)))[:, :1]


def barrier(peers):
    sem = pltpu.get_barrier_semaphore()
    for peer in peers:
        pl.semaphore_signal(sem, inc=1, device_id=peer, device_id_type=MESH)
    pl.semaphore_wait(sem, len(peers))


def gather_kernel(x_ref, dy_ref, ids_ref, wg_hbm, wu_hbm, wd_hbm, x_all, dy_all, ids_all, s_out, dns_out, wg, wu, wd, s_send, s_recv, d_send, d_recv, w_sem, send_sem, recv_sem, y_send_sem, y_recv_sem):
    me = lax.axis_index("ep")
    side = lax.axis_index("etp")
    mate = jnp.bitwise_xor(me, 1)
    across = jnp.bitwise_xor(me, 2)
    to_mate, to_across, to_twin = {"ep": mate}, {"ep": across}, {"etp": 1 - side}
    loads = [pltpu.make_async_copy(src, dst, w_sem.at[k]) for k, (src, dst) in enumerate(((wg_hbm, wg), (wu_hbm, wu), (wd_hbm, wd)))]
    for load in loads:
        load.start()
    barrier((to_mate, to_across, to_twin))
    half_rows = TOK // 2

    def pieces(shard):
        return [
            (ids_ref, ids_all.at[shard]),
            (x_ref.at[:half_rows], x_all.at[shard, :half_rows]),
            (x_ref.at[half_rows:], x_all.at[shard, half_rows:]),
            (dy_ref.at[:half_rows], dy_all.at[shard, :half_rows]),
            (dy_ref.at[half_rows:], dy_all.at[shard, half_rows:]),
        ]

    def remote(src, dst, lane, k, target):
        return pltpu.make_async_remote_copy(src_ref=src, dst_ref=dst, send_sem=send_sem.at[lane, k], recv_sem=recv_sem.at[lane, k], device_id=target, device_id_type=MESH)

    out_across = [remote(src, dst, 0, k, to_across) for k, (src, dst) in enumerate(pieces(me))]
    out_mate = [remote(src, dst, 1, k, to_mate) for k, (src, dst) in enumerate(pieces(me))]
    for copy in out_across:
        copy.start()
    for copy in out_mate:
        copy.start()
    x_all[me] = x_ref[...]
    dy_all[me] = dy_ref[...]
    ids_all[me] = ids_ref[...]

    x_wide = x_ref[...].astype(F32)
    normed = (x_wide * inv_rms_of(x_wide)).astype(BF16)
    for load in loads:
        load.wait()
    act_gate = mm(normed, wg[...])
    act_up = mm(normed, wu[...])
    hidden = (jax.nn.silu(act_gate) * act_up).astype(BF16)
    theirs = pl.ds(pl.multiple_of((1 - side) * HALF, HALF), HALF)
    mine = pl.ds(pl.multiple_of(side * HALF, HALF), HALF)
    s_send[...] = mm(hidden, wd[:, theirs])
    s_copy = pltpu.make_async_remote_copy(src_ref=s_send, dst_ref=s_recv, send_sem=y_send_sem.at[0], recv_sem=y_recv_sem.at[0], device_id=to_twin, device_id_type=MESH)
    s_copy.start()
    d_gate, d_up = glu_grads(mm(dy_ref[...], wd[...], NT), act_gate, act_up)
    d_send[...] = mm(d_gate, wg[theirs, :], NT) + mm(d_up, wu[theirs, :], NT)
    d_copy = pltpu.make_async_remote_copy(src_ref=d_send, dst_ref=d_recv, send_sem=y_send_sem.at[1], recv_sem=y_recv_sem.at[1], device_id=to_twin, device_id_type=MESH)
    d_copy.start()
    s_out[...] = mm(hidden, wd[:, mine])
    dns_out[...] = mm(d_gate, wg[mine, :], NT) + mm(d_up, wu[mine, :], NT)

    forwards = []
    for k, (_, dst) in enumerate(pieces(across)):
        out_across[k].wait_recv()
        forward = remote(dst, dst, 2, k, to_mate)
        forward.start()
        forwards.append(forward)
    s_copy.wait_recv()
    s_out[...] += s_recv[...]
    d_copy.wait_recv()
    dns_out[...] += d_recv[...]
    for copy in out_mate + forwards:
        copy.wait_recv()
    for copy in out_across + out_mate + forwards + [s_copy, d_copy]:
        copy.wait_send()


def gather_call(x_in, y_grad, ids, sh_gate, sh_up, sh_down):
    width = sh_gate.shape[1]
    return pl.pallas_call(
        gather_kernel,
        out_shape=(
            jax.ShapeDtypeStruct((SHARDS, TOK, DIM), BF16),
            jax.ShapeDtypeStruct((SHARDS, TOK, DIM), BF16),
            jax.ShapeDtypeStruct((SHARDS, 8, TOK), jnp.int32),
            jax.ShapeDtypeStruct((TOK, HALF), F32),
            jax.ShapeDtypeStruct((TOK, HALF), F32),
        ),
        in_specs=[VMEM, VMEM, VMEM, ANY, ANY, ANY],
        out_specs=(VMEM,) * 5,
        scratch_shapes=[
            pltpu.VMEM((DIM, width), BF16),
            pltpu.VMEM((DIM, width), BF16),
            pltpu.VMEM((width, DIM), BF16),
            pltpu.VMEM((TOK, HALF), F32),
            pltpu.VMEM((TOK, HALF), F32),
            pltpu.VMEM((TOK, HALF), F32),
            pltpu.VMEM((TOK, HALF), F32),
            pltpu.SemaphoreType.DMA((3,)),
            pltpu.SemaphoreType.DMA((3, 5)),
            pltpu.SemaphoreType.DMA((3, 5)),
            pltpu.SemaphoreType.DMA((2,)),
            pltpu.SemaphoreType.DMA((2,)),
        ],
        compiler_params=pltpu.CompilerParams(collective_id=0, has_side_effects=True),
        name="gather_tokens",
    )(x_in, y_grad, ids, sh_gate, sh_up, sh_down)


def forward_kernel(x_ref, dy_ref, ids_ref, wr_ref, wg, wu, wd, o_send, o_keep, xs, us, a_out, b_out, h_out, n_out, meta, p_out):
    me = lax.axis_index("ep")
    side = lax.axis_index("etp")
    total = SHARDS * TOK

    @pl.when(pl.program_id(0) == 0)
    def route():
        x_wide = x_ref[...].reshape(total, DIM).astype(F32)
        normed = (x_wide * inv_rms_of(x_wide)).astype(BF16)
        n_out[...] = normed
        logits = mm(normed, wr_ref[...])
        top = jnp.max(logits, axis=1, keepdims=True)
        expo = jnp.exp(logits - top)
        probs = expo / jnp.sum(expo, axis=1, keepdims=True)
        wide = jnp.concatenate([probs, jnp.zeros((total, TOK - EXPERTS), F32)], axis=1)
        probs_t = jnp.concatenate([jnp.transpose(wide[s * TOK : (s + 1) * TOK])[:EXPERTS] for s in range(SHARDS)], axis=1)
        p_out[...] = probs_t

        prim = jnp.concatenate([ids_ref[s, 0:1, :] for s in range(SHARDS)], axis=1)
        alt = jnp.concatenate([ids_ref[s, 1:2, :] for s in range(SHARDS)], axis=1)
        expert = lax.broadcasted_iota(jnp.int32, (EXPERTS, total), 0)
        before = (lax.broadcasted_iota(jnp.int32, (total, total), 0) < lax.broadcasted_iota(jnp.int32, (total, total), 1)).astype(F32).astype(BF16)
        one_prim = (expert == prim).astype(F32)
        rank_prim = jnp.sum(one_prim * mm(one_prim.astype(BF16), before), axis=0, keepdims=True)
        keep_prim = rank_prim < CAP
        kept = jnp.minimum(jnp.sum(one_prim, axis=1, keepdims=True), float(CAP))
        one_alt = jnp.where(keep_prim, 0.0, (expert == alt).astype(F32))
        slot_alt = jnp.sum(one_alt * (mm(one_alt.astype(BF16), before) + kept), axis=0, keepdims=True)
        keep_alt = jnp.logical_and(jnp.logical_not(keep_prim), slot_alt < CAP)
        assign = jnp.where(keep_prim, prim, jnp.where(keep_alt, alt, -1))
        slot = jnp.where(keep_prim, rank_prim, slot_alt).astype(jnp.int32)
        gate = jnp.sum(jnp.where(expert == assign, probs_t, 0.0), axis=0, keepdims=True)
        flat = jnp.where(assign >= 0, assign * CAP + slot, -1)
        meta[0:1] = assign.astype(F32)
        meta[1:2] = flat.astype(F32)
        meta[2:3] = gate
        meta[3:8] = jnp.zeros((5, total), F32)

        local = assign - me * OWN
        owned = jnp.logical_and(local >= 0, local < OWN)
        target = jnp.where(owned, local * PAD + slot, -1)
        picked = lax.broadcasted_iota(jnp.int32, (OWN * PAD, total), 0) == target
        pick = picked.astype(F32).astype(BF16)
        xs[...] = mm(pick, normed).astype(BF16)
        gate_slot = jnp.sum(jnp.where(picked, gate, 0.0), axis=1, keepdims=True)
        us[...] = (gate_slot * mm(pick, dy_ref[...].reshape(total, DIM))).astype(BF16)

    theirs = pl.ds(pl.multiple_of((1 - side) * HALF, HALF), HALF)
    mine = pl.ds(pl.multiple_of(side * HALF, HALF), HALF)
    for j in range(2):
        row = pl.multiple_of((pl.program_id(0) * 2 + j) * PAD, PAD)
        rows = xs[pl.ds(row, PAD), :]
        act_gate = mm(rows, wg[j])
        act_up = mm(rows, wu[j])
        hidden = (jax.nn.silu(act_gate) * act_up).astype(BF16)
        a_out[j] = act_gate
        b_out[j] = act_up
        h_out[j] = hidden
        o_send[0, j * CAP : (j + 1) * CAP, :] = mm(hidden, wd[j, :, theirs])[:CAP]
        o_keep[0, j * CAP : (j + 1) * CAP, :] = mm(hidden, wd[j, :, mine])[:CAP]


def whole(shape):
    return pl.BlockSpec(shape, lambda i: (0,) * len(shape))


def forward_call(x_all, dy_all, ids_all, w_router, exp_gate, exp_up, exp_down):
    width = exp_gate.shape[2]
    total = SHARDS * TOK
    pair = lambda *shape: pl.BlockSpec((2,) + shape, lambda i: (i, 0, 0))
    part = pl.BlockSpec((1, 2 * CAP, HALF), lambda i: (i, 0, 0))
    return pl.pallas_call(
        forward_kernel,
        grid=(OWN // 2,),
        out_shape=(
            jax.ShapeDtypeStruct((OWN // 2, 2 * CAP, HALF), F32),
            jax.ShapeDtypeStruct((OWN // 2, 2 * CAP, HALF), F32),
            jax.ShapeDtypeStruct((OWN * PAD, DIM), BF16),
            jax.ShapeDtypeStruct((OWN * PAD, DIM), BF16),
            jax.ShapeDtypeStruct((OWN, PAD, width), F32),
            jax.ShapeDtypeStruct((OWN, PAD, width), F32),
            jax.ShapeDtypeStruct((OWN, PAD, width), BF16),
            jax.ShapeDtypeStruct((total, DIM), BF16),
            jax.ShapeDtypeStruct((8, total), F32),
            jax.ShapeDtypeStruct((EXPERTS, total), F32),
        ),
        in_specs=[whole((SHARDS, TOK, DIM)), whole((SHARDS, TOK, DIM)), whole((SHARDS, 8, TOK)), whole((DIM, EXPERTS)), pair(DIM, width), pair(DIM, width), pair(width, DIM)],
        out_specs=(part, part, whole((OWN * PAD, DIM)), whole((OWN * PAD, DIM)), pair(PAD, width), pair(PAD, width), pair(PAD, width), whole((total, DIM)), whole((8, total)), whole((EXPERTS, total))),
        compiler_params=pltpu.CompilerParams(dimension_semantics=("arbitrary",), vmem_limit_bytes=48 << 20),
        cost_estimate=pl.CostEstimate(flops=2 * 3 * OWN * PAD * DIM * width, bytes_accessed=16 << 20, transcendentals=0),
        name="expert_forward",
    )(x_all, dy_all, ids_all, w_router, exp_gate, exp_up, exp_down)


def backward_kernel(us, a_in, b_in, wg, wu, wd, d_send, d_keep, da_out, db_out):
    side = lax.axis_index("etp")
    theirs = pl.ds(pl.multiple_of((1 - side) * HALF, HALF), HALF)
    mine = pl.ds(pl.multiple_of(side * HALF, HALF), HALF)
    for j in range(2):
        row = pl.multiple_of((pl.program_id(0) * 2 + j) * PAD, PAD)
        d_gate, d_up = glu_grads(mm(us[pl.ds(row, PAD), :], wd[j], NT), a_in[j], b_in[j])
        da_out[j] = d_gate
        db_out[j] = d_up
        d_send[0, j * CAP : (j + 1) * CAP, :] = (mm(d_gate, wg[j, theirs, :], NT) + mm(d_up, wu[j, theirs, :], NT))[:CAP]
        d_keep[0, j * CAP : (j + 1) * CAP, :] = (mm(d_gate, wg[j, mine, :], NT) + mm(d_up, wu[j, mine, :], NT))[:CAP]


def backward_call(us, act_gate, act_up, exp_gate, exp_up, exp_down):
    width = exp_gate.shape[2]
    pair = lambda *shape: pl.BlockSpec((2,) + shape, lambda i: (i, 0, 0))
    part = pl.BlockSpec((1, 2 * CAP, HALF), lambda i: (i, 0, 0))
    return pl.pallas_call(
        backward_kernel,
        grid=(OWN // 2,),
        out_shape=(
            jax.ShapeDtypeStruct((OWN // 2, 2 * CAP, HALF), F32),
            jax.ShapeDtypeStruct((OWN // 2, 2 * CAP, HALF), F32),
            jax.ShapeDtypeStruct((OWN, PAD, width), BF16),
            jax.ShapeDtypeStruct((OWN, PAD, width), BF16),
        ),
        in_specs=[whole((OWN * PAD, DIM)), pair(PAD, width), pair(PAD, width), pair(DIM, width), pair(DIM, width), pair(width, DIM)],
        out_specs=(part, part, pair(PAD, width), pair(PAD, width)),
        compiler_params=pltpu.CompilerParams(dimension_semantics=("arbitrary",), vmem_limit_bytes=40 << 20),
        cost_estimate=pl.CostEstimate(flops=2 * 3 * OWN * PAD * DIM * width, bytes_accessed=16 << 20, transcendentals=0),
        name="expert_backward",
    )(us, act_gate, act_up, exp_gate, exp_up, exp_down)


def grads_kernel(xs, us, h_in, da_in, db_in, n_ref, dy_ref, sg, su, sd, g_gate, g_up, g_down, gs_gate, gs_up, gs_down):
    @pl.when(pl.program_id(0) == 0)
    def shared():
        normed = n_ref[...]
        d_rows = dy_ref[...].reshape(SHARDS * TOK, DIM)
        act_gate = mm(normed, sg[...])
        act_up = mm(normed, su[...])
        hidden = (jax.nn.silu(act_gate) * act_up).astype(BF16)
        d_gate, d_up = glu_grads(mm(d_rows, sd[...], NT), act_gate, act_up)
        gs_down[...] = mm(hidden, d_rows, TN)
        gs_gate[...] = mm(normed, d_gate, TN)
        gs_up[...] = mm(normed, d_up, TN)

    row = pl.multiple_of(pl.program_id(0) * PAD, PAD)
    rows = xs[pl.ds(row, PAD), :]
    g_down[0] = mm(h_in[0], us[pl.ds(row, PAD), :], TN)
    g_gate[0] = mm(rows, da_in[0], TN)
    g_up[0] = mm(rows, db_in[0], TN)


def grads_call(xs, us, hidden, d_gate, d_up, normed, dy_all, sh_gate, sh_up, sh_down):
    width = sh_gate.shape[1]
    total = SHARDS * TOK
    one = lambda *shape: pl.BlockSpec((1,) + shape, lambda i: (i, 0, 0))
    return pl.pallas_call(
        grads_kernel,
        grid=(OWN,),
        out_shape=(
            jax.ShapeDtypeStruct((OWN, DIM, width), F32),
            jax.ShapeDtypeStruct((OWN, DIM, width), F32),
            jax.ShapeDtypeStruct((OWN, width, DIM), F32),
            jax.ShapeDtypeStruct((DIM, width), F32),
            jax.ShapeDtypeStruct((DIM, width), F32),
            jax.ShapeDtypeStruct((width, DIM), F32),
        ),
        in_specs=[whole((OWN * PAD, DIM)), whole((OWN * PAD, DIM)), one(PAD, width), one(PAD, width), one(PAD, width), whole((total, DIM)), whole((SHARDS, TOK, DIM)), whole((DIM, width)), whole((DIM, width)), whole((width, DIM))],
        out_specs=(one(DIM, width), one(DIM, width), one(width, DIM), whole((DIM, width)), whole((DIM, width)), whole((width, DIM))),
        compiler_params=pltpu.CompilerParams(dimension_semantics=("arbitrary",), vmem_limit_bytes=48 << 20),
        cost_estimate=pl.CostEstimate(flops=8 << 30, bytes_accessed=32 << 20, transcendentals=0),
        name="weight_grads",
    )(xs, us, hidden, d_gate, d_up, normed, dy_all, sh_gate, sh_up, sh_down)


def finish_kernel(o_keep, o_recv, d_keep, d_recv, x_ref, dy_ref, s_ref, dns_ref, meta, p_ref, n_ref, wr_ref, y_out, dx_out, gr_out, o_all, d_all, dg_mine, dg_all, np_mine, np_recv, y_half, dx_half, send_sem, recv_sem, y_send_sem, y_recv_sem, g_send_sem, g_recv_sem):
    me = lax.axis_index("ep")
    side = lax.axis_index("etp")
    mate = jnp.bitwise_xor(me, 1)
    across = jnp.bitwise_xor(me, 2)
    to_mate, to_across, to_twin = {"ep": mate}, {"ep": across}, {"etp": 1 - side}
    others = [{"etp": jnp.bitwise_xor(side, k // SHARDS), "ep": jnp.bitwise_xor(me, k % SHARDS)} for k in range(1, 2 * SHARDS)]
    barrier(others)

    def remote(buf, shard, lane, k, target):
        view = buf.at[shard]
        return pltpu.make_async_remote_copy(src_ref=view, dst_ref=view, send_sem=send_sem.at[lane, k], recv_sem=recv_sem.at[lane, k], device_id=target, device_id_type=MESH)

    def twin(src, dst, k):
        return pltpu.make_async_remote_copy(src_ref=src, dst_ref=dst, send_sem=y_send_sem.at[k], recv_sem=y_recv_sem.at[k], device_id=to_twin, device_id_type=MESH)

    o_all[me] = (o_keep[...].reshape(SLOTS, HALF) + o_recv[...].reshape(SLOTS, HALF)).astype(BF16)
    o_copies = [remote(o_all, me, 0, 0, to_across), remote(o_all, me, 1, 0, to_mate)]
    for copy in o_copies:
        copy.start()
    d_all[me] = (d_keep[...].reshape(SLOTS, HALF) + d_recv[...].reshape(SLOTS, HALF)).astype(BF16)
    d_copies = [remote(d_all, me, 0, 1, to_across), remote(d_all, me, 1, 1, to_mate)]
    for copy in d_copies:
        copy.start()

    mine = pl.ds(pl.multiple_of(side * HALF, HALF), HALF)
    theirs = pl.ds(pl.multiple_of((1 - side) * HALF, HALF), HALF)
    home = pl.ds(pl.multiple_of(me * TOK, TOK), TOK)
    x_wide = x_ref[...].astype(F32)
    inv_rms = inv_rms_of(x_wide)
    x_half = x_ref[:, mine].astype(F32)
    dy_half = dy_ref[:, mine].astype(F32)
    gate = to_col(meta[2:3, home])
    flat = to_col(meta[1:2, home]).astype(jnp.int32)
    pick = (lax.broadcasted_iota(jnp.int32, (TOK, SHARDS * SLOTS), 1) == flat).astype(F32).astype(BF16)

    o_copies[0].wait_recv()
    o_forward = remote(o_all, across, 2, 0, to_mate)
    o_forward.start()
    o_copies[1].wait_recv()
    o_forward.wait_recv()
    tok_out = mm(pick, o_all[...].reshape(SHARDS * SLOTS, HALF))
    dg_mine[...] = to_row(jnp.sum(dy_half * tok_out, axis=1, keepdims=True))
    slot = side * SHARDS + me
    dg_copies = [pltpu.make_async_remote_copy(src_ref=dg_mine, dst_ref=dg_all.at[slot], send_sem=g_send_sem.at[k], recv_sem=g_recv_sem.at[k], device_id=other, device_id_type=MESH) for k, other in enumerate(others)]
    for copy in dg_copies:
        copy.start()
    dg_all[slot] = dg_mine[...]
    y_half[...] = (x_half + s_ref[...] + gate * tok_out).astype(BF16)
    y_copy = twin(y_half, y_out.at[:, mine], 0)
    y_copy.start()
    y_out[:, mine] = y_half[...]

    d_copies[0].wait_recv()
    d_forward = remote(d_all, across, 2, 1, to_mate)
    d_forward.start()
    d_copies[1].wait_recv()
    d_forward.wait_recv()
    dn_routed = mm(pick, d_all[...].reshape(SHARDS * SLOTS, HALF))
    for copy in dg_copies:
        copy.wait_recv()
    dg = jnp.concatenate([dg_all[s, 0:1, :] + dg_all[SHARDS + s, 0:1, :] for s in range(SHARDS)], axis=1)
    expert = lax.broadcasted_iota(jnp.int32, (EXPERTS, SHARDS * TOK), 0)
    one_assign = (expert == meta[0:1, :].astype(jnp.int32)).astype(F32)
    d_logits = (dg * meta[2:3, :] * (one_assign - p_ref[...])).astype(BF16)
    home_one = (lax.broadcasted_iota(jnp.int32, (EXPERTS, TOK), 0) == meta[0:1, home].astype(jnp.int32)).astype(F32)
    dg_home = dg_all[me, 0:1, :] + dg_all[SHARDS + me, 0:1, :]
    d_logits_home = (dg_home * meta[2:3, home] * (home_one - p_ref[:, home])).astype(BF16)
    dn_router = mm(d_logits_home.T, wr_ref[mine, :], NT)
    d_normed = dns_ref[...] + dn_router + dn_routed
    np_part = jnp.sum(d_normed * x_half, axis=1, keepdims=True)
    np_mine[...] = to_row(np_part)
    np_copy = twin(np_mine, np_recv, 1)
    np_copy.start()
    gr_out[...] = mm(d_logits, n_ref[...])
    np_copy.wait_recv()
    norm_proj = (np_part + to_col(np_recv[0:1, :])) / DIM
    dx_half[...] = (dy_half + inv_rms * d_normed - x_half * inv_rms**3 * norm_proj).astype(BF16)
    dx_copy = twin(dx_half, dx_out.at[:, mine], 2)
    dx_copy.start()
    dx_out[:, mine] = dx_half[...]
    y_copy.wait_recv()
    dx_copy.wait_recv()
    for copy in o_copies + d_copies + [o_forward, d_forward] + dg_copies + [y_copy, np_copy, dx_copy]:
        copy.wait_send()


def finish_call(*args):
    return pl.pallas_call(
        finish_kernel,
        out_shape=(
            jax.ShapeDtypeStruct((TOK, DIM), BF16),
            jax.ShapeDtypeStruct((TOK, DIM), BF16),
            jax.ShapeDtypeStruct((EXPERTS, DIM), F32),
        ),
        in_specs=[VMEM] * 12,
        out_specs=(VMEM,) * 3,
        scratch_shapes=[
            pltpu.VMEM((SHARDS, SLOTS, HALF), BF16),
            pltpu.VMEM((SHARDS, SLOTS, HALF), BF16),
            pltpu.VMEM((8, TOK), F32),
            pltpu.VMEM((2 * SHARDS, 8, TOK), F32),
            pltpu.VMEM((8, TOK), F32),
            pltpu.VMEM((8, TOK), F32),
            pltpu.VMEM((TOK, HALF), BF16),
            pltpu.VMEM((TOK, HALF), BF16),
            pltpu.SemaphoreType.DMA((3, 2)),
            pltpu.SemaphoreType.DMA((3, 2)),
            pltpu.SemaphoreType.DMA((3,)),
            pltpu.SemaphoreType.DMA((3,)),
            pltpu.SemaphoreType.DMA((7,)),
            pltpu.SemaphoreType.DMA((7,)),
        ],
        compiler_params=pltpu.CompilerParams(collective_id=1, has_side_effects=True),
        name="finish_tokens",
    )(*args)


def solution(mesh):
    tok_spec = P(("dp", "ep"), None)
    id_spec = P(("dp", "ep"))
    in_specs = (tok_spec, tok_spec, id_spec, id_spec, P(None, None), P("ep", None, "etp"), P("ep", None, "etp"), P("ep", "etp", None), P(None, "etp"), P(None, "etp"), P("etp", None))
    out_specs = (tok_spec, tok_spec, P(("dp", "ep"), None, "etp"), P(("dp", "ep"), None, "etp"), P(("dp", "ep"), "etp", None), P("dp", "etp"), P("dp", "etp"), P(("dp", "etp"), None), P("dp", None))

    def local_step(x_in, y_grad, prim_exp, alt_exp, w_router, exp_gate, exp_up, exp_down, sh_gate, sh_up, sh_down):
        ids = jnp.concatenate([prim_exp[None], alt_exp[None], jnp.zeros((6, TOK), jnp.int32)], axis=0)
        x_all, dy_all, ids_all, s_half, dns_half = gather_call(x_in, y_grad, ids, sh_gate, sh_up, sh_down)
        o_send, o_keep, xs, us, act_gate, act_up, hidden, normed, meta, probs = forward_call(x_all, dy_all, ids_all, w_router, exp_gate, exp_up, exp_down)
        swap = [(0, 1), (1, 0)]
        o_recv = lax.ppermute(o_send, "etp", swap)
        d_send, d_keep, d_gate, d_up = backward_call(us, act_gate, act_up, exp_gate, exp_up, exp_down)
        d_recv = lax.ppermute(d_send, "etp", swap)
        g_gate, g_up, g_down, gs_gate, gs_up, gs_down = grads_call(xs, us, hidden, d_gate, d_up, normed, dy_all, sh_gate, sh_up, sh_down)
        y_out, x_grad, g_router = finish_call(o_keep, o_recv, d_keep, d_recv, x_in, y_grad, s_half, dns_half, meta, probs, normed, w_router)
        return (y_out, x_grad, g_gate, g_up, g_down, gs_gate, gs_up, gs_down, g_router.T)

    return jax.shard_map(local_step, mesh=mesh, in_specs=in_specs, out_specs=out_specs, check_vma=False)
```

time: 249 us -> 91.9 us (0.37)
  waiting for transfers between devices: 75.9 us -> 0.01 us
  blocking collectives: 71.3 us -> 0 us
  Pallas kernels: 0 us -> 68.6 us
  matrix products: 37.7 us -> 0 us
  between operations: 15.3 us -> 0.79 us
  other arithmetic: 15.2 us -> 1.41 us
  starting transfers between devices: 14.3 us -> 2.04 us
    pallas_call x0 -> x5, Pallas kernels: none -> 68.6 us  [the longest x1 22.1 us: finish_call(): pl.pallas_call(finish_kernel, out_shape=(jax.ShapeDtypeStruct((TOK, DIM),...]
    psum x2 -> x0, waiting for transfers between devices: 50.5 us -> none  [the longest x1 50.5 us: local_step(): lax.psum(jnp.einsum('td,tf->df', normed, sh_d_gate, preferred_element_typ...]
    psum x1 -> x0, blocking collectives: 40.5 us -> none  [local_step(): lax.psum(jnp.einsum('ecf,efd->ecd', hidden, exp_down, preferred_element_t...]
    dot_general x21 -> x0, matrix products: 37.7 us -> none  [the longest x1 5.61 us: local_step(): jnp.einsum('ecd,ecf->edf', expert_rows, d_up, preferred_element_type=F32)]
    all_to_all x4 -> x0, waiting for transfers between devices: 25.3 us -> none  [the longest x2 13.5 us: send_back(): lax.all_to_all(flat_rows.reshape(ep_size, tok_local, model_dim), 'ep', 0,...]
    all_gather x2 -> x0, blocking collectives: 19.8 us -> none  [the longest x1 11.7 us: local_step(): all_slot = lax.all_gather(slot_idx, 'ep', tiled=True)]
    all_to_all x4 -> x0, starting transfers between devices: 14.2 us -> none  [the longest x2 7.17 us: send_back(): lax.all_to_all(flat_rows.reshape(ep_size, tok_local, model_dim), 'ep', 0,...]
    unnamed x2 -> x0, blocking collectives: 11 us -> none
  transfers between devices with their start and end apart: 6 -> 2, of which waited for: 4 -> 0; matrix products, arithmetic and copies ran while one was open for 20% -> 0% of each run, Pallas kernels for 0% -> 20%
where the time goes in v1:
time: 91.9 us; the launch traced here: 91.4 us
  Pallas kernels  68.6 us (75%)
  local copies, waits for them, and re-layouts  18.6 us (20%)
  starting transfers between devices  2.04 us (2%)
  other arithmetic  1.41 us (2%)
    pallas_call x1, Pallas kernels, finish_call(): pl.pallas_call(finish_kernel, out_shape=(jax.ShapeDtypeStruct((TOK, DIM),...  22.1 us
    pallas_call x1, Pallas kernels, gather_call(): pl.pallas_call(gather_kernel, out_shape=(jax.ShapeDtypeStruct((SHARDS, TO...  20.4 us
    unnamed x44, local copies, waits for them, and re-layouts  18.5 us
    pallas_call x1, Pallas kernels, grads_call(): pl.pallas_call(grads_kernel, grid=(OWN,), out_shape=(jax.ShapeDtypeStruct...  12.7 us
    pallas_call x1, Pallas kernels, forward_call(): pl.pallas_call(forward_kernel, grid=(OWN // 2,), out_shape=(jax.ShapeDtyp...  7.91 us
    pallas_call x1, Pallas kernels, backward_call(): pl.pallas_call(backward_kernel, grid=(OWN // 2,), out_shape=(jax.ShapeDty...  5.44 us
  transfers between devices with their start and end apart: 2, of which 0 were waited for; matrix products, arithmetic and copies ran while one was open for 0% of the time, Pallas kernels for 20%

profile of v1, /device:TPU:0, one launch (start us, length us, event | category | flops | bytes accessed | tf_op | source)
XLA Modules:
  0.0 91.4 jit_solution(12630273354908174460)
XLA Ops:
  0.7 1.0 %copy.20.wr_ref = bf16[1024,32]{1,0:T(8,128)(2,1)S(1)} copy(bf16[1024,32]{0,1:T(8,128)(2,1)} %param.15) | data formatting | bytes 131072 | tf_op args[4]
  1.8 1.4 %add_add_fusion.ids_ref = s32[8,128]{1,0:T(8,128)} fusion(s32[1,128]{1,0:T(1,128)} %bitcast.4, s32[1,128]{1,0:T(1,128)} %bitcast.5, s32[8]{0:T(128)S(1)} %pad.2.clone), kind=kLoop, calls=%fused_computation | loop fusion | flops 2048 | bytes 5152 | tf_op jit(solution)/shard_map/concatenate | solution.py:458
  3.2 20.4 %gather_tokens.1 = (bf16[4,128,1024]{2,1,0:T(8,128)(2,1)}, bf16[4,128,1024]{2,1,0:T(8,128)(2,1)}, s32[4,8,128]{2,1,0:T(8,128)}, f32[128,512]{1,0:T(8,128)}, f32[128,512]{1,0:T(8,128)}) custom-call(bf16[128,1024]{1,0:T(8,128)(2,1)} %x_ref.3, bf16[128,1024]{1,0:T(8,128)(2,1)} %dy_ref.3, s32[8,128]{1,0:T(8,128)} %add_add_fusion.ids_ref, bf16[1024,256]{1,0:T(8,128)(2,1)} %sg.1, ...), custom_call_target="tpu_custom_call" | custom-call | tf_op jit(solution)/shard_map/gather_tokens/pallas_call | solution.py:132
  23.6 1.4 %copy-done.5 = bf16[4,128,1024]{2,1,0:T(8,128)(2,1)S(1)} copy-done((bf16[4,128,1024]{2,1,0:T(8,128)(2,1)S(1)}, bf16[4,128,1024]{2,1,0:T(8,128)(2,1)}, u32[]{:S(2)}) %copy-start.5) | copy-done | bytes 1048600
  25.0 1.9 %copy-done.7 = bf16[4,128,1024]{2,1,0:T(8,128)(2,1)S(1)} copy-done((bf16[4,128,1024]{2,1,0:T(8,128)(2,1)S(1)}, bf16[4,128,1024]{2,1,0:T(8,128)(2,1)}, u32[]{:S(2)}) %copy-start.7) | copy-done | bytes 1048600
  26.9 0.7 copy-done.17
  27.6 7.9 %expert_forward.1 = (f32[4,40,512]{2,1,0:T(8,128)S(1)}, f32[4,40,512]{2,1,0:T(8,128)S(1)}, bf16[256,1024]{1,0:T(8,128)(2,1)S(1)}, bf16[256,1024]{1,0:T(8,128)(2,...) custom-call(bf16[4,128,1024]{2,1,0:T(8,128)(2,1)S(1)} %copy-done.7, ...), custom_call_target="tpu_custom_call" | custom-call | flops 402653184 | bytes 16777216 | tf_op jit(solution)/shard_map/expert_forward/pallas_call | solution.py:233
  35.5 0.6 copy-done.15
  36.1 0.6 copy-done.16
  36.8 1.0 %collective-permute-start = (f32[4,40,512]{2,1,0:T(8,128)S(1)}, f32[4,40,512]{2,1,0:T(8,128)S(1)}, u32[]{:S(2)}, u32[]{:S(2)}) collective-permute-start(f32[4,40,512]{2,1,0:T(8,128)S(1)} %get-tuple-element.41), channel_id=1, source_target_pairs={{0,4},{4,0},{1,5},{5,1},{2,6},{6,2},{3,7},{7,3}} | collective-permute-start | bytes 983048 | tf_op jit(solution)/shard_map/ppermute | solution.py:462
  37.7 2.2 %copy-done.2 = bf16[8,256,1024]{2,1,0:T(8,128)(2,1)S(1)} copy-done((bf16[8,256,1024]{2,1,0:T(8,128)(2,1)S(1)}, bf16[8,256,1024]{2,1,0:T(8,128)(2,1)}, u32[]{:S(2)}) %copy-start.2) | copy-done | bytes 4194328
  39.9 5.4 %expert_backward.1 = (f32[4,40,512]{2,1,0:T(8,128)S(1)}, f32[4,40,512]{2,1,0:T(8,128)S(1)}, bf16[8,32,256]{2,1,0:T(8,128)(2,1)S(1)}, bf16[8,32,256]{2,1,0:T(8,128)(2,1)S(1)}) custom-call(bf16[256,1024]{1,0:T(8,128)(2,1)S(1)} %get-tuple-element.42.us, f32[8,32,256]{2,1,0:T(8,128)S(1)} %get-tuple-element.43.a_in, f32[8,32,256]{2,1,0:T(8,128)S(1)} %get-tuple-element.44.b_in, ...), custom_call_target="tpu_custom_call" | custom-call | flops 402653184 | bytes 16777216 | tf_op jit(solution)/shard_map/expert_backward/pallas_call | solution.py:273
  45.4 1.1 %collective-permute-start.1 = (f32[4,40,512]{2,1,0:T(8,128)S(1)}, f32[4,40,512]{2,1,0:T(8,128)S(1)}, u32[]{:S(2)}, u32[]{:S(2)}) collective-permute-start(f32[4,40,512]{2,1,0:T(8,128)S(1)} %get-tuple-element.46), channel_id=1, source_target_pairs={{0,4},{4,0},{1,5},{5,1},{2,6},{6,2},{3,7},{7,3}} | collective-permute-start | bytes 983048 | tf_op jit(solution)/shard_map/ppermute | solution.py:464
  46.5 1.2 %copy-done.6 = bf16[4,128,1024]{2,1,0:T(8,128)(2,1)S(1)} copy-done((bf16[4,128,1024]{2,1,0:T(8,128)(2,1)S(1)}, bf16[4,128,1024]{2,1,0:T(8,128)(2,1)}, u32[]{:S(2)}) %copy-start.6) | copy-done | bytes 1048600
  47.7 1.0 %copy-done.9 = bf16[1024,256]{1,0:T(8,128)(2,1)S(1)} copy-done((bf16[1024,256]{1,0:T(8,128)(2,1)S(1)}, bf16[1024,256]{1,0:T(8,128)(2,1)}, u32[]{:S(2)}) %copy-start.9) | copy-done | bytes 524312
  48.7 1.0 %copy-done.10 = bf16[256,1024]{1,0:T(8,128)(2,1)S(1)} copy-done((bf16[256,1024]{1,0:T(8,128)(2,1)S(1)}, bf16[256,1024]{1,0:T(8,128)(2,1)}, u32[]{:S(2)}) %copy-start.10) | copy-done | bytes 524312
  49.8 1.0 %copy-done.12 = bf16[256,1024]{1,0:T(8,128)(2,1)S(1)} copy-done((bf16[256,1024]{1,0:T(8,128)(2,1)S(1)}, bf16[256,1024]{1,0:T(8,128)(2,1)}, u32[]{:S(2)}) %copy-start.12) | copy-done | bytes 524312
  50.8 12.7 %weight_grads.1 = (f32[8,1024,256]{2,1,0:T(8,128)}, f32[8,1024,256]{2,1,0:T(8,128)}, f32[8,256,1024]{2,1,0:T(8,128)}, f32[1024,256]{1,0:T(8,128)}, f32[1024,256]{1,0:T(8,128)}, /*index=5*/f32[256,1024]{1,0:T(8,128)}) custom-call(bf16[256,1024]{1,0:T(8,128)(2,1)S(1)} %get-tuple-element.54.xs, bf16[256,1024]{1,0:T(8,128)(2,1)S(1)} %copy-done.12, ...), custom_call_target="tpu_custom_call" | custom-call | flops 8589934592 | bytes 33554432 | tf_op jit(solution)/shard_map/weight_grads/pallas_call | solution.py:314
  63.5 0.7 copy-done.18
  64.2 0.1 copy-done.19
  64.4 22.1 %finish_tokens.1 = (bf16[128,1024]{1,0:T(8,128)(2,1)}, bf16[128,1024]{1,0:T(8,128)(2,1)}, f32[32,1024]{1,0:T(8,128)}) custom-call(f32[4,40,512]{2,1,0:T(8,128)} %copy-done.13, f32[4,40,512]{2,1,0:T(8,128)} %copy-done.18, f32[4,40,512]{2,1,0:T(8,128)} %copy-done.14, f32[4,40,512]{2,1,0:T(8,128)} %copy-done.19, bf16[128,1024]{1,0:T(8,128)(2,1)} %x_ref.3, ...), custom_call_target="tpu_custom_call" | custom-call | tf_op jit(solution)/shard_map/finish_tokens/pallas_call | solution.py:421
  86.5 1.7 %copy.25 = bf16[128,1024]{1,0:T(8,128)(2,1)} copy(bf16[128,1024]{1,0:T(8,128)(2,1)} %get-tuple-element.74) | data formatting | bytes 524288
  88.1 1.7 %copy.26 = bf16[128,1024]{1,0:T(8,128)(2,1)} copy(bf16[128,1024]{1,0:T(8,128)(2,1)} %get-tuple-element.75) | data formatting | bytes 524288
  89.8 1.6 %copy.27 = f32[1024,32]{0,1:T(8,128)} copy(f32[1024,32]{0,1:T(8,128)} %bitcast.3) | data formatting | bytes 262144
  (32 shorter events, 0.1 us)
Async XLA Ops:
  1.7 33.8 %copy-start.3 = (bf16[1024,32]{1,0:T(8,128)(2,1)}, bf16[1024,32]{1,0:T(8,128)(2,1)S(1)}, u32[]{:S(2)}) copy-start(bf16[1024,32]{1,0:T(8,128)(2,1)S(1)} %copy.20.wr_ref) | copy-start | bytes 196612
  23.6 14.1 %copy-start = (bf16[8,1024,256]{2,1,0:T(8,128)(2,1)S(1)}, bf16[8,1024,256]{2,1,0:T(8,128)(2,1)}, u32[]{:S(2)}) copy-start(bf16[8,1024,256]{2,1,0:T(8,128)(2,1)} %wg.3) | copy-start | bytes 12582916
  23.6 14.1 %copy-start.1 = (bf16[8,1024,256]{2,1,0:T(8,128)(2,1)S(1)}, bf16[8,1024,256]{2,1,0:T(8,128)(2,1)}, u32[]{:S(2)}) copy-start(bf16[8,1024,256]{2,1,0:T(8,128)(2,1)} %wu.3) | copy-start | bytes 12582916
  23.6 1.4 %copy-start.5 = (bf16[4,128,1024]{2,1,0:T(8,128)(2,1)S(1)}, bf16[4,128,1024]{2,1,0:T(8,128)(2,1)}, u32[]{:S(2)}) copy-start(bf16[4,128,1024]{2,1,0:T(8,128)(2,1)} %get-tuple-element.38.dy_ref) | copy-start | bytes 3145732
  25.0 1.9 %copy-start.7 = (bf16[4,128,1024]{2,1,0:T(8,128)(2,1)S(1)}, bf16[4,128,1024]{2,1,0:T(8,128)(2,1)}, u32[]{:S(2)}) copy-start(bf16[4,128,1024]{2,1,0:T(8,128)(2,1)} %get-tuple-element.37.x_ref) | copy-start | bytes 3145732
  26.9 0.7 copy-start.17
  27.6 18.9 %copy-start.8 = (bf16[1024,256]{1,0:T(8,128)(2,1)S(1)}, bf16[1024,256]{1,0:T(8,128)(2,1)}, u32[]{:S(2)}) copy-start(bf16[1024,256]{1,0:T(8,128)(2,1)} %sg.1) | copy-start | bytes 1572868
  35.5 0.6 copy-start.15
  36.1 0.6 copy-start.16
  36.7 9.7 %copy-start.11 = (bf16[256,1024]{1,0:T(8,128)(2,1)}, bf16[256,1024]{1,0:T(8,128)(2,1)S(1)}, u32[]{:S(2)}) copy-start(bf16[256,1024]{1,0:T(8,128)(2,1)S(1)} %get-tuple-element.42.us) | copy-start | bytes 1572868
  36.8 9.7 %copy-start.13 = (f32[4,40,512]{2,1,0:T(8,128)}, f32[4,40,512]{2,1,0:T(8,128)S(1)}, u32[]{:S(2)}) copy-start(f32[4,40,512]{2,1,0:T(8,128)S(1)} %get-tuple-element.40.o_keep) | copy-start | bytes 983044
  36.8 26.7 %copy-start.4 = (bf16[512,1024]{1,0:T(8,128)(2,1)}, bf16[512,1024]{1,0:T(8,128)(2,1)S(1)}, u32[]{:S(2)}) copy-start(bf16[512,1024]{1,0:T(8,128)(2,1)S(1)} %get-tuple-element.51.n_ref) | copy-start | bytes 3145732
  36.8 26.7 %collective-permute-start = (f32[4,40,512]{2,1,0:T(8,128)S(1)}, f32[4,40,512]{2,1,0:T(8,128)S(1)}, u32[]{:S(2)}, u32[]{:S(2)}) collective-permute-start(f32[4,40,512]{2,1,0:T(8,128)S(1)} %get-tuple-element.41), channel_id=1, source_target_pairs={{0,4},{4,0},{1,5},{5,1},{2,6},{6,2},{3,7},{7,3}} | collective-permute-start | bytes 983048 | tf_op jit(solution)/shard_map/ppermute | solution.py:462
  37.7 2.2 %copy-start.2 = (bf16[8,256,1024]{2,1,0:T(8,128)(2,1)S(1)}, bf16[8,256,1024]{2,1,0:T(8,128)(2,1)}, u32[]{:S(2)}) copy-start(bf16[8,256,1024]{2,1,0:T(8,128)(2,1)} %wd.3) | copy-start | bytes 12582916
  45.4 18.1 %copy-start.14 = (f32[4,40,512]{2,1,0:T(8,128)}, f32[4,40,512]{2,1,0:T(8,128)S(1)}, u32[]{:S(2)}) copy-start(f32[4,40,512]{2,1,0:T(8,128)S(1)} %get-tuple-element.45.d_keep) | copy-start | bytes 983044
  45.4 18.1 %collective-permute-start.1 = (f32[4,40,512]{2,1,0:T(8,128)S(1)}, f32[4,40,512]{2,1,0:T(8,128)S(1)}, u32[]{:S(2)}, u32[]{:S(2)}) collective-permute-start(f32[4,40,512]{2,1,0:T(8,128)S(1)} %get-tuple-element.46), channel_id=1, source_target_pairs={{0,4},{4,0},{1,5},{5,1},{2,6},{6,2},{3,7},{7,3}} | collective-permute-start | bytes 983048 | tf_op jit(solution)/shard_map/ppermute | solution.py:464
  46.5 1.2 %copy-start.6 = (bf16[4,128,1024]{2,1,0:T(8,128)(2,1)S(1)}, bf16[4,128,1024]{2,1,0:T(8,128)(2,1)}, u32[]{:S(2)}) copy-start(bf16[4,128,1024]{2,1,0:T(8,128)(2,1)} %get-tuple-element.38.dy_ref) | copy-start | bytes 3145732
  47.7 1.0 %copy-start.9 = (bf16[1024,256]{1,0:T(8,128)(2,1)S(1)}, bf16[1024,256]{1,0:T(8,128)(2,1)}, u32[]{:S(2)}) copy-start(bf16[1024,256]{1,0:T(8,128)(2,1)} %su.1) | copy-start | bytes 1572868
  48.7 1.0 %copy-start.10 = (bf16[256,1024]{1,0:T(8,128)(2,1)S(1)}, bf16[256,1024]{1,0:T(8,128)(2,1)}, u32[]{:S(2)}) copy-start(bf16[256,1024]{1,0:T(8,128)(2,1)} %sd.1) | copy-start | bytes 1572868
  49.8 1.0 %copy-start.12 = (bf16[256,1024]{1,0:T(8,128)(2,1)S(1)}, bf16[256,1024]{1,0:T(8,128)(2,1)}, u32[]{:S(2)}) copy-start(bf16[256,1024]{1,0:T(8,128)(2,1)} %copy-done.11) | copy-start | bytes 1572868
  63.5 0.7 copy-start.18
  63.5 0.8 copy-start.19

commit v2 on v0

v2 whole, which is shorter than its diff:
```python
import functools

import jax
import jax.numpy as jnp
from jax import lax
from jax.experimental import pallas as pl
from jax.experimental.pallas import tpu as pltpu
from jax.sharding import PartitionSpec as P

EPS = 1e-5
F32 = jnp.float32
BF16 = jnp.bfloat16
MESH = pl.DeviceIdType.MESH
ANY = pl.BlockSpec(memory_space=pl.ANY)
VMEM = pl.BlockSpec(memory_space=pltpu.VMEM)
NN = (((1,), (0,)), ((), ()))
NT = (((1,), (1,)), ((), ()))
TN = (((0,), (0,)), ((), ()))

SHARDS = 4
TOK = 128
DIM = 1024
HALF = 512
EXPERTS = 32
OWN = 8
CAP = 20
PAD = 32
SLOTS = OWN * CAP


def mm(a, b, dims=NN):
    return lax.dot_general(a, b, dims, preferred_element_type=F32)


def inv_rms_of(x_wide):
    return lax.rsqrt(jnp.mean(x_wide * x_wide, axis=1, keepdims=True) + EPS)


def glu_grads(d_hidden, act_gate, act_up):
    sig_gate = jax.nn.sigmoid(act_gate)
    d_gate = (d_hidden * act_up * sig_gate * (1.0 + act_gate * (1.0 - sig_gate))).astype(BF16)
    d_up = (d_hidden * act_gate * sig_gate).astype(BF16)
    return d_gate, d_up


def to_row(col):
    return jnp.transpose(jnp.broadcast_to(col, (TOK, TOK)))[:8]


def to_col(row):
    return jnp.transpose(jnp.broadcast_to(row, (TOK, TOK)))[:, :1]


def barrier(peers):
    sem = pltpu.get_barrier_semaphore()
    for peer in peers:
        pl.semaphore_signal(sem, inc=1, device_id=peer, device_id_type=MESH)
    pl.semaphore_wait(sem, len(peers))


def layer_kernel(x_hbm, dy_hbm, prim_hbm, alt_hbm, wr_hbm, wg_hbm, wu_hbm, wd_hbm, sg_hbm, su_hbm, sd_hbm,
                 y_out, dx_out, gr_out, xs_hbm, us_hbm, h_hbm, da_hbm, db_hbm, n_hbm, dy_all_hbm, sh_hbm, sda_hbm, sdb_hbm,
                 x_all, dy_all, ids_all, wr, wg, wu, wd, sg, su, sd, n_all, xs, us, acts, acts_up, hid, da, db, hid_s, da_s, db_s,
                 probs, meta, s_send, s_recv, s_keep, n_send, n_recv, n_keep, o_send, o_recv, o_keep, d_send, d_recv, d_keep,
                 o_all, d_all, dg_mine, dg_all, np_mine, np_recv, y_half, dx_half,
                 in_sem, w_sem, out_sem, send_sem, recv_sem, r_send_sem, r_recv_sem, y_send_sem, y_recv_sem, g_send_sem, g_recv_sem):
    me = lax.axis_index("ep")
    side = lax.axis_index("etp")
    total = SHARDS * TOK
    mate = jnp.bitwise_xor(me, 1)
    across = jnp.bitwise_xor(me, 2)
    to_mate, to_across, to_twin = {"ep": mate}, {"ep": across}, {"etp": 1 - side}
    others = [{"etp": jnp.bitwise_xor(side, k // SHARDS), "ep": jnp.bitwise_xor(me, k % SHARDS)} for k in range(1, 2 * SHARDS)]
    theirs = pl.ds(pl.multiple_of((1 - side) * HALF, HALF), HALF)
    mine = pl.ds(pl.multiple_of(side * HALF, HALF), HALF)
    home = pl.ds(pl.multiple_of(me * TOK, TOK), TOK)

    loads = [pltpu.make_async_copy(src, dst, in_sem.at[k]) for k, (src, dst) in enumerate((
        (x_hbm, x_all.at[me]), (prim_hbm, ids_all.at[me, 0:1]), (alt_hbm, ids_all.at[me, 1:2]), (dy_hbm, dy_all.at[me]),
        (sg_hbm, sg), (su_hbm, su), (sd_hbm, sd), (wr_hbm, wr)))]
    for load in loads:
        load.start()
    w_loads = [[pltpu.make_async_copy(src.at[e], dst.at[e], w_sem.at[k, e]) for k, (src, dst) in enumerate(((wg_hbm, wg), (wu_hbm, wu), (wd_hbm, wd)))] for e in range(OWN)]
    for group in w_loads:
        for load in group:
            load.start()
    barrier(others)

    def remote(view, lane, k, target):
        return pltpu.make_async_remote_copy(src_ref=view, dst_ref=view, send_sem=send_sem.at[lane, k], recv_sem=recv_sem.at[lane, k], device_id=target, device_id_type=MESH)

    def ret(buf, shard, chunk, lane, k, target):
        view = buf.at[shard, chunk * (SLOTS // 2) : (chunk + 1) * (SLOTS // 2)]
        return pltpu.make_async_remote_copy(src_ref=view, dst_ref=view, send_sem=r_send_sem.at[lane, k], recv_sem=r_recv_sem.at[lane, k], device_id=target, device_id_type=MESH)

    def twin(src, dst, k):
        return pltpu.make_async_remote_copy(src_ref=src, dst_ref=dst, send_sem=y_send_sem.at[k], recv_sem=y_recv_sem.at[k], device_id=to_twin, device_id_type=MESH)

    def pieces(shard):
        rows = TOK // 2
        return [ids_all.at[shard], x_all.at[shard, :rows], x_all.at[shard, rows:], dy_all.at[shard, :rows], dy_all.at[shard, rows:]]

    out_across = [remote(view, 0, k, to_across) for k, view in enumerate(pieces(me))]
    out_mate = [remote(view, 1, k, to_mate) for k, view in enumerate(pieces(me))]
    forwards = [remote(view, 2, k, to_mate) for k, view in enumerate(pieces(across))]
    for load in loads[:3]:
        load.wait()
    for k in range(3):
        out_across[k].start()
        out_mate[k].start()
    loads[3].wait()
    for k in range(3, 5):
        out_across[k].start()
        out_mate[k].start()

    x_wide = x_all[me].astype(F32)
    inv_rms = inv_rms_of(x_wide)
    normed = (x_wide * inv_rms).astype(BF16)
    for load in loads[4:7]:
        load.wait()
    act_gate = mm(normed, sg[...])
    act_up = mm(normed, su[...])
    hidden = (jax.nn.silu(act_gate) * act_up).astype(BF16)
    d_gate, d_up = glu_grads(mm(dy_all[me], sd[...], NT), act_gate, act_up)
    n_send[...] = mm(d_gate, sg[theirs, :], NT) + mm(d_up, su[theirs, :], NT)
    n_copy = twin(n_send, n_recv, 0)
    n_copy.start()
    s_send[...] = mm(hidden, sd[:, theirs])
    s_copy = twin(s_send, s_recv, 1)
    s_copy.start()
    n_keep[...] = mm(d_gate, sg[mine, :], NT) + mm(d_up, su[mine, :], NT)
    s_keep[...] = mm(hidden, sd[:, mine])

    for k in range(3):
        out_across[k].wait_recv()
        forwards[k].start()
    for k in range(3):
        out_mate[k].wait_recv()
        forwards[k].wait_recv()

    x_wide = x_all[...].reshape(total, DIM).astype(F32)
    n_all[...] = (x_wide * inv_rms_of(x_wide)).astype(BF16)
    loads[7].wait()
    logits = mm(n_all[...], wr[...], NT)
    top = jnp.max(logits, axis=1, keepdims=True)
    expo = jnp.exp(logits - top)
    share = expo / jnp.sum(expo, axis=1, keepdims=True)
    wide = jnp.concatenate([share, jnp.zeros((total, TOK - EXPERTS), F32)], axis=1)
    probs_t = jnp.concatenate([jnp.transpose(wide[s * TOK : (s + 1) * TOK])[:EXPERTS] for s in range(SHARDS)], axis=1)
    probs[...] = probs_t
    prim = jnp.concatenate([ids_all[s, 0:1, :] for s in range(SHARDS)], axis=1)
    alt = jnp.concatenate([ids_all[s, 1:2, :] for s in range(SHARDS)], axis=1)
    expert = lax.broadcasted_iota(jnp.int32, (EXPERTS, total), 0)
    before = (lax.broadcasted_iota(jnp.int32, (total, total), 0) < lax.broadcasted_iota(jnp.int32, (total, total), 1)).astype(F32).astype(BF16)
    one_prim = (expert == prim).astype(F32)
    rank_prim = jnp.sum(one_prim * mm(one_prim.astype(BF16), before), axis=0, keepdims=True)
    keep_prim = rank_prim < CAP
    kept = jnp.minimum(jnp.sum(one_prim, axis=1, keepdims=True), float(CAP))
    one_alt = jnp.where(keep_prim, 0.0, (expert == alt).astype(F32))
    slot_alt = jnp.sum(one_alt * (mm(one_alt.astype(BF16), before) + kept), axis=0, keepdims=True)
    keep_alt = jnp.logical_and(jnp.logical_not(keep_prim), slot_alt < CAP)
    assign = jnp.where(keep_prim, prim, jnp.where(keep_alt, alt, -1))
    slot = jnp.where(keep_prim, rank_prim, slot_alt).astype(jnp.int32)
    gate = jnp.sum(jnp.where(expert == assign, probs_t, 0.0), axis=0, keepdims=True)
    flat = jnp.where(assign >= 0, assign * CAP + slot, -1)
    meta[0:1] = assign.astype(F32)
    meta[1:2] = flat.astype(F32)
    meta[2:3] = gate
    local = assign - me * OWN
    owned = jnp.logical_and(local >= 0, local < OWN)
    target = jnp.where(owned, local * PAD + slot, -1)
    picked = lax.broadcasted_iota(jnp.int32, (OWN * PAD, total), 0) == target
    pick_own = picked.astype(F32).astype(BF16)
    gate_slot = jnp.sum(jnp.where(picked, gate, 0.0), axis=1, keepdims=True)
    xs[...] = mm(pick_own, n_all[...]).astype(BF16)

    o_copies, d_copies = [], []
    for e in range(OWN):
        for load in w_loads[e]:
            load.wait()
        rows = slice(e * PAD, (e + 1) * PAD)
        act_gate = mm(xs[rows, :], wg[e])
        act_up = mm(xs[rows, :], wu[e])
        hidden = (jax.nn.silu(act_gate) * act_up).astype(BF16)
        acts[rows, :] = act_gate
        acts_up[rows, :] = act_up
        hid[rows, :] = hidden
        part = slice(e * CAP, (e + 1) * CAP)
        o_send[part, :] = mm(hidden, wd[e, :, theirs])[:CAP]
        o_keep[part, :] = mm(hidden, wd[e, :, mine])[:CAP]
        if e % 2:
            chunk = slice((e - 1) * CAP, (e + 1) * CAP)
            o_copies.append(twin(o_send.at[chunk], o_recv.at[chunk], 2 + e // 2))
            o_copies[-1].start()
        if e in (1, 4):
            k = 3 if e == 1 else 4
            out_across[k].wait_recv()
            forwards[k].start()
    for k in range(3, 5):
        out_mate[k].wait_recv()
        forwards[k].wait_recv()
    us[...] = (gate_slot * mm(pick_own, dy_all[...].reshape(total, DIM))).astype(BF16)

    returns = []

    def give_back(buf, keep, recv, copies, chunk, base):
        for copy in copies[2 * chunk : 2 * chunk + 2]:
            copy.wait_recv()
        rows = slice(chunk * (SLOTS // 2), (chunk + 1) * (SLOTS // 2))
        buf[me, rows] = (keep[rows, :] + recv[rows, :]).astype(BF16)
        k = base + chunk
        first, second = ret(buf, me, chunk, 0, k, to_across), ret(buf, me, chunk, 1, k, to_mate)
        first.start()
        second.start()
        third = ret(buf, across, chunk, 2, k, to_mate)
        returns.extend((first, second, third))
        return first, second, third

    def pass_on(group):
        group[0].wait_recv()
        group[2].start()

    o_back = []
    for e in range(OWN):
        rows = slice(e * PAD, (e + 1) * PAD)
        d_gate, d_up = glu_grads(mm(us[rows, :], wd[e], NT), acts[rows, :], acts_up[rows, :])
        da[rows, :] = d_gate
        db[rows, :] = d_up
        part = slice(e * CAP, (e + 1) * CAP)
        d_send[part, :] = (mm(d_gate, wg[e, theirs, :], NT) + mm(d_up, wu[e, theirs, :], NT))[:CAP]
        d_keep[part, :] = (mm(d_gate, wg[e, mine, :], NT) + mm(d_up, wu[e, mine, :], NT))[:CAP]
        if e % 2:
            chunk = slice((e - 1) * CAP, (e + 1) * CAP)
            d_copies.append(twin(d_send.at[chunk], d_recv.at[chunk], 6 + e // 2))
            d_copies[-1].start()
        if e == 5:
            o_back.append(give_back(o_all, o_keep, o_recv, o_copies, 0, 0))

    saves = [pltpu.make_async_copy(src, dst, out_sem.at[k]) for k, (src, dst) in enumerate((
        (xs, xs_hbm), (us, us_hbm), (hid, h_hbm), (da, da_hbm), (db, db_hbm), (n_all, n_hbm), (dy_all, dy_all_hbm), (hid_s, sh_hbm), (da_s, sda_hbm), (db_s, sdb_hbm)))]
    for save in saves[:7]:
        save.start()
    act_gate = mm(n_all[...], sg[...])
    act_up = mm(n_all[...], su[...])
    hid_s[...] = (jax.nn.silu(act_gate) * act_up).astype(BF16)
    d_gate, d_up = glu_grads(mm(dy_all[...].reshape(total, DIM), sd[...], NT), act_gate, act_up)
    da_s[...] = d_gate
    db_s[...] = d_up
    for save in saves[7:]:
        save.start()

    o_back.append(give_back(o_all, o_keep, o_recv, o_copies, 1, 0))
    pass_on(o_back[0])
    x_half = x_all[me, :, mine].astype(F32)
    dy_half = dy_all[me, :, mine].astype(F32)
    gate_home = to_col(meta[2:3, home])
    flat_home = to_col(meta[1:2, home]).astype(jnp.int32)
    pick = (lax.broadcasted_iota(jnp.int32, (TOK, SHARDS * SLOTS), 1) == flat_home).astype(F32).astype(BF16)
    pass_on(o_back[1])
    for group in o_back:
        group[1].wait_recv()
        group[2].wait_recv()
    tok_out = mm(pick, o_all[...].reshape(SHARDS * SLOTS, HALF))
    dg_mine[...] = to_row(jnp.sum(dy_half * tok_out, axis=1, keepdims=True))
    place = side * SHARDS + me
    dg_copies = [pltpu.make_async_remote_copy(src_ref=dg_mine, dst_ref=dg_all.at[place], send_sem=g_send_sem.at[k], recv_sem=g_recv_sem.at[k], device_id=other, device_id_type=MESH) for k, other in enumerate(others)]
    for copy in dg_copies:
        copy.start()
    dg_all[place] = dg_mine[...]
    s_copy.wait_recv()
    y_half[...] = (x_half + (s_keep[...] + s_recv[...]) + gate_home * tok_out).astype(BF16)
    y_copy = twin(y_half, y_out.at[:, mine], 10)
    y_copy.start()
    y_out[:, mine] = y_half[...]

    d_back = [give_back(d_all, d_keep, d_recv, d_copies, 0, 2)]
    for copy in dg_copies:
        copy.wait_recv()
    dg = jnp.concatenate([dg_all[s, 0:1, :] + dg_all[SHARDS + s, 0:1, :] for s in range(SHARDS)], axis=1)
    one_assign = (lax.broadcasted_iota(jnp.int32, (EXPERTS, total), 0) == meta[0:1, :].astype(jnp.int32)).astype(F32)
    d_logits = (dg * meta[2:3, :] * (one_assign - probs[...])).astype(BF16)
    home_one = (lax.broadcasted_iota(jnp.int32, (EXPERTS, TOK), 0) == meta[0:1, home].astype(jnp.int32)).astype(F32)
    dg_home = dg_all[me, 0:1, :] + dg_all[SHARDS + me, 0:1, :]
    d_logits_home = (dg_home * meta[2:3, home] * (home_one - probs[:, home])).astype(BF16)
    n_copy.wait_recv()
    d_normed = n_keep[...] + n_recv[...] + mm(d_logits_home, wr[:, mine], TN)
    pass_on(d_back[0])
    d_back.append(give_back(d_all, d_keep, d_recv, d_copies, 1, 2))
    gr_out[...] = mm(d_logits, n_all[...])
    pass_on(d_back[1])
    for group in d_back:
        group[1].wait_recv()
        group[2].wait_recv()
    d_normed = d_normed + mm(pick, d_all[...].reshape(SHARDS * SLOTS, HALF))
    np_part = jnp.sum(d_normed * x_half, axis=1, keepdims=True)
    np_mine[...] = to_row(np_part)
    np_copy = twin(np_mine, np_recv, 11)
    np_copy.start()
    np_copy.wait_recv()
    norm_proj = (np_part + to_col(np_recv[0:1, :])) / DIM
    dx_half[...] = (dy_half + inv_rms * d_normed - x_half * inv_rms**3 * norm_proj).astype(BF16)
    dx_copy = twin(dx_half, dx_out.at[:, mine], 12)
    dx_copy.start()
    dx_out[:, mine] = dx_half[...]
    for save in saves:
        save.wait()
    y_copy.wait_recv()
    dx_copy.wait_recv()
    for copy in out_across + out_mate + forwards + [n_copy, s_copy] + o_copies + d_copies + returns + dg_copies + [y_copy, np_copy, dx_copy]:
        copy.wait_send()


def layer_call(x_in, y_grad, prim, alt, wr_t, exp_gate, exp_up, exp_down, sh_gate, sh_up, sh_down):
    width = sh_gate.shape[1]
    total = SHARDS * TOK
    rows = OWN * PAD
    shape = jax.ShapeDtypeStruct
    dma = pltpu.SemaphoreType.DMA
    half_f32 = pltpu.VMEM((TOK, HALF), F32)
    slots_f32 = pltpu.VMEM((SLOTS, HALF), F32)
    return pl.pallas_call(
        layer_kernel,
        out_shape=(
            shape((TOK, DIM), BF16), shape((TOK, DIM), BF16), shape((EXPERTS, DIM), F32),
            shape((rows, DIM), BF16), shape((rows, DIM), BF16), shape((rows, width), BF16), shape((rows, width), BF16), shape((rows, width), BF16),
            shape((total, DIM), BF16), shape((SHARDS, TOK, DIM), BF16), shape((total, width), BF16), shape((total, width), BF16), shape((total, width), BF16),
        ),
        in_specs=[ANY] * 11,
        out_specs=(VMEM,) * 3 + (ANY,) * 10,
        scratch_shapes=[
            pltpu.VMEM((SHARDS, TOK, DIM), BF16), pltpu.VMEM((SHARDS, TOK, DIM), BF16), pltpu.VMEM((SHARDS, 8, TOK), jnp.int32), pltpu.VMEM((EXPERTS, DIM), BF16),
            pltpu.VMEM((OWN, DIM, width), BF16), pltpu.VMEM((OWN, DIM, width), BF16), pltpu.VMEM((OWN, width, DIM), BF16),
            pltpu.VMEM((DIM, width), BF16), pltpu.VMEM((DIM, width), BF16), pltpu.VMEM((width, DIM), BF16),
            pltpu.VMEM((total, DIM), BF16), pltpu.VMEM((rows, DIM), BF16), pltpu.VMEM((rows, DIM), BF16),
            pltpu.VMEM((rows, width), F32), pltpu.VMEM((rows, width), F32), pltpu.VMEM((rows, width), BF16), pltpu.VMEM((rows, width), BF16), pltpu.VMEM((rows, width), BF16),
            pltpu.VMEM((total, width), BF16), pltpu.VMEM((total, width), BF16), pltpu.VMEM((total, width), BF16),
            pltpu.VMEM((EXPERTS, total), F32), pltpu.VMEM((8, total), F32),
            half_f32, half_f32, half_f32, half_f32, half_f32, half_f32,
            slots_f32, slots_f32, slots_f32, slots_f32, slots_f32, slots_f32,
            pltpu.VMEM((SHARDS, SLOTS, HALF), BF16), pltpu.VMEM((SHARDS, SLOTS, HALF), BF16),
            pltpu.VMEM((8, TOK), F32), pltpu.VMEM((2 * SHARDS, 8, TOK), F32), pltpu.VMEM((8, TOK), F32), pltpu.VMEM((8, TOK), F32),
            pltpu.VMEM((TOK, HALF), BF16), pltpu.VMEM((TOK, HALF), BF16),
            dma((8,)), dma((3, OWN)), dma((10,)), dma((3, 5)), dma((3, 5)), dma((3, 4)), dma((3, 4)), dma((13,)), dma((13,)), dma((7,)), dma((7,)),
        ],
        compiler_params=pltpu.CompilerParams(collective_id=0, has_side_effects=True, vmem_limit_bytes=60 << 20),
        name="moe_layer",
    )(x_in, y_grad, prim, alt, wr_t, exp_gate, exp_up, exp_down, sh_gate, sh_up, sh_down)


def grads_kernel(xs, us, h_in, da_in, db_in, n_ref, dy_ref, hid_s, da_s, db_s, y_in, dx_in, gr_in, g_gate, g_up, g_down, gs_gate, gs_up, gs_down, y_out, dx_out, gr_out, sem):
    step = pl.program_id(0)
    moves = [pltpu.make_async_copy(src, dst, sem.at[k]) for k, (src, dst) in enumerate(((y_in, y_out), (dx_in, dx_out), (gr_in, gr_out)))]

    @pl.when(step == 0)
    def begin():
        for move in moves:
            move.start()

    g_down[0] = mm(h_in[...], us[...], TN)
    g_gate[0] = mm(xs[...], da_in[...], TN)
    g_up[0] = mm(xs[...], db_in[...], TN)
    gs_gate[...] = mm(n_ref[...], da_s[...], TN)
    gs_up[...] = mm(n_ref[...], db_s[...], TN)
    gs_down[...] = mm(hid_s[...], dy_ref[...], TN)

    @pl.when(step == pl.num_programs(0) - 1)
    def end():
        for move in moves:
            move.wait()


def grads_call(xs, us, hid, da, db, n_all, dy_all, hid_s, da_s, db_s, y_out, dx_out, gr_out):
    width = hid.shape[1]
    total = SHARDS * TOK
    block = DIM // OWN
    shape = jax.ShapeDtypeStruct
    whole = lambda *dims: pl.BlockSpec(dims, lambda i: (0,) * len(dims))
    one = lambda *dims: pl.BlockSpec((1,) + dims, lambda i: (i, 0, 0))
    slots = lambda cols: pl.BlockSpec((PAD, cols), lambda i: (i, 0))
    cols = lambda height: pl.BlockSpec((height, block), lambda i: (0, i))
    return pl.pallas_call(
        grads_kernel,
        grid=(OWN,),
        out_shape=(
            shape((OWN, DIM, width), F32), shape((OWN, DIM, width), F32), shape((OWN, width, DIM), F32),
            shape((DIM, width), F32), shape((DIM, width), F32), shape((width, DIM), F32),
            shape((TOK, DIM), BF16), shape((TOK, DIM), BF16), shape((EXPERTS, DIM), F32),
        ),
        in_specs=[slots(DIM), slots(DIM), slots(width), slots(width), slots(width), cols(total), cols(total), whole(total, width), whole(total, width), whole(total, width), VMEM, VMEM, VMEM],
        out_specs=(one(DIM, width), one(DIM, width), one(width, DIM), pl.BlockSpec((block, width), lambda i: (i, 0)), pl.BlockSpec((block, width), lambda i: (i, 0)), cols(width), ANY, ANY, ANY),
        scratch_shapes=[pltpu.SemaphoreType.DMA((3,))],
        compiler_params=pltpu.CompilerParams(dimension_semantics=("arbitrary",), vmem_limit_bytes=63 << 20),
        cost_estimate=pl.CostEstimate(flops=8 << 30, bytes_accessed=32 << 20, transcendentals=0),
        name="weight_grads",
    )(xs, us, hid, da, db, n_all, dy_all.reshape(total, DIM), hid_s, da_s, db_s, y_out, dx_out, gr_out)


def solution(mesh):
    tok_spec = P(("dp", "ep"), None)
    id_spec = P(("dp", "ep"))
    in_specs = (tok_spec, tok_spec, id_spec, id_spec, P(None, None), P("ep", None, "etp"), P("ep", None, "etp"), P("ep", "etp", None), P(None, "etp"), P(None, "etp"), P("etp", None))
    out_specs = (tok_spec, tok_spec, P(("dp", "ep"), None, "etp"), P(("dp", "ep"), None, "etp"), P(("dp", "ep"), "etp", None), P("dp", "etp"), P("dp", "etp"), P(("dp", "etp"), None), P("dp", None))

    def local_step(x_in, y_grad, prim_exp, alt_exp, w_router, exp_gate, exp_up, exp_down, sh_gate, sh_up, sh_down):
        y, dx, gr, *saved = layer_call(x_in, y_grad, prim_exp.reshape(1, TOK), alt_exp.reshape(1, TOK), w_router.T, exp_gate, exp_up, exp_down, sh_gate, sh_up, sh_down)
        g_gate, g_up, g_down, gs_gate, gs_up, gs_down, y_out, x_grad, g_router = grads_call(*saved, y, dx, gr)
        return (y_out, x_grad, g_gate, g_up, g_down, gs_gate, gs_up, gs_down, g_router.T)

    return jax.shard_map(local_step, mesh=mesh, in_specs=in_specs, out_specs=out_specs, check_vma=False)
```

time: 249 us -> 66.5 us (0.27)
  waiting for transfers between devices: 75.9 us -> 0 us
  blocking collectives: 71.3 us -> 0 us
  Pallas kernels: 0 us -> 65.6 us
  matrix products: 37.7 us -> 0 us
  local copies, waits for them, and re-layouts: 18.5 us -> 0 us
  other arithmetic: 15.2 us -> 0 us
  between operations: 15.3 us -> 0.65 us
  starting transfers between devices: 14.3 us -> 0 us
    pallas_call x0 -> x2, Pallas kernels: none -> 65.6 us  [the longest x1 52.1 us: layer_call(): pl.pallas_call(layer_kernel, out_shape=(shape((TOK, DIM), BF16), shape((T...]
    psum x2 -> x0, waiting for transfers between devices: 50.5 us -> none  [the longest x1 50.5 us: local_step(): lax.psum(jnp.einsum('td,tf->df', normed, sh_d_gate, preferred_element_typ...]
    psum x1 -> x0, blocking collectives: 40.5 us -> none  [local_step(): lax.psum(jnp.einsum('ecf,efd->ecd', hidden, exp_down, preferred_element_t...]
    dot_general x21 -> x0, matrix products: 37.7 us -> none  [the longest x1 5.61 us: local_step(): jnp.einsum('ecd,ecf->edf', expert_rows, d_up, preferred_element_type=F32)]
    all_to_all x4 -> x0, waiting for transfers between devices: 25.3 us -> none  [the longest x2 13.5 us: send_back(): lax.all_to_all(flat_rows.reshape(ep_size, tok_local, model_dim), 'ep', 0,...]
    all_gather x2 -> x0, blocking collectives: 19.8 us -> none  [the longest x1 11.7 us: local_step(): all_slot = lax.all_gather(slot_idx, 'ep', tiled=True)]
    all_to_all x4 -> x0, starting transfers between devices: 14.2 us -> none  [the longest x2 7.17 us: send_back(): lax.all_to_all(flat_rows.reshape(ep_size, tok_local, model_dim), 'ep', 0,...]
    unnamed x2 -> x0, blocking collectives: 11 us -> none
  transfers between devices with their start and end apart: 6 -> 0, of which waited for: 4 -> 0; matrix products, arithmetic and copies ran while one was open for 20% -> 0% of each run, Pallas kernels for 0% -> 0%
where the time goes in v2:
time: 66.5 us; the launch traced here: 66.2 us
  Pallas kernels  65.6 us (99%)
    pallas_call x1, Pallas kernels, layer_call(): pl.pallas_call(layer_kernel, out_shape=(shape((TOK, DIM), BF16), shape((T...  52.1 us
    pallas_call x1, Pallas kernels, grads_call(): pl.pallas_call(grads_kernel, grid=(OWN,), out_shape=(shape((OWN, DIM, wid...  13.4 us

profile of v2, /device:TPU:0, one launch (start us, length us, event | category | flops | bytes accessed | tf_op | source)
XLA Modules:
  0.0 66.2 jit_solution(14686339571129436640)
XLA Ops:
  0.6 52.1 %moe_layer.1 = (bf16[128,1024]{1,0:T(8,128)(2,1)}, bf16[128,1024]{1,0:T(8,128)(2,1)}, f32[32,1024]{1,0:T(8,128)}, bf16[256,1024]{1,0:T(8,128)(2,1)}, bf16[256,10...) custom-call(bf16[128,1024]{1,0:T(8,128)(2,1)} %x_hbm.1, ...), custom_call_target="tpu_custom_call" | custom-call | tf_op jit(solution)/shard_map/moe_layer/pallas_call | solution.py:321
  52.8 13.4 %weight_grads.1 = (f32[8,1024,256]{2,1,0:T(8,128)}, f32[8,1024,256]{2,1,0:T(8,128)}, f32[8,256,1024]{2,1,0:T(8,128)}, f32[1024,256]{1,0:T(8,128)}, f32[1024,256]...) custom-call(bf16[256,1024]{1,0:T(8,128)(2,1)} %get-tuple-element.31., ...), custom_call_target="tpu_custom_call" | custom-call | flops 8589934592 | bytes 33554432 | tf_op jit(solution)/shard_map/weight_grads/pallas_call | solution.py:381

commit v3 on v2

v3 whole, which is shorter than its diff:
```python
import functools

import jax
import jax.numpy as jnp
from jax import lax
from jax.experimental import pallas as pl
from jax.experimental.pallas import tpu as pltpu
from jax.sharding import PartitionSpec as P

EPS = 1e-5
F32 = jnp.float32
BF16 = jnp.bfloat16
MESH = pl.DeviceIdType.MESH
ANY = pl.BlockSpec(memory_space=pl.ANY)
VMEM = pl.BlockSpec(memory_space=pltpu.VMEM)
NN = (((1,), (0,)), ((), ()))
NT = (((1,), (1,)), ((), ()))
TN = (((0,), (0,)), ((), ()))

SHARDS = 4
TOK = 128
DIM = 1024
HALF = 512
EXPERTS = 32
OWN = 8
WIDTH = 256
CAP = 20
PAD = 32
SLOTS = OWN * CAP


def mm(a, b, dims=NN):
    return lax.dot_general(a, b, dims, preferred_element_type=F32)


def inv_rms_of(x_wide):
    return lax.rsqrt(jnp.mean(x_wide * x_wide, axis=1, keepdims=True) + EPS)


def glu_grads(d_hidden, act_gate, act_up):
    sig_gate = jax.nn.sigmoid(act_gate)
    d_gate = (d_hidden * act_up * sig_gate * (1.0 + act_gate * (1.0 - sig_gate))).astype(BF16)
    d_up = (d_hidden * act_gate * sig_gate).astype(BF16)
    return d_gate, d_up


def to_row(col):
    return jnp.transpose(jnp.broadcast_to(col, (TOK, TOK)))[:8]


def to_col(row):
    return jnp.transpose(jnp.broadcast_to(row, (TOK, TOK)))[:, :1]


def barrier(peers):
    sem = pltpu.get_barrier_semaphore()
    for peer in peers:
        pl.semaphore_signal(sem, inc=1, device_id=peer, device_id_type=MESH)
    pl.semaphore_wait(sem, len(peers))


def layer_kernel(x_hbm, dy_hbm, prim_hbm, alt_hbm, wr_hbm, wg_hbm, wu_hbm, wd_hbm, sg_hbm, su_hbm, sd_hbm,
                 y_hbm, dn_hbm, gr_hbm, xs_hbm, us_hbm, h_hbm, dab_hbm, n_hbm, dy_all_hbm, sh_hbm, sdab_hbm,
                 x_all, dy_all, ids_all, wr, wg, wu, wd, sg, su, sd, n_all, xs, us, pick_own, acts, acts_up, hid, dab, hid_s, dab_s,
                 probs, meta, s_send, s_recv, s_keep, n_send, n_recv, n_keep, o_send, o_recv, o_keep, d_send, d_recv, d_keep,
                 o_all, d_all, dg_mine, dg_all, y_half, dn_half, gr_buf,
                 in_sem, w_sem, out_sem, send_sem, recv_sem, r_send_sem, r_recv_sem, y_send_sem, y_recv_sem, g_send_sem, g_recv_sem):
    me = lax.axis_index("ep")
    side = lax.axis_index("etp")
    total = SHARDS * TOK
    mate = jnp.bitwise_xor(me, 1)
    across = jnp.bitwise_xor(me, 2)
    to_mate, to_across, to_twin = {"ep": mate}, {"ep": across}, {"etp": 1 - side}
    others = [{"etp": jnp.bitwise_xor(side, k // SHARDS), "ep": jnp.bitwise_xor(me, k % SHARDS)} for k in range(1, 2 * SHARDS)]
    theirs = pl.ds(pl.multiple_of((1 - side) * HALF, HALF), HALF)
    mine = pl.ds(pl.multiple_of(side * HALF, HALF), HALF)
    home = pl.ds(pl.multiple_of(me * TOK, TOK), TOK)

    loads = [pltpu.make_async_copy(src, dst, in_sem.at[k]) for k, (src, dst) in enumerate((
        (x_hbm, x_all.at[me]), (prim_hbm, ids_all.at[me, 0:1]), (alt_hbm, ids_all.at[me, 1:2]), (dy_hbm, dy_all.at[me]),
        (sg_hbm, sg), (su_hbm, su), (sd_hbm, sd), (wr_hbm, wr)))]
    for load in loads:
        load.start()
    w_loads = [[pltpu.make_async_copy(src.at[e], dst.at[e], w_sem.at[k, e]) for k, (src, dst) in enumerate(((wg_hbm, wg), (wu_hbm, wu), (wd_hbm, wd)))] for e in range(OWN)]
    barrier(others)

    def remote(view, lane, k, target):
        return pltpu.make_async_remote_copy(src_ref=view, dst_ref=view, send_sem=send_sem.at[lane, k], recv_sem=recv_sem.at[lane, k], device_id=target, device_id_type=MESH)

    CHUNKS = (((0, 80), (80, 160)), ((0, 80), (80, 112), (112, 160)))
    READY = ((2, 4), (2, 3, 4))
    DIRECT = ((True, False), (False, True, True))
    returns = []

    def give_back(lane, chunk):
        buf, keep, recv, copies = ((o_all, o_keep, o_recv, o_copies), (d_all, d_keep, d_recv, d_copies))[lane]
        for copy in copies[READY[lane][chunk - 1] if chunk else 0 : READY[lane][chunk]]:
            copy.wait_recv()
        rows = slice(*CHUNKS[lane][chunk])
        buf[me, rows] = (keep[rows, :] + recv[rows, :]).astype(BF16)

        def send(owner, k, j):
            view = buf.at[owner, rows]
            return pltpu.make_async_remote_copy(src_ref=view, dst_ref=view, send_sem=r_send_sem.at[lane, chunk, j], recv_sem=r_recv_sem.at[lane, chunk, j], device_id={"ep": jnp.bitwise_xor(me, k)}, device_id_type=MESH)

        group = [send(me, 2, 0), send(me, 1, 1), send(me, 3, 2) if DIRECT[lane][chunk] else send(across, 1, 2)]
        for copy in group if DIRECT[lane][chunk] else group[:2]:
            copy.start()
        returns.append(group)
        return group

    def pass_on(group):
        group[0].wait_recv()
        group[2].start()

    def arrived(group, forwarded):
        for copy in group[1:] if forwarded else group:
            copy.wait_recv()

    def twin(src, dst, k):
        return pltpu.make_async_remote_copy(src_ref=src, dst_ref=dst, send_sem=y_send_sem.at[k], recv_sem=y_recv_sem.at[k], device_id=to_twin, device_id_type=MESH)

    def pieces(shard):
        rows = TOK // 2
        return [ids_all.at[shard], x_all.at[shard, :rows], x_all.at[shard, rows:], dy_all.at[shard, :rows], dy_all.at[shard, rows:]]

    out_across = [remote(view, 0, k, to_across) for k, view in enumerate(pieces(me))]
    out_mate = [remote(view, 1, k, to_mate) for k, view in enumerate(pieces(me))]
    forwards = [remote(view, 2, k, to_mate) for k, view in enumerate(pieces(across))]
    for load in loads[:3]:
        load.wait()
    for k in range(3):
        out_across[k].start()
        out_mate[k].start()
    loads[3].wait()
    for k in range(3, 5):
        out_across[k].start()
        out_mate[k].start()
    for group in w_loads:
        for load in group:
            load.start()

    x_wide = x_all[me].astype(F32)
    normed = (x_wide * inv_rms_of(x_wide)).astype(BF16)
    for load in loads[4:7]:
        load.wait()
    act_gate = mm(normed, sg[...])
    act_up = mm(normed, su[...])
    hidden = (jax.nn.silu(act_gate) * act_up).astype(BF16)
    d_gate, d_up = glu_grads(mm(dy_all[me], sd[...], NT), act_gate, act_up)
    n_send[...] = mm(d_gate, sg[theirs, :], NT) + mm(d_up, su[theirs, :], NT)
    n_copy = twin(n_send, n_recv, 0)
    n_copy.start()
    s_send[...] = mm(hidden, sd[:, theirs])
    s_copies = [twin(s_send.at[k * (TOK // 2) : (k + 1) * (TOK // 2)], s_recv.at[k * (TOK // 2) : (k + 1) * (TOK // 2)], 12 + k) for k in range(2)]
    s_copies[0].start()
    n_keep[...] = mm(d_gate, sg[mine, :], NT) + mm(d_up, su[mine, :], NT)
    s_keep[...] = mm(hidden, sd[:, mine])

    def norm(shard):
        rows = x_all[shard].astype(F32)
        n_all[pl.ds(pl.multiple_of(shard * TOK, TOK), TOK), :] = (rows * inv_rms_of(rows)).astype(BF16)

    n_all[home, :] = normed
    out_across[0].wait_recv()
    forwards[0].start()
    for copy in (out_mate[0], forwards[0]):
        copy.wait_recv()
    prim = jnp.concatenate([ids_all[s, 0:1, :] for s in range(SHARDS)], axis=1)
    alt = jnp.concatenate([ids_all[s, 1:2, :] for s in range(SHARDS)], axis=1)
    expert = lax.broadcasted_iota(jnp.int32, (EXPERTS, total), 0)
    before = (lax.broadcasted_iota(jnp.int32, (total, total), 0) < lax.broadcasted_iota(jnp.int32, (total, total), 1)).astype(F32).astype(BF16)
    one_prim = (expert == prim).astype(F32)
    rank_prim = jnp.sum(one_prim * mm(one_prim.astype(BF16), before), axis=0, keepdims=True)
    keep_prim = rank_prim < CAP
    kept = jnp.minimum(jnp.sum(one_prim, axis=1, keepdims=True), float(CAP))
    one_alt = jnp.where(keep_prim, 0.0, (expert == alt).astype(F32))
    slot_alt = jnp.sum(one_alt * (mm(one_alt.astype(BF16), before) + kept), axis=0, keepdims=True)
    keep_alt = jnp.logical_and(jnp.logical_not(keep_prim), slot_alt < CAP)
    assign = jnp.where(keep_prim, prim, jnp.where(keep_alt, alt, -1))
    slot = jnp.where(keep_prim, rank_prim, slot_alt).astype(jnp.int32)
    meta[0:1] = assign.astype(F32)
    meta[1:2] = jnp.where(assign >= 0, assign * CAP + slot, -1).astype(F32)
    local = assign - me * OWN
    owned = jnp.logical_and(local >= 0, local < OWN)
    target = jnp.where(owned, local * PAD + slot, -1)
    pick_own[...] = (lax.broadcasted_iota(jnp.int32, (OWN * PAD, total), 0) == target).astype(F32).astype(BF16)

    for k in range(1, 3):
        out_mate[k].wait_recv()
    norm(mate)
    for k in range(1, 3):
        out_across[k].wait_recv()
        forwards[k].start()
    norm(across)
    for k in range(1, 3):
        forwards[k].wait_recv()
    norm(jnp.bitwise_xor(me, 3))
    xs[...] = mm(pick_own[...], n_all[...]).astype(BF16)

    o_copies, d_copies = [], []
    for e in range(OWN):
        for load in w_loads[e]:
            load.wait()
        rows = slice(e * PAD, (e + 1) * PAD)
        act_gate = mm(xs[rows, :], wg[e])
        act_up = mm(xs[rows, :], wu[e])
        hidden = (jax.nn.silu(act_gate) * act_up).astype(BF16)
        acts[rows, :] = act_gate
        acts_up[rows, :] = act_up
        hid[rows, :] = hidden
        part = slice(e * CAP, (e + 1) * CAP)
        o_send[part, :] = mm(hidden, wd[e, :, theirs])[:CAP]
        o_keep[part, :] = mm(hidden, wd[e, :, mine])[:CAP]
        if e % 2:
            chunk = slice((e - 1) * CAP, (e + 1) * CAP)
            o_copies.append(twin(o_send.at[chunk], o_recv.at[chunk], 2 + e // 2))
            o_copies[-1].start()
        if e in (1, 4):
            k = 3 if e == 1 else 4
            out_across[k].wait_recv()
            forwards[k].start()
    loads[7].wait()
    logits = mm(n_all[...], wr[...], NT)
    top = jnp.max(logits, axis=1, keepdims=True)
    expo = jnp.exp(logits - top)
    share = expo / jnp.sum(expo, axis=1, keepdims=True)
    wide = jnp.concatenate([share, jnp.zeros((total, TOK - EXPERTS), F32)], axis=1)
    probs_t = jnp.concatenate([jnp.transpose(wide[s * TOK : (s + 1) * TOK])[:EXPERTS] for s in range(SHARDS)], axis=1)
    probs[...] = probs_t
    one_assign = lax.broadcasted_iota(jnp.int32, (EXPERTS, total), 0) == meta[0:1, :].astype(jnp.int32)
    gate = jnp.sum(jnp.where(one_assign, probs_t, 0.0), axis=0, keepdims=True)
    meta[2:3] = gate
    gate_slot = jnp.sum(pick_own[...].astype(F32) * gate, axis=1, keepdims=True)
    for k in range(3, 5):
        out_mate[k].wait_recv()
        forwards[k].wait_recv()
    us[...] = (gate_slot * mm(pick_own[...], dy_all[...].reshape(total, DIM))).astype(BF16)

    for e in range(OWN):
        rows = slice(e * PAD, (e + 1) * PAD)
        d_gate, d_up = glu_grads(mm(us[rows, :], wd[e], NT), acts[rows, :], acts_up[rows, :])
        dab[rows, :WIDTH] = d_gate
        dab[rows, WIDTH:] = d_up
        part = slice(e * CAP, (e + 1) * CAP)
        d_send[part, :] = (mm(d_gate, wg[e, theirs, :], NT) + mm(d_up, wu[e, theirs, :], NT))[:CAP]
        d_keep[part, :] = (mm(d_gate, wg[e, mine, :], NT) + mm(d_up, wu[e, mine, :], NT))[:CAP]
        if e % 2:
            chunk = slice((e - 1) * CAP, (e + 1) * CAP)
            d_copies.append(twin(d_send.at[chunk], d_recv.at[chunk], 6 + e // 2))
            d_copies[-1].start()
        if e == 3:
            o_first = give_back(0, 0)

    s_copies[1].start()
    o_second = give_back(0, 1)

    saves = [pltpu.make_async_copy(src, dst, out_sem.at[k]) for k, (src, dst) in enumerate((
        (xs, xs_hbm), (us, us_hbm), (hid, h_hbm), (dab, dab_hbm), (n_all, n_hbm), (dy_all, dy_all_hbm), (hid_s, sh_hbm), (dab_s, sdab_hbm), (y_half, y_hbm), (gr_buf, gr_hbm), (dn_half, dn_hbm)))]
    save_y, save_gr, save_dn = saves[8:]
    saves = saves[:8]
    for save in saves[:6]:
        save.start()
    act_gate = mm(n_all[...], sg[...])
    act_up = mm(n_all[...], su[...])
    hid_s[...] = (jax.nn.silu(act_gate) * act_up).astype(BF16)
    d_gate, d_up = glu_grads(mm(dy_all[...].reshape(total, DIM), sd[...], NT), act_gate, act_up)
    dab_s[:, :WIDTH] = d_gate
    dab_s[:, WIDTH:] = d_up
    for save in saves[6:]:
        save.start()

    x_half = x_all[me, :, mine].astype(F32)
    dy_half = dy_all[me, :, mine].astype(F32)
    gate_home = to_col(meta[2:3, home])
    flat_home = to_col(meta[1:2, home]).astype(jnp.int32)
    pick = (lax.broadcasted_iota(jnp.int32, (TOK, SHARDS * SLOTS), 1) == flat_home).astype(F32).astype(BF16)
    d_first = give_back(1, 0)
    pass_on(o_second)
    arrived(o_first, False)
    d_second = give_back(1, 1)
    arrived(o_second, True)
    tok_out = mm(pick, o_all[...].reshape(SHARDS * SLOTS, HALF))
    dg_mine[...] = to_row(jnp.sum(dy_half * tok_out, axis=1, keepdims=True))
    place = side * SHARDS + me
    dg_copies = [pltpu.make_async_remote_copy(src_ref=dg_mine, dst_ref=dg_all.at[place], send_sem=g_send_sem.at[k], recv_sem=g_recv_sem.at[k], device_id=other, device_id_type=MESH) for k, other in enumerate(others)]
    for copy in dg_copies:
        copy.start()
    dg_all[place] = dg_mine[...]
    d_third = give_back(1, 2)
    pass_on(d_first)
    for copy in s_copies:
        copy.wait_recv()
    y_half[...] = (x_half + (s_keep[...] + s_recv[...]) + gate_home * tok_out).astype(BF16)
    save_y.start()
    for copy in dg_copies:
        copy.wait_recv()
    dg = jnp.concatenate([dg_all[s, 0:1, :] + dg_all[SHARDS + s, 0:1, :] for s in range(SHARDS)], axis=1)
    one_assign = (lax.broadcasted_iota(jnp.int32, (EXPERTS, total), 0) == meta[0:1, :].astype(jnp.int32)).astype(F32)
    d_logits = (dg * meta[2:3, :] * (one_assign - probs[...])).astype(BF16)
    home_one = (lax.broadcasted_iota(jnp.int32, (EXPERTS, TOK), 0) == meta[0:1, home].astype(jnp.int32)).astype(F32)
    dg_home = dg_all[me, 0:1, :] + dg_all[SHARDS + me, 0:1, :]
    d_logits_home = (dg_home * meta[2:3, home] * (home_one - probs[:, home])).astype(BF16)
    n_copy.wait_recv()
    d_normed = n_keep[...] + n_recv[...] + mm(d_logits_home, wr[:, mine], TN)
    gr_buf[...] = mm(d_logits, n_all[...])
    save_gr.start()
    arrived(d_second, False)
    arrived(d_first, True)
    arrived(d_third, False)
    dn_half[...] = d_normed + mm(pick, d_all[...].reshape(SHARDS * SLOTS, HALF))
    save_dn.start()
    for copy in out_across + out_mate + forwards + [n_copy] + s_copies + o_copies + d_copies + sum(returns, []) + dg_copies:
        copy.wait_send()
    for save in saves + [save_y, save_gr, save_dn]:
        save.wait()


def layer_call(x_in, y_grad, prim, alt, wr_t, exp_gate, exp_up, exp_down, sh_gate, sh_up, sh_down):
    width = sh_gate.shape[1]
    total = SHARDS * TOK
    rows = OWN * PAD
    shape = jax.ShapeDtypeStruct
    dma = pltpu.SemaphoreType.DMA
    half_f32 = pltpu.VMEM((TOK, HALF), F32)
    slots_f32 = pltpu.VMEM((SLOTS, HALF), F32)
    return pl.pallas_call(
        layer_kernel,
        out_shape=(
            shape((TOK, HALF), BF16), shape((TOK, HALF), F32), shape((EXPERTS, DIM), F32),
            shape((rows, DIM), BF16), shape((rows, DIM), BF16), shape((rows, width), BF16), shape((rows, 2 * width), BF16),
            shape((total, DIM), BF16), shape((SHARDS, TOK, DIM), BF16), shape((total, width), BF16), shape((total, 2 * width), BF16),
        ),
        in_specs=[ANY] * 11,
        out_specs=(ANY,) * 11,
        scratch_shapes=[
            pltpu.VMEM((SHARDS, TOK, DIM), BF16), pltpu.VMEM((SHARDS, TOK, DIM), BF16), pltpu.VMEM((SHARDS, 8, TOK), jnp.int32), pltpu.VMEM((EXPERTS, DIM), BF16),
            pltpu.VMEM((OWN, DIM, width), BF16), pltpu.VMEM((OWN, DIM, width), BF16), pltpu.VMEM((OWN, width, DIM), BF16),
            pltpu.VMEM((DIM, width), BF16), pltpu.VMEM((DIM, width), BF16), pltpu.VMEM((width, DIM), BF16),
            pltpu.VMEM((total, DIM), BF16), pltpu.VMEM((rows, DIM), BF16), pltpu.VMEM((rows, DIM), BF16), pltpu.VMEM((rows, total), BF16),
            pltpu.VMEM((rows, width), F32), pltpu.VMEM((rows, width), F32), pltpu.VMEM((rows, width), BF16), pltpu.VMEM((rows, 2 * width), BF16),
            pltpu.VMEM((total, width), BF16), pltpu.VMEM((total, 2 * width), BF16),
            pltpu.VMEM((EXPERTS, total), F32), pltpu.VMEM((8, total), F32),
            half_f32, half_f32, half_f32, half_f32, half_f32, half_f32,
            slots_f32, slots_f32, slots_f32, slots_f32, slots_f32, slots_f32,
            pltpu.VMEM((SHARDS, SLOTS, HALF), BF16), pltpu.VMEM((SHARDS, SLOTS, HALF), BF16),
            pltpu.VMEM((8, TOK), F32), pltpu.VMEM((2 * SHARDS, 8, TOK), F32), pltpu.VMEM((TOK, HALF), BF16), half_f32, pltpu.VMEM((EXPERTS, DIM), F32),
            dma((8,)), dma((3, OWN)), dma((11,)), dma((3, 5)), dma((3, 5)), dma((2, 3, 3)), dma((2, 3, 3)), dma((14,)), dma((14,)), dma((7,)), dma((7,)),
        ],
        compiler_params=pltpu.CompilerParams(collective_id=0, has_side_effects=True, vmem_limit_bytes=60 << 20),
        name="moe_layer",
    )(x_in, y_grad, prim, alt, wr_t, exp_gate, exp_up, exp_down, sh_gate, sh_up, sh_down)


def grads_kernel(xs_hbm, us_hbm, h_hbm, dab_hbm, n_hbm, dy_hbm, sh_hbm, sdab_hbm, gr_hbm, g_gate_hbm, g_up_hbm, g_down_hbm, gs_gate_hbm, gs_up_hbm, gs_down_hbm, g_router_hbm,
                 xs, us, hid, dab, n_all, dy_all, hid_s, dab_s, g_router, g_gate, g_up, g_down, gs_gate, gs_up, gs_down, in_sem, out_sem, sh_sem):
    loads = [pltpu.make_async_copy(src, dst, in_sem.at[k]) for k, (src, dst) in enumerate((
        (h_hbm, hid), (us_hbm, us), (xs_hbm, xs), (dab_hbm, dab), (n_hbm, n_all), (sdab_hbm, dab_s), (sh_hbm, hid_s), (dy_hbm, dy_all), (gr_hbm, g_router)))]
    for load in loads:
        load.start()
    writes = []

    def write(src, dst, sem):
        writes.append(pltpu.make_async_copy(src, dst, sem))
        writes[-1].start()

    for load in loads[:2]:
        load.wait()
    for e in range(OWN):
        rows = slice(e * PAD, (e + 1) * PAD)
        g_down[e] = mm(hid[rows, :], us[rows, :], TN)
        write(g_down.at[e], g_down_hbm.at[e], out_sem.at[0, e])
        if e == 0:
            for load in loads[2:4]:
                load.wait()
        both = mm(xs[rows, :], dab[rows, :], TN)
        g_gate[e] = both[:, :WIDTH]
        g_up[e] = both[:, WIDTH:]
        write(g_gate.at[e], g_gate_hbm.at[e], out_sem.at[1, e])
        write(g_up.at[e], g_up_hbm.at[e], out_sem.at[2, e])
    for load in loads[4:]:
        load.wait()
    both = mm(n_all[...], dab_s[...], TN)
    gs_gate[...] = both[:, :WIDTH]
    gs_up[...] = both[:, WIDTH:]
    write(gs_gate, gs_gate_hbm, sh_sem.at[0])
    write(gs_up, gs_up_hbm, sh_sem.at[1])
    gs_down[...] = mm(hid_s[...], dy_all[...], TN)
    write(gs_down, gs_down_hbm, sh_sem.at[2])
    write(g_router, g_router_hbm, sh_sem.at[3])
    for copy in writes:
        copy.wait()


def grads_call(*saved):
    shape = jax.ShapeDtypeStruct
    outs = ((OWN, DIM, WIDTH), (OWN, DIM, WIDTH), (OWN, WIDTH, DIM), (DIM, WIDTH), (DIM, WIDTH), (WIDTH, DIM), (EXPERTS, DIM))
    return pl.pallas_call(
        grads_kernel,
        out_shape=tuple(shape(dims, F32) for dims in outs),
        in_specs=[ANY] * 9,
        out_specs=(ANY,) * 7,
        scratch_shapes=[pltpu.VMEM(a.shape, a.dtype) for a in saved] + [pltpu.VMEM(dims, F32) for dims in outs[:-1]] + [pltpu.SemaphoreType.DMA((9,)), pltpu.SemaphoreType.DMA((3, OWN)), pltpu.SemaphoreType.DMA((4,))],
        compiler_params=pltpu.CompilerParams(vmem_limit_bytes=63 << 20),
        cost_estimate=pl.CostEstimate(flops=8 << 30, bytes_accessed=32 << 20, transcendentals=0),
        name="weight_grads",
    )(*saved)


def finish_kernel(x_ref, dy_ref, y_mine, y_recv, dn_mine, dn_recv, y_out, dx_out):
    side = lax.axis_index("etp")
    theirs = pl.ds(pl.multiple_of((1 - side) * HALF, HALF), HALF)
    mine = pl.ds(pl.multiple_of(side * HALF, HALF), HALF)
    y_out[:, mine] = y_mine[...]
    y_out[:, theirs] = y_recv[...]
    x_wide = x_ref[...].astype(F32)
    inv_rms = inv_rms_of(x_wide)
    halves = ((mine, dn_mine), (theirs, dn_recv))
    norm_proj = sum(jnp.sum(dn[...] * x_ref[:, cols].astype(F32), axis=1, keepdims=True) for cols, dn in halves) / DIM
    for cols, dn in halves:
        dx_out[:, cols] = (dy_ref[:, cols].astype(F32) + inv_rms * dn[...] - x_ref[:, cols].astype(F32) * inv_rms**3 * norm_proj).astype(BF16)


def finish_call(*args):
    shape = jax.ShapeDtypeStruct
    return pl.pallas_call(
        finish_kernel,
        out_shape=(shape((TOK, DIM), BF16), shape((TOK, DIM), BF16)),
        in_specs=[VMEM] * 6,
        out_specs=(VMEM,) * 2,
        compiler_params=pltpu.CompilerParams(vmem_limit_bytes=8 << 20),
        name="finish_tokens",
    )(*args)


def solution(mesh):
    tok_spec = P(("dp", "ep"), None)
    id_spec = P(("dp", "ep"))
    in_specs = (tok_spec, tok_spec, id_spec, id_spec, P(None, None), P("ep", None, "etp"), P("ep", None, "etp"), P("ep", "etp", None), P(None, "etp"), P(None, "etp"), P("etp", None))
    out_specs = (tok_spec, tok_spec, P(("dp", "ep"), None, "etp"), P(("dp", "ep"), None, "etp"), P(("dp", "ep"), "etp", None), P("dp", "etp"), P("dp", "etp"), P(("dp", "etp"), None), P("dp", None))

    def local_step(x_in, y_grad, prim_exp, alt_exp, w_router, exp_gate, exp_up, exp_down, sh_gate, sh_up, sh_down):
        y_half, dn_half, gr, xs, us, hid, dab, n_all, dy_all, hid_s, dab_s = layer_call(x_in, y_grad, prim_exp.reshape(1, TOK), alt_exp.reshape(1, TOK), w_router.T, exp_gate, exp_up, exp_down, sh_gate, sh_up, sh_down)
        swap = [(0, 1), (1, 0)]
        dn_other = lax.ppermute(dn_half, "etp", swap)
        y_other = lax.ppermute(y_half, "etp", swap)
        g_gate, g_up, g_down, gs_gate, gs_up, gs_down, g_router = grads_call(xs, us, hid, dab, n_all, dy_all.reshape(SHARDS * TOK, DIM), hid_s, dab_s, gr)
        y_out, x_grad = finish_call(x_in, y_grad, y_half, y_other, dn_half, dn_other)
        return (y_out, x_grad, g_gate, g_up, g_down, gs_gate, gs_up, gs_down, g_router.T)

    return jax.shard_map(local_step, mesh=mesh, in_specs=in_specs, out_specs=out_specs, check_vma=False)
```

time: 66.5 us -> 54.4 us (0.82)
  Pallas kernels: 65.6 us -> 51.5 us
  starting transfers between devices: 0 us -> 2.05 us
    pallas_call x2 -> x3, Pallas kernels: 65.6 us -> 51.5 us  [the longest x1 38.3 us: layer_call(): pl.pallas_call(layer_kernel, out_shape=(shape((TOK, HALF), BF16), shape((...]
    ppermute x0 -> x2, starting transfers between devices: none -> 2.05 us  [the longest x1 1.84 us: local_step(): y_other = lax.ppermute(y_half, 'etp', swap)]
  transfers between devices with their start and end apart: 0 -> 2, of which waited for: 0 -> 0; matrix products, arithmetic and copies ran while one was open for 0% -> 0% of each run, Pallas kernels for 0% -> 21%
where the time goes in v3:
time: 54.4 us; the launch traced here: 54.3 us
  Pallas kernels  51.5 us (95%)
  starting transfers between devices  2.05 us (4%)
  between operations  0.71 us (1%)
    pallas_call x1, Pallas kernels, layer_call(): pl.pallas_call(layer_kernel, out_shape=(shape((TOK, HALF), BF16), shape((...  38.3 us
    pallas_call x1, Pallas kernels, grads_call(): pl.pallas_call(grads_kernel, out_shape=tuple((shape(dims, F32) for dims i...  11.2 us
    pallas_call x1, Pallas kernels, finish_call(): pl.pallas_call(finish_kernel, out_shape=(shape((TOK, DIM), BF16), shape((...  2.01 us
    ppermute x1, starting transfers between devices, local_step(): y_other = lax.ppermute(y_half, 'etp', swap)  1.84 us
  transfers between devices with their start and end apart: 2, of which 0 were waited for; matrix products, arithmetic and copies ran while one was open for 0% of the time, Pallas kernels for 21%

profile of v3, /device:TPU:0, one launch (start us, length us, event | category | flops | bytes accessed | tf_op | source)
XLA Modules:
  0.0 54.3 jit_solution(7135730909418302003)
XLA Ops:
  0.6 38.3 %moe_layer.1 = (bf16[128,512]{1,0:T(8,128)(2,1)}, f32[128,512]{1,0:T(8,128)}, f32[32,1024]{1,0:T(8,128)}, bf16[256,1024]{1,0:T(8,128)(2,1)}, bf16[256,1024]{1,0:...) custom-call(bf16[128,1024]{1,0:T(8,128)(2,1)} %x_ref.1, ...), custom_call_target="tpu_custom_call" | custom-call | tf_op jit(solution)/shard_map/moe_layer/pallas_call | solution.py:327
  38.9 0.2 collective-permute-start.1
  39.1 1.8 %collective-permute-start = (bf16[128,512]{1,0:T(8,128)(2,1)}, bf16[128,512]{1,0:T(8,128)(2,1)}, u32[]{:S(2)}, u32[]{:S(2)}) collective-permute-start(bf16[128,512]{1,0:T(8,128)(2,1)} %get-tuple-element.29.y_mine), channel_id=1, source_target_pairs={{0,4},{4,0},{1,5},{5,1},{2,6},{6,2},{3,7},{7,3}} | collective-permute-start | bytes 393224 | tf_op jit(solution)/shard_map/ppermute | solution.py:446
  41.0 0.0 copy-start
  41.0 0.0 copy-start.1
  41.0 0.0 copy-start.2
  41.0 0.0 copy-start.3
  41.0 11.2 %weight_grads.1 = (f32[8,1024,256]{2,1,0:T(8,128)}, f32[8,1024,256]{2,1,0:T(8,128)}, f32[8,256,1024]{2,1,0:T(8,128)}, f32[1024,256]{1,0:T(8,128)}, f32[1024,256]...) custom-call(bf16[256,1024]{1,0:T(8,128)(2,1)} %get-tuple-element.33.xs_hbm, ...), custom_call_target="tpu_custom_call" | custom-call | flops 8589934592 | bytes 33554432 | tf_op jit(solution)/shard_map/weight_grads/pallas_call | solution.py:398
  52.2 0.0 collective-permute-done.y_recv
  52.2 0.0 collective-permute-done.1.dn_recv
  52.2 0.0 copy-done
  52.2 0.0 copy-done.1
  52.3 0.0 copy-done.2
  52.3 0.0 copy-done.3
  52.3 2.0 %finish_tokens.1 = (bf16[128,1024]{1,0:T(8,128)(2,1)}, bf16[128,1024]{1,0:T(8,128)(2,1)}) custom-call(bf16[128,1024]{1,0:T(8,128)(2,1)S(1)} %copy-done, bf16[128,1024]{1,0:T(8,128)(2,1)S(1)} %copy-done.1, bf16[128,512]{1,0:T(8,128)(2,1)S(1)} %copy-done.3, bf16[128,512]{1,0:T(8,128)(2,1)} %collective-permute-done.y_recv, f32[128,512]{1,0:T(8,128)S(1)} %copy-done.2, ...), custom_call_target="tpu_custom_call" | custom-call | tf_op jit(solution)/shard_map/finish_tokens/pallas_call | solution.py:426
Async XLA Ops:
  38.9 13.3 %collective-permute-start.1 = (f32[128,512]{1,0:T(8,128)}, f32[128,512]{1,0:T(8,128)}, u32[]{:S(2)}, u32[]{:S(2)}) collective-permute-start(f32[128,512]{1,0:T(8,128)} %get-tuple-element.30.dn_mine), channel_id=1, source_target_pairs={{0,4},{4,0},{1,5},{5,1},{2,6},{6,2},{3,7},{7,3}} | collective-permute-start | bytes 786440 | tf_op jit(solution)/shard_map/ppermute | solution.py:445
  39.1 13.1 %collective-permute-start = (bf16[128,512]{1,0:T(8,128)(2,1)}, bf16[128,512]{1,0:T(8,128)(2,1)}, u32[]{:S(2)}, u32[]{:S(2)}) collective-permute-start(bf16[128,512]{1,0:T(8,128)(2,1)} %get-tuple-element.29.y_mine), channel_id=1, source_target_pairs={{0,4},{4,0},{1,5},{5,1},{2,6},{6,2},{3,7},{7,3}} | collective-permute-start | bytes 393224 | tf_op jit(solution)/shard_map/ppermute | solution.py:446
  41.0 11.3 %copy-start = (bf16[128,1024]{1,0:T(8,128)(2,1)S(1)}, bf16[128,1024]{1,0:T(8,128)(2,1)}, u32[]{:S(2)}) copy-start(bf16[128,1024]{1,0:T(8,128)(2,1)} %x_ref.1) | copy-start | bytes 786436
  41.0 11.3 %copy-start.1 = (bf16[128,1024]{1,0:T(8,128)(2,1)S(1)}, bf16[128,1024]{1,0:T(8,128)(2,1)}, u32[]{:S(2)}) copy-start(bf16[128,1024]{1,0:T(8,128)(2,1)} %dy_ref.1) | copy-start | bytes 786436
  41.0 11.3 %copy-start.2 = (f32[128,512]{1,0:T(8,128)S(1)}, f32[128,512]{1,0:T(8,128)}, u32[]{:S(2)}) copy-start(f32[128,512]{1,0:T(8,128)} %get-tuple-element.30.dn_mine) | copy-start | bytes 786436
  41.0 11.3 %copy-start.3 = (bf16[128,512]{1,0:T(8,128)(2,1)S(1)}, bf16[128,512]{1,0:T(8,128)(2,1)}, u32[]{:S(2)}) copy-start(bf16[128,512]{1,0:T(8,128)(2,1)} %get-tuple-element.29.y_mine) | copy-start | bytes 393220

commit v4 on v3

--- a/solution.py
+++ b/solution.py
@@ -62,9 +62,9 @@
 def layer_kernel(x_hbm, dy_hbm, prim_hbm, alt_hbm, wr_hbm, wg_hbm, wu_hbm, wd_hbm, sg_hbm, su_hbm, sd_hbm,
                  y_hbm, dn_hbm, gr_hbm, xs_hbm, us_hbm, h_hbm, dab_hbm, n_hbm, dy_all_hbm, sh_hbm, sdab_hbm,
                  x_all, dy_all, ids_all, wr, wg, wu, wd, sg, su, sd, n_all, xs, us, pick_own, acts, acts_up, hid, dab, hid_s, dab_s,
-                 probs, meta, s_send, s_recv, s_keep, n_send, n_recv, n_keep, o_send, o_recv, o_keep, d_send, d_recv, d_keep,
+                 probs, meta, hid_own, hid_twin, sd_twin, s_keep, n_send, n_recv, n_keep, o_send, o_recv, o_keep, d_send, d_recv, d_keep,
                  o_all, d_all, dg_mine, dg_all, y_half, dn_half, gr_buf,
-                 in_sem, w_sem, out_sem, send_sem, recv_sem, r_send_sem, r_recv_sem, y_send_sem, y_recv_sem, g_send_sem, g_recv_sem):
+                 in_sem, w_sem, out_sem, send_sem, recv_sem, r_send_sem, r_recv_sem, y_send_sem, y_recv_sem, g_send_sem, g_recv_sem, q_send_sem, q_recv_sem):
     me = lax.axis_index("ep")
     side = lax.axis_index("etp")
     total = SHARDS * TOK
@@ -81,44 +81,14 @@
         (sg_hbm, sg), (su_hbm, su), (sd_hbm, sd), (wr_hbm, wr)))]
     for load in loads:
         load.start()
-    w_loads = [[pltpu.make_async_copy(src.at[e], dst.at[e], w_sem.at[k, e]) for k, (src, dst) in enumerate(((wg_hbm, wg), (wu_hbm, wu), (wd_hbm, wd)))] for e in range(OWN)]
+    w_loads = [pltpu.make_async_copy(src, dst, w_sem.at[k]) for k, (src, dst) in enumerate(((wg_hbm, wg), (wu_hbm, wu), (wd_hbm, wd)))]
     barrier(others)
 
     def remote(view, lane, k, target):
-        return pltpu.make_async_remote_copy(src_ref=view, dst_ref=view, send_sem=send_sem.at[lane, k], recv_sem=recv_sem.at[lane, k], device_id=target, device_id_type=MESH)
-
-    CHUNKS = (((0, 80), (80, 160)), ((0, 80), (80, 112), (112, 160)))
-    READY = ((2, 4), (2, 3, 4))
-    DIRECT = ((True, False), (False, True, True))
-    returns = []
-
-    def give_back(lane, chunk):
-        buf, keep, recv, copies = ((o_all, o_keep, o_recv, o_copies), (d_all, d_keep, d_recv, d_copies))[lane]
-        for copy in copies[READY[lane][chunk - 1] if chunk else 0 : READY[lane][chunk]]:
-            copy.wait_recv()
-        rows = slice(*CHUNKS[lane][chunk])
-        buf[me, rows] = (keep[rows, :] + recv[rows, :]).astype(BF16)
-
-        def send(owner, k, j):
-            view = buf.at[owner, rows]
-            return pltpu.make_async_remote_copy(src_ref=view, dst_ref=view, send_sem=r_send_sem.at[lane, chunk, j], recv_sem=r_recv_sem.at[lane, chunk, j], device_id={"ep": jnp.bitwise_xor(me, k)}, device_id_type=MESH)
-
-        group = [send(me, 2, 0), send(me, 1, 1), send(me, 3, 2) if DIRECT[lane][chunk] else send(across, 1, 2)]
-        for copy in group if DIRECT[lane][chunk] else group[:2]:
-            copy.start()
-        returns.append(group)
-        return group
-
-    def pass_on(group):
-        group[0].wait_recv()
-        group[2].start()
-
-    def arrived(group, forwarded):
-        for copy in group[1:] if forwarded else group:
-            copy.wait_recv()
-
-    def twin(src, dst, k):
-        return pltpu.make_async_remote_copy(src_ref=src, dst_ref=dst, send_sem=y_send_sem.at[k], recv_sem=y_recv_sem.at[k], device_id=to_twin, device_id_type=MESH)
+        return pltpu.make_async_remote_copy(src_ref=view, dst_ref=view, send_sem=send_sem.at[(k + 1) // 2], recv_sem=recv_sem.at[lane, k], device_id=target, device_id_type=MESH)
+
+    def twin(src, dst, k, group):
+        return pltpu.make_async_remote_copy(src_ref=src, dst_ref=dst, send_sem=y_send_sem.at[group], recv_sem=y_recv_sem.at[k], device_id=to_twin, device_id_type=MESH)
 
     def pieces(shard):
         rows = TOK // 2
@@ -127,6 +97,11 @@
     out_across = [remote(view, 0, k, to_across) for k, view in enumerate(pieces(me))]
     out_mate = [remote(view, 1, k, to_mate) for k, view in enumerate(pieces(me))]
     forwards = [remote(view, 2, k, to_mate) for k, view in enumerate(pieces(across))]
+    def quarter(shard):
+        return pl.ds(pl.multiple_of(shard * (WIDTH // SHARDS), WIDTH // SHARDS), WIDTH // SHARDS)
+
+    sd_copy = twin(sd_hbm.at[quarter(me), theirs], sd_twin.at[quarter(me)], 2, 2)
+    sd_copy.start()
     for load in loads[:3]:
         load.wait()
     for k in range(3):
@@ -136,9 +111,8 @@
     for k in range(3, 5):
         out_across[k].start()
         out_mate[k].start()
-    for group in w_loads:
-        for load in group:
-            load.start()
+    for load in w_loads:
+        load.start()
 
     x_wide = x_all[me].astype(F32)
     normed = (x_wide * inv_rms_of(x_wide)).astype(BF16)
@@ -149,11 +123,11 @@
     hidden = (jax.nn.silu(act_gate) * act_up).astype(BF16)
     d_gate, d_up = glu_grads(mm(dy_all[me], sd[...], NT), act_gate, act_up)
     n_send[...] = mm(d_gate, sg[theirs, :], NT) + mm(d_up, su[theirs, :], NT)
-    n_copy = twin(n_send, n_recv, 0)
+    n_copy = twin(n_send, n_recv, 0, 0)
     n_copy.start()
-    s_send[...] = mm(hidden, sd[:, theirs])
-    s_copies = [twin(s_send.at[k * (TOK // 2) : (k + 1) * (TOK // 2)], s_recv.at[k * (TOK // 2) : (k + 1) * (TOK // 2)], 12 + k) for k in range(2)]
-    s_copies[0].start()
+    hid_own[...] = hidden
+    h_copy = twin(hid_own, hid_twin, 1, 1)
+    h_copy.start()
     n_keep[...] = mm(d_gate, sg[mine, :], NT) + mm(d_up, su[mine, :], NT)
     s_keep[...] = mm(hidden, sd[:, mine])
 
@@ -186,6 +160,11 @@
     target = jnp.where(owned, local * PAD + slot, -1)
     pick_own[...] = (lax.broadcasted_iota(jnp.int32, (OWN * PAD, total), 0) == target).astype(F32).astype(BF16)
 
+    sd_copy.wait_recv()
+    view = sd_twin.at[quarter(me)]
+    sd_spread = [pltpu.make_async_remote_copy(src_ref=view, dst_ref=view, send_sem=q_send_sem.at[0], recv_sem=q_recv_sem.at[k - 1], device_id={"ep": jnp.bitwise_xor(me, k)}, device_id_type=MESH) for k in range(1, SHARDS)]
+    for copy in sd_spread:
+        copy.start()
     for k in range(1, 3):
         out_mate[k].wait_recv()
     norm(mate)
@@ -200,8 +179,9 @@
 
     o_copies, d_copies = [], []
     for e in range(OWN):
-        for load in w_loads[e]:
-            load.wait()
+        if e == 0:
+            for load in w_loads:
+                load.wait()
         rows = slice(e * PAD, (e + 1) * PAD)
         act_gate = mm(xs[rows, :], wg[e])
         act_up = mm(xs[rows, :], wu[e])
@@ -214,12 +194,45 @@
         o_keep[part, :] = mm(hidden, wd[e, :, mine])[:CAP]
         if e % 2:
             chunk = slice((e - 1) * CAP, (e + 1) * CAP)
-            o_copies.append(twin(o_send.at[chunk], o_recv.at[chunk], 2 + e // 2))
+            o_copies.append(twin(o_send.at[chunk], o_recv.at[chunk], 3 + e // 2, 3))
             o_copies[-1].start()
-        if e in (1, 4):
-            k = 3 if e == 1 else 4
-            out_across[k].wait_recv()
-            forwards[k].start()
+        if e == 5:
+            out_across[3].wait_recv()
+            forwards[3].start()
+    D_PIECES = {1: (0, 40), 3: (40, 80), 5: (80, 120), 6: (120, 136), 7: (136, 160)}
+    CHUNKS = (((0, 80), (80, 160)), ((0, 80), (80, 128), (128, 160)))
+    READY = ((2, 4), (2, 4, 5))
+    DIRECT = ((True, False), (False, False, True))
+
+    def give_back(lane, chunk):
+        buf, keep, recv, copies = ((o_all, o_keep, o_recv, o_copies), (d_all, d_keep, d_recv, d_copies))[lane]
+        for copy in copies[READY[lane][chunk - 1] if chunk else 0 : READY[lane][chunk]]:
+            copy.wait_recv()
+        rows = slice(*CHUNKS[lane][chunk])
+        buf[me, rows] = (keep[rows, :] + recv[rows, :]).astype(BF16)
+
+        def send(owner, k, j):
+            view = buf.at[owner, rows]
+            return pltpu.make_async_remote_copy(src_ref=view, dst_ref=view, send_sem=r_send_sem.at[lane], recv_sem=r_recv_sem.at[lane, chunk, j], device_id={"ep": jnp.bitwise_xor(me, k)}, device_id_type=MESH)
+
+        group = [send(me, 2, 0), send(me, 1, 1), send(me, 3, 2) if DIRECT[lane][chunk] else send(across, 1, 2)]
+        for copy in group if DIRECT[lane][chunk] else group[:2]:
+            copy.start()
+        return group
+
+    def pass_on(group):
+        group[0].wait_recv()
+        group[2].start()
+
+    def arrived(group, forwarded):
+        for copy in group[1:] if forwarded else group:
+            copy.wait_recv()
+
+    @pl.when(me % 2 == 1)
+    def forward_early():
+        out_across[4].wait_recv()
+        forwards[4].start()
+
     loads[7].wait()
     logits = mm(n_all[...], wr[...], NT)
     top = jnp.max(logits, axis=1, keepdims=True)
@@ -232,6 +245,11 @@
     gate = jnp.sum(jnp.where(one_assign, probs_t, 0.0), axis=0, keepdims=True)
     meta[2:3] = gate
     gate_slot = jnp.sum(pick_own[...].astype(F32) * gate, axis=1, keepdims=True)
+    @pl.when(me % 2 == 0)
+    def forward_late():
+        out_across[4].wait_recv()
+        forwards[4].start()
+
     for k in range(3, 5):
         out_mate[k].wait_recv()
         forwards[k].wait_recv()
@@ -245,18 +263,18 @@
         part = slice(e * CAP, (e + 1) * CAP)
         d_send[part, :] = (mm(d_gate, wg[e, theirs, :], NT) + mm(d_up, wu[e, theirs, :], NT))[:CAP]
         d_keep[part, :] = (mm(d_gate, wg[e, mine, :], NT) + mm(d_up, wu[e, mine, :], NT))[:CAP]
-        if e % 2:
-            chunk = slice((e - 1) * CAP, (e + 1) * CAP)
-            d_copies.append(twin(d_send.at[chunk], d_recv.at[chunk], 6 + e // 2))
+        if e in D_PIECES:
+            chunk = slice(*D_PIECES[e])
+            d_copies.append(twin(d_send.at[chunk], d_recv.at[chunk], 7 + len(d_copies), 4))
             d_copies[-1].start()
-        if e == 3:
+        if e == 1:
             o_first = give_back(0, 0)
-
-    s_copies[1].start()
-    o_second = give_back(0, 1)
+        if e == 5:
+            o_second = give_back(0, 1)
+
 
     saves = [pltpu.make_async_copy(src, dst, out_sem.at[k]) for k, (src, dst) in enumerate((
-        (xs, xs_hbm), (us, us_hbm), (hid, h_hbm), (dab, dab_hbm), (n_all, n_hbm), (dy_all, dy_all_hbm), (hid_s, sh_hbm), (dab_s, sdab_hbm), (y_half, y_hbm), (gr_buf, gr_hbm), (dn_half, dn_hbm)))]
+        (xs, xs_hbm), (us, us_hbm), (hid, h_hbm), (dab, dab_hbm), (n_all, n_hbm), (dy_all, dy_all_hbm), (hid_s, sh_hbm), (dab_s, sdab_hbm), (y_half, y_hbm.at[:, mine]), (gr_buf, gr_hbm), (dn_half, dn_hbm)))]
     save_y, save_gr, save_dn = saves[8:]
     saves = saves[:8]
     for save in saves[:6]:
@@ -275,26 +293,30 @@
     gate_home = to_col(meta[2:3, home])
     flat_home = to_col(meta[1:2, home]).astype(jnp.int32)
     pick = (lax.broadcasted_iota(jnp.int32, (TOK, SHARDS * SLOTS), 1) == flat_home).astype(F32).astype(BF16)
+    pass_on(o_second)
     d_first = give_back(1, 0)
-    pass_on(o_second)
     arrived(o_first, False)
-    d_second = give_back(1, 1)
     arrived(o_second, True)
     tok_out = mm(pick, o_all[...].reshape(SHARDS * SLOTS, HALF))
     dg_mine[...] = to_row(jnp.sum(dy_half * tok_out, axis=1, keepdims=True))
     place = side * SHARDS + me
-    dg_copies = [pltpu.make_async_remote_copy(src_ref=dg_mine, dst_ref=dg_all.at[place], send_sem=g_send_sem.at[k], recv_sem=g_recv_sem.at[k], device_id=other, device_id_type=MESH) for k, other in enumerate(others)]
+    dg_copies = [pltpu.make_async_remote_copy(src_ref=dg_mine, dst_ref=dg_all.at[place], send_sem=g_send_sem.at[0], recv_sem=g_recv_sem.at[0], device_id=other, device_id_type=MESH) for other in others]
     for copy in dg_copies:
         copy.start()
     dg_all[place] = dg_mine[...]
+    h_copy.wait_recv()
+    for copy in sd_spread:
+        copy.wait_recv()
+    y_half[...] = (x_half + (s_keep[...] + mm(hid_twin[...], sd_twin[...])) + gate_home * tok_out).astype(BF16)
+    y_copy = twin(y_half, y_hbm.at[:, mine], 12, 5)
+    y_copy.start()
+    save_y.start()
+    d_second = give_back(1, 1)
     d_third = give_back(1, 2)
     pass_on(d_first)
-    for copy in s_copies:
-        copy.wait_recv()
-    y_half[...] = (x_half + (s_keep[...] + s_recv[...]) + gate_home * tok_out).astype(BF16)
-    save_y.start()
-    for copy in dg_copies:
-        copy.wait_recv()
+    pass_on(d_second)
+    seven = pltpu.make_async_remote_copy(src_ref=dg_all.at[1:], dst_ref=dg_all.at[1:], send_sem=g_send_sem.at[0], recv_sem=g_recv_sem.at[0], device_id=to_twin, device_id_type=MESH)
+    seven.wait_recv()
     dg = jnp.concatenate([dg_all[s, 0:1, :] + dg_all[SHARDS + s, 0:1, :] for s in range(SHARDS)], axis=1)
     one_assign = (lax.broadcasted_iota(jnp.int32, (EXPERTS, total), 0) == meta[0:1, :].astype(jnp.int32)).astype(F32)
     d_logits = (dg * meta[2:3, :] * (one_assign - probs[...])).astype(BF16)
@@ -305,13 +327,25 @@
     d_normed = n_keep[...] + n_recv[...] + mm(d_logits_home, wr[:, mine], TN)
     gr_buf[...] = mm(d_logits, n_all[...])
     save_gr.start()
-    arrived(d_second, False)
     arrived(d_first, True)
+    arrived(d_second, True)
     arrived(d_third, False)
     dn_half[...] = d_normed + mm(pick, d_all[...].reshape(SHARDS * SLOTS, HALF))
     save_dn.start()
-    for copy in out_across + out_mate + forwards + [n_copy] + s_copies + o_copies + d_copies + sum(returns, []) + dg_copies:
+    def sent(ref, sem):
+        pltpu.make_async_remote_copy(src_ref=ref, dst_ref=ref, send_sem=sem, recv_sem=sem, device_id=to_twin, device_id_type=MESH).wait_send()
+
+    for k, ref in enumerate((ids_all, x_all, dy_all)):
+        sent(ref.at[1:], send_sem.at[k])
+    for copy in (n_copy, h_copy, sd_copy, y_copy):
         copy.wait_send()
+    sent(o_send, y_send_sem.at[3])
+    sent(d_send, y_send_sem.at[4])
+    sent(sd_twin.at[: 3 * (WIDTH // SHARDS)], q_send_sem.at[0])
+    sent(o_all.at[1:], r_send_sem.at[0])
+    sent(d_all.at[1:], r_send_sem.at[1])
+    seven.wait_send()
+    y_copy.wait_recv()
     for save in saves + [save_y, save_gr, save_dn]:
         save.wait()
 
@@ -327,7 +361,7 @@
     return pl.pallas_call(
         layer_kernel,
         out_shape=(
-            shape((TOK, HALF), BF16), shape((TOK, HALF), F32), shape((EXPERTS, DIM), F32),
+            shape((TOK, DIM), BF16), shape((TOK, HALF), F32), shape((EXPERTS, DIM), F32),
             shape((rows, DIM), BF16), shape((rows, DIM), BF16), shape((rows, width), BF16), shape((rows, 2 * width), BF16),
             shape((total, DIM), BF16), shape((SHARDS, TOK, DIM), BF16), shape((total, width), BF16), shape((total, 2 * width), BF16),
         ),
@@ -341,55 +375,55 @@
             pltpu.VMEM((rows, width), F32), pltpu.VMEM((rows, width), F32), pltpu.VMEM((rows, width), BF16), pltpu.VMEM((rows, 2 * width), BF16),
             pltpu.VMEM((total, width), BF16), pltpu.VMEM((total, 2 * width), BF16),
             pltpu.VMEM((EXPERTS, total), F32), pltpu.VMEM((8, total), F32),
-            half_f32, half_f32, half_f32, half_f32, half_f32, half_f32,
+            pltpu.VMEM((TOK, width), BF16), pltpu.VMEM((TOK, width), BF16), pltpu.VMEM((width, HALF), BF16), half_f32, half_f32, half_f32, half_f32,
             slots_f32, slots_f32, slots_f32, slots_f32, slots_f32, slots_f32,
             pltpu.VMEM((SHARDS, SLOTS, HALF), BF16), pltpu.VMEM((SHARDS, SLOTS, HALF), BF16),
             pltpu.VMEM((8, TOK), F32), pltpu.VMEM((2 * SHARDS, 8, TOK), F32), pltpu.VMEM((TOK, HALF), BF16), half_f32, pltpu.VMEM((EXPERTS, DIM), F32),
-            dma((8,)), dma((3, OWN)), dma((11,)), dma((3, 5)), dma((3, 5)), dma((2, 3, 3)), dma((2, 3, 3)), dma((14,)), dma((14,)), dma((7,)), dma((7,)),
+            dma((8,)), dma((3,)), dma((11,)), dma((3,)), dma((3, 5)), dma((2,)), dma((2, 3, 3)), dma((6,)), dma((13,)), dma((1,)), dma((1,)), dma((1,)), dma((3,)),
         ],
         compiler_params=pltpu.CompilerParams(collective_id=0, has_side_effects=True, vmem_limit_bytes=60 << 20),
         name="moe_layer",
     )(x_in, y_grad, prim, alt, wr_t, exp_gate, exp_up, exp_down, sh_gate, sh_up, sh_down)
 
 
-def grads_kernel(xs_hbm, us_hbm, h_hbm, dab_hbm, n_hbm, dy_hbm, sh_hbm, sdab_hbm, gr_hbm, g_gate_hbm, g_up_hbm, g_down_hbm, gs_gate_hbm, gs_up_hbm, gs_down_hbm, g_router_hbm,
-                 xs, us, hid, dab, n_all, dy_all, hid_s, dab_s, g_router, g_gate, g_up, g_down, gs_gate, gs_up, gs_down, in_sem, out_sem, sh_sem):
+def grads_kernel(xs_hbm, us_hbm, h_hbm, dab_hbm, n_hbm, dy_hbm, sh_hbm, sdab_hbm, gr_hbm, y_hbm, g_gate_hbm, g_up_hbm, g_down_hbm, gs_gate_hbm, gs_up_hbm, gs_down_hbm, g_router_hbm, y_out_hbm,
+                 xs, us, hid, dab, n_all, dy_all, hid_s, dab_s, g_router, y_out, g_gate, g_up, g_down, gs_gate, gs_up, gs_down, in_sem, out_sem, sh_sem):
     loads = [pltpu.make_async_copy(src, dst, in_sem.at[k]) for k, (src, dst) in enumerate((
-        (h_hbm, hid), (us_hbm, us), (xs_hbm, xs), (dab_hbm, dab), (n_hbm, n_all), (sdab_hbm, dab_s), (sh_hbm, hid_s), (dy_hbm, dy_all), (gr_hbm, g_router)))]
+        (h_hbm, hid), (us_hbm, us), (xs_hbm, xs), (dab_hbm, dab), (n_hbm, n_all), (sdab_hbm, dab_s), (sh_hbm, hid_s), (dy_hbm, dy_all), (gr_hbm, g_router), (y_hbm, y_out)))]
     for load in loads:
         load.start()
-    writes = []
 
     def write(src, dst, sem):
-        writes.append(pltpu.make_async_copy(src, dst, sem))
-        writes[-1].start()
+        copy = pltpu.make_async_copy(src, dst, sem)
+        copy.start()
+        return copy
 
     for load in loads[:2]:
         load.wait()
     for e in range(OWN):
         rows = slice(e * PAD, (e + 1) * PAD)
         g_down[e] = mm(hid[rows, :], us[rows, :], TN)
-        write(g_down.at[e], g_down_hbm.at[e], out_sem.at[0, e])
+        write(g_down.at[e], g_down_hbm.at[e], out_sem.at[0])
         if e == 0:
             for load in loads[2:4]:
                 load.wait()
         both = mm(xs[rows, :], dab[rows, :], TN)
         g_gate[e] = both[:, :WIDTH]
         g_up[e] = both[:, WIDTH:]
-        write(g_gate.at[e], g_gate_hbm.at[e], out_sem.at[1, e])
-        write(g_up.at[e], g_up_hbm.at[e], out_sem.at[2, e])
+        write(g_gate.at[e], g_gate_hbm.at[e], out_sem.at[1])
+        write(g_up.at[e], g_up_hbm.at[e], out_sem.at[2])
     for load in loads[4:]:
         load.wait()
     both = mm(n_all[...], dab_s[...], TN)
     gs_gate[...] = both[:, :WIDTH]
     gs_up[...] = both[:, WIDTH:]
-    write(gs_gate, gs_gate_hbm, sh_sem.at[0])
-    write(gs_up, gs_up_hbm, sh_sem.at[1])
+    writes = [write(gs_gate, gs_gate_hbm, sh_sem.at[0]), write(gs_up, gs_up_hbm, sh_sem.at[1])]
     gs_down[...] = mm(hid_s[...], dy_all[...], TN)
-    write(gs_down, gs_down_hbm, sh_sem.at[2])
-    write(g_router, g_router_hbm, sh_sem.at[3])
+    writes += [write(gs_down, gs_down_hbm, sh_sem.at[2]), write(g_router, g_router_hbm, sh_sem.at[3]), write(y_out, y_out_hbm, sh_sem.at[4])]
     for copy in writes:
         copy.wait()
+    for k, (src, dst) in enumerate(((g_down, g_down_hbm), (g_gate, g_gate_hbm), (g_up, g_up_hbm))):
+        pltpu.make_async_copy(src, dst, out_sem.at[k]).wait()
 
 
 def grads_call(*saved):
@@ -397,22 +431,20 @@
     outs = ((OWN, DIM, WIDTH), (OWN, DIM, WIDTH), (OWN, WIDTH, DIM), (DIM, WIDTH), (DIM, WIDTH), (WIDTH, DIM), (EXPERTS, DIM))
     return pl.pallas_call(
         grads_kernel,
-        out_shape=tuple(shape(dims, F32) for dims in outs),
-        in_specs=[ANY] * 9,
-        out_specs=(ANY,) * 7,
-        scratch_shapes=[pltpu.VMEM(a.shape, a.dtype) for a in saved] + [pltpu.VMEM(dims, F32) for dims in outs[:-1]] + [pltpu.SemaphoreType.DMA((9,)), pltpu.SemaphoreType.DMA((3, OWN)), pltpu.SemaphoreType.DMA((4,))],
+        out_shape=tuple(shape(dims, F32) for dims in outs) + (shape((TOK, DIM), BF16),),
+        in_specs=[ANY] * 10,
+        out_specs=(ANY,) * 8,
+        scratch_shapes=[pltpu.VMEM(a.shape, a.dtype) for a in saved] + [pltpu.VMEM(dims, F32) for dims in outs[:-1]] + [pltpu.SemaphoreType.DMA((10,)), pltpu.SemaphoreType.DMA((3,)), pltpu.SemaphoreType.DMA((5,))],
         compiler_params=pltpu.CompilerParams(vmem_limit_bytes=63 << 20),
         cost_estimate=pl.CostEstimate(flops=8 << 30, bytes_accessed=32 << 20, transcendentals=0),
         name="weight_grads",
     )(*saved)
 
 
-def finish_kernel(x_ref, dy_ref, y_mine, y_recv, dn_mine, dn_recv, y_out, dx_out):
+def finish_kernel(x_ref, dy_ref, dn_mine, dn_recv, dx_out):
     side = lax.axis_index("etp")
     theirs = pl.ds(pl.multiple_of((1 - side) * HALF, HALF), HALF)
     mine = pl.ds(pl.multiple_of(side * HALF, HALF), HALF)
-    y_out[:, mine] = y_mine[...]
-    y_out[:, theirs] = y_recv[...]
     x_wide = x_ref[...].astype(F32)
     inv_rms = inv_rms_of(x_wide)
     halves = ((mine, dn_mine), (theirs, dn_recv))
@@ -422,12 +454,11 @@
 
 
 def finish_call(*args):
-    shape = jax.ShapeDtypeStruct
     return pl.pallas_call(
         finish_kernel,
-        out_shape=(shape((TOK, DIM), BF16), shape((TOK, DIM), BF16)),
-        in_specs=[VMEM] * 6,
-        out_specs=(VMEM,) * 2,
+        out_shape=jax.ShapeDtypeStruct((TOK, DIM), BF16),
+        in_specs=[VMEM] * 4,
+        out_specs=VMEM,
         compiler_params=pltpu.CompilerParams(vmem_limit_bytes=8 << 20),
         name="finish_tokens",
     )(*args)
@@ -440,12 +471,10 @@
     out_specs = (tok_spec, tok_spec, P(("dp", "ep"), None, "etp"), P(("dp", "ep"), None, "etp"), P(("dp", "ep"), "etp", None), P("dp", "etp"), P("dp", "etp"), P(("dp", "etp"), None), P("dp", None))
 
     def local_step(x_in, y_grad, prim_exp, alt_exp, w_router, exp_gate, exp_up, exp_down, sh_gate, sh_up, sh_down):
-        y_half, dn_half, gr, xs, us, hid, dab, n_all, dy_all, hid_s, dab_s = layer_call(x_in, y_grad, prim_exp.reshape(1, TOK), alt_exp.reshape(1, TOK), w_router.T, exp_gate, exp_up, exp_down, sh_gate, sh_up, sh_down)
-        swap = [(0, 1), (1, 0)]
-        dn_other = lax.ppermute(dn_half, "etp", swap)
-        y_other = lax.ppermute(y_half, "etp", swap)
-        g_gate, g_up, g_down, gs_gate, gs_up, gs_down, g_router = grads_call(xs, us, hid, dab, n_all, dy_all.reshape(SHARDS * TOK, DIM), hid_s, dab_s, gr)
-        y_out, x_grad = finish_call(x_in, y_grad, y_half, y_other, dn_half, dn_other)
+        y_full, dn_half, gr, xs, us, hid, dab, n_all, dy_all, hid_s, dab_s = layer_call(x_in, y_grad, prim_exp.reshape(1, TOK), alt_exp.reshape(1, TOK), w_router.T, exp_gate, exp_up, exp_down, sh_gate, sh_up, sh_down)
+        dn_other = lax.ppermute(dn_half, "etp", [(0, 1), (1, 0)])
+        g_gate, g_up, g_down, gs_gate, gs_up, gs_down, g_router, y_out = grads_call(xs, us, hid, dab, n_all, dy_all.reshape(SHARDS * TOK, DIM), hid_s, dab_s, gr, y_full)
+        x_grad = finish_call(x_in, y_grad, dn_half, dn_other)
         return (y_out, x_grad, g_gate, g_up, g_down, gs_gate, gs_up, gs_down, g_router.T)
 
     return jax.shard_map(local_step, mesh=mesh, in_specs=in_specs, out_specs=out_specs, check_vma=False)

time: 54.4 us -> 51 us (0.938)
  Pallas kernels: 51.5 us -> 49 us
  starting transfers between devices: 2.05 us -> 1.16 us
    pallas_call x2, Pallas kernels: 40.3 us -> 37.9 us  [the longest x1 35.9 us: layer_call(): pl.pallas_call(layer_kernel, out_shape=(shape((TOK, DIM), BF16), shape((T...]
    ppermute x2 -> x1, starting transfers between devices: 2.05 us -> 1.16 us  [local_step(): dn_other = lax.ppermute(dn_half, 'etp', [(0, 1), (1, 0)])]
  transfers between devices with their start and end apart: 2 -> 1, of which waited for: 0 -> 0; matrix products, arithmetic and copies ran while one was open for 0% -> 0% of each run, Pallas kernels for 21% -> 22%
where the time goes in v4:
time: 51 us; the launch traced here: 50.9 us
  Pallas kernels  49 us (96%)
  starting transfers between devices  1.16 us (2%)
  between operations  0.7 us (1%)
    pallas_call x1, Pallas kernels, layer_call(): pl.pallas_call(layer_kernel, out_shape=(shape((TOK, DIM), BF16), shape((T...  35.9 us
    pallas_call x1, Pallas kernels, grads_call(): pl.pallas_call(grads_kernel, out_shape=tuple((shape(dims, F32) for dims i...  11.1 us
    pallas_call x1, Pallas kernels, finish_call(): pl.pallas_call(finish_kernel, out_shape=jax.ShapeDtypeStruct((TOK, DIM),...  1.91 us
    ppermute x1, starting transfers between devices, local_step(): dn_other = lax.ppermute(dn_half, 'etp', [(0, 1), (1, 0)])  1.16 us
  transfers between devices with their start and end apart: 1, of which 0 were waited for; matrix products, arithmetic and copies ran while one was open for 0% of the time, Pallas kernels for 22%

profile of v4, /device:TPU:0, one launch (start us, length us, event | category | flops | bytes accessed | tf_op | source)
XLA Modules:
  0.0 50.9 jit_solution(16923092034484166163)
XLA Ops:
  0.6 35.9 %moe_layer.1 = (bf16[128,1024]{1,0:T(8,128)(2,1)}, f32[128,512]{1,0:T(8,128)}, f32[32,1024]{1,0:T(8,128)}, bf16[256,1024]{1,0:T(8,128)(2,1)}, bf16[256,1024]{1,0...) custom-call(bf16[128,1024]{1,0:T(8,128)(2,1)} %x_ref.1, ...), custom_call_target="tpu_custom_call" | custom-call | tf_op jit(solution)/shard_map/moe_layer/pallas_call | solution.py:361
  36.6 1.2 %collective-permute-start = (f32[128,512]{1,0:T(8,128)}, f32[128,512]{1,0:T(8,128)}, u32[]{:S(2)}, u32[]{:S(2)}) collective-permute-start(f32[128,512]{1,0:T(8,128)} %get-tuple-element.39.dn_mine), channel_id=1, source_target_pairs={{0,4},{4,0},{1,5},{5,1},{2,6},{6,2},{3,7},{7,3}} | collective-permute-start | bytes 786440 | tf_op jit(solution)/shard_map/ppermute | solution.py:475
  37.8 0.0 copy-start
  37.8 0.0 copy-start.1
  37.8 0.0 copy-start.2
  37.8 11.1 %weight_grads.1 = (f32[8,1024,256]{2,1,0:T(8,128)}, f32[8,1024,256]{2,1,0:T(8,128)}, f32[8,256,1024]{2,1,0:T(8,128)}, f32[1024,256]{1,0:T(8,128)}, f32[1024,256]...) custom-call(bf16[256,1024]{1,0:T(8,128)(2,1)} %get-tuple-element.28.xs_hbm, ...), custom_call_target="tpu_custom_call" | custom-call | flops 8589934592 | bytes 33554432 | tf_op jit(solution)/shard_map/weight_grads/pallas_call | solution.py:432
  48.9 0.0 collective-permute-done.dn_recv
  48.9 0.0 copy-done
  48.9 0.0 copy-done.1
  48.9 0.0 copy-done.2
  49.0 1.9 %finish_tokens.1 = bf16[128,1024]{1,0:T(8,128)(2,1)} custom-call(bf16[128,1024]{1,0:T(8,128)(2,1)S(1)} %copy-done, bf16[128,1024]{1,0:T(8,128)(2,1)S(1)} %copy-done.1, f32[128,512]{1,0:T(8,128)S(1)} %copy-done.2, f32[128,512]{1,0:T(8,128)} %collective-permute-done.dn_recv), custom_call_target="tpu_custom_call" | custom-call | tf_op jit(solution)/shard_map/finish_tokens/pallas_call | solution.py:457
Async XLA Ops:
  36.6 12.3 %collective-permute-start = (f32[128,512]{1,0:T(8,128)}, f32[128,512]{1,0:T(8,128)}, u32[]{:S(2)}, u32[]{:S(2)}) collective-permute-start(f32[128,512]{1,0:T(8,128)} %get-tuple-element.39.dn_mine), channel_id=1, source_target_pairs={{0,4},{4,0},{1,5},{5,1},{2,6},{6,2},{3,7},{7,3}} | collective-permute-start | bytes 786440 | tf_op jit(solution)/shard_map/ppermute | solution.py:475
  37.8 11.2 %copy-start = (bf16[128,1024]{1,0:T(8,128)(2,1)S(1)}, bf16[128,1024]{1,0:T(8,128)(2,1)}, u32[]{:S(2)}) copy-start(bf16[128,1024]{1,0:T(8,128)(2,1)} %x_ref.1) | copy-start | bytes 786436
  37.8 11.2 %copy-start.1 = (bf16[128,1024]{1,0:T(8,128)(2,1)S(1)}, bf16[128,1024]{1,0:T(8,128)(2,1)}, u32[]{:S(2)}) copy-start(bf16[128,1024]{1,0:T(8,128)(2,1)} %dy_ref.1) | copy-start | bytes 786436
  37.8 11.2 %copy-start.2 = (f32[128,512]{1,0:T(8,128)S(1)}, f32[128,512]{1,0:T(8,128)}, u32[]{:S(2)}) copy-start(f32[128,512]{1,0:T(8,128)} %get-tuple-element.39.dn_mine) | copy-start | bytes 786436

commit v5 on v4

--- a/solution.py
+++ b/solution.py
@@ -60,11 +60,11 @@
 
 
 def layer_kernel(x_hbm, dy_hbm, prim_hbm, alt_hbm, wr_hbm, wg_hbm, wu_hbm, wd_hbm, sg_hbm, su_hbm, sd_hbm,
-                 y_hbm, dn_hbm, gr_hbm, xs_hbm, us_hbm, h_hbm, dab_hbm, n_hbm, dy_all_hbm, sh_hbm, sdab_hbm,
-                 x_all, dy_all, ids_all, wr, wg, wu, wd, sg, su, sd, n_all, xs, us, pick_own, acts, acts_up, hid, dab, hid_s, dab_s,
+                 y_out, dn_half, gr_out, xs, us, hid, dab, n_all, dy_all, hid_s, dab_s,
+                 x_all, ids_all, wr, wg, wu, wd, sg, su, sd, pick_own, acts, acts_up,
                  probs, meta, hid_own, hid_twin, sd_twin, s_keep, n_send, n_recv, n_keep, o_send, o_recv, o_keep, d_send, d_recv, d_keep,
-                 o_all, d_all, dg_mine, dg_all, y_half, dn_half, gr_buf,
-                 in_sem, w_sem, out_sem, send_sem, recv_sem, r_send_sem, r_recv_sem, y_send_sem, y_recv_sem, g_send_sem, g_recv_sem, q_send_sem, q_recv_sem):
+                 o_all, d_all, dg_mine, dg_all,
+                 in_sem, w_sem, send_sem, recv_sem, r_send_sem, r_recv_sem, y_send_sem, y_recv_sem, g_send_sem, g_recv_sem, q_send_sem, q_recv_sem):
     me = lax.axis_index("ep")
     side = lax.axis_index("etp")
     total = SHARDS * TOK
@@ -177,6 +177,7 @@
     norm(jnp.bitwise_xor(me, 3))
     xs[...] = mm(pick_own[...], n_all[...]).astype(BF16)
 
+    O_PIECES = {0: (0, 16), 1: (16, 40), 3: (40, 80), 5: (80, 120), 7: (120, 160)}
     o_copies, d_copies = [], []
     for e in range(OWN):
         if e == 0:
@@ -192,17 +193,17 @@
         part = slice(e * CAP, (e + 1) * CAP)
         o_send[part, :] = mm(hidden, wd[e, :, theirs])[:CAP]
         o_keep[part, :] = mm(hidden, wd[e, :, mine])[:CAP]
-        if e % 2:
-            chunk = slice((e - 1) * CAP, (e + 1) * CAP)
-            o_copies.append(twin(o_send.at[chunk], o_recv.at[chunk], 3 + e // 2, 3))
+        if e in O_PIECES:
+            chunk = slice(*O_PIECES[e])
+            o_copies.append(twin(o_send.at[chunk], o_recv.at[chunk], 13 if e == 0 else 3 + e // 2, 3))
             o_copies[-1].start()
         if e == 5:
             out_across[3].wait_recv()
             forwards[3].start()
     D_PIECES = {1: (0, 40), 3: (40, 80), 5: (80, 120), 6: (120, 136), 7: (136, 160)}
     CHUNKS = (((0, 80), (80, 160)), ((0, 80), (80, 128), (128, 160)))
-    READY = ((2, 4), (2, 4, 5))
-    DIRECT = ((True, False), (False, False, True))
+    READY = ((3, 5), (2, 4, 5))
+    DIRECT = ((False, False), (False, False, True))
 
     def give_back(lane, chunk):
         buf, keep, recv, copies = ((o_all, o_keep, o_recv, o_copies), (d_all, d_keep, d_recv, d_copies))[lane]
@@ -273,29 +274,22 @@
             o_second = give_back(0, 1)
 
 
-    saves = [pltpu.make_async_copy(src, dst, out_sem.at[k]) for k, (src, dst) in enumerate((
-        (xs, xs_hbm), (us, us_hbm), (hid, h_hbm), (dab, dab_hbm), (n_all, n_hbm), (dy_all, dy_all_hbm), (hid_s, sh_hbm), (dab_s, sdab_hbm), (y_half, y_hbm.at[:, mine]), (gr_buf, gr_hbm), (dn_half, dn_hbm)))]
-    save_y, save_gr, save_dn = saves[8:]
-    saves = saves[:8]
-    for save in saves[:6]:
-        save.start()
+    pass_on(o_first)
     act_gate = mm(n_all[...], sg[...])
     act_up = mm(n_all[...], su[...])
     hid_s[...] = (jax.nn.silu(act_gate) * act_up).astype(BF16)
     d_gate, d_up = glu_grads(mm(dy_all[...].reshape(total, DIM), sd[...], NT), act_gate, act_up)
     dab_s[:, :WIDTH] = d_gate
     dab_s[:, WIDTH:] = d_up
-    for save in saves[6:]:
-        save.start()
 
     x_half = x_all[me, :, mine].astype(F32)
     dy_half = dy_all[me, :, mine].astype(F32)
     gate_home = to_col(meta[2:3, home])
     flat_home = to_col(meta[1:2, home]).astype(jnp.int32)
     pick = (lax.broadcasted_iota(jnp.int32, (TOK, SHARDS * SLOTS), 1) == flat_home).astype(F32).astype(BF16)
+    d_first = give_back(1, 0)
     pass_on(o_second)
-    d_first = give_back(1, 0)
-    arrived(o_first, False)
+    arrived(o_first, True)
     arrived(o_second, True)
     tok_out = mm(pick, o_all[...].reshape(SHARDS * SLOTS, HALF))
     dg_mine[...] = to_row(jnp.sum(dy_half * tok_out, axis=1, keepdims=True))
@@ -307,10 +301,9 @@
     h_copy.wait_recv()
     for copy in sd_spread:
         copy.wait_recv()
-    y_half[...] = (x_half + (s_keep[...] + mm(hid_twin[...], sd_twin[...])) + gate_home * tok_out).astype(BF16)
-    y_copy = twin(y_half, y_hbm.at[:, mine], 12, 5)
+    y_out[:, mine] = (x_half + (s_keep[...] + mm(hid_twin[...], sd_twin[...])) + gate_home * tok_out).astype(BF16)
+    y_copy = twin(y_out.at[:, mine], y_out.at[:, mine], 12, 5)
     y_copy.start()
-    save_y.start()
     d_second = give_back(1, 1)
     d_third = give_back(1, 2)
     pass_on(d_first)
@@ -325,13 +318,11 @@
     d_logits_home = (dg_home * meta[2:3, home] * (home_one - probs[:, home])).astype(BF16)
     n_copy.wait_recv()
     d_normed = n_keep[...] + n_recv[...] + mm(d_logits_home, wr[:, mine], TN)
-    gr_buf[...] = mm(d_logits, n_all[...])
-    save_gr.start()
+    gr_out[...] = mm(d_logits, n_all[...])
     arrived(d_first, True)
     arrived(d_second, True)
     arrived(d_third, False)
     dn_half[...] = d_normed + mm(pick, d_all[...].reshape(SHARDS * SLOTS, HALF))
-    save_dn.start()
     def sent(ref, sem):
         pltpu.make_async_remote_copy(src_ref=ref, dst_ref=ref, send_sem=sem, recv_sem=sem, device_id=to_twin, device_id_type=MESH).wait_send()
 
@@ -346,8 +337,6 @@
     sent(d_all.at[1:], r_send_sem.at[1])
     seven.wait_send()
     y_copy.wait_recv()
-    for save in saves + [save_y, save_gr, save_dn]:
-        save.wait()
 
 
 def layer_call(x_in, y_grad, prim, alt, wr_t, exp_gate, exp_up, exp_down, sh_gate, sh_up, sh_down):
@@ -366,54 +355,41 @@
             shape((total, DIM), BF16), shape((SHARDS, TOK, DIM), BF16), shape((total, width), BF16), shape((total, 2 * width), BF16),
         ),
         in_specs=[ANY] * 11,
-        out_specs=(ANY,) * 11,
+        out_specs=(VMEM,) * 11,
         scratch_shapes=[
-            pltpu.VMEM((SHARDS, TOK, DIM), BF16), pltpu.VMEM((SHARDS, TOK, DIM), BF16), pltpu.VMEM((SHARDS, 8, TOK), jnp.int32), pltpu.VMEM((EXPERTS, DIM), BF16),
+            pltpu.VMEM((SHARDS, TOK, DIM), BF16), pltpu.VMEM((SHARDS, 8, TOK), jnp.int32), pltpu.VMEM((EXPERTS, DIM), BF16),
             pltpu.VMEM((OWN, DIM, width), BF16), pltpu.VMEM((OWN, DIM, width), BF16), pltpu.VMEM((OWN, width, DIM), BF16),
             pltpu.VMEM((DIM, width), BF16), pltpu.VMEM((DIM, width), BF16), pltpu.VMEM((width, DIM), BF16),
-            pltpu.VMEM((total, DIM), BF16), pltpu.VMEM((rows, DIM), BF16), pltpu.VMEM((rows, DIM), BF16), pltpu.VMEM((rows, total), BF16),
-            pltpu.VMEM((rows, width), F32), pltpu.VMEM((rows, width), F32), pltpu.VMEM((rows, width), BF16), pltpu.VMEM((rows, 2 * width), BF16),
-            pltpu.VMEM((total, width), BF16), pltpu.VMEM((total, 2 * width), BF16),
+            pltpu.VMEM((rows, total), BF16),
+            pltpu.VMEM((rows, width), F32), pltpu.VMEM((rows, width), F32),
             pltpu.VMEM((EXPERTS, total), F32), pltpu.VMEM((8, total), F32),
             pltpu.VMEM((TOK, width), BF16), pltpu.VMEM((TOK, width), BF16), pltpu.VMEM((width, HALF), BF16), half_f32, half_f32, half_f32, half_f32,
             slots_f32, slots_f32, slots_f32, slots_f32, slots_f32, slots_f32,
             pltpu.VMEM((SHARDS, SLOTS, HALF), BF16), pltpu.VMEM((SHARDS, SLOTS, HALF), BF16),
-            pltpu.VMEM((8, TOK), F32), pltpu.VMEM((2 * SHARDS, 8, TOK), F32), pltpu.VMEM((TOK, HALF), BF16), half_f32, pltpu.VMEM((EXPERTS, DIM), F32),
-            dma((8,)), dma((3,)), dma((11,)), dma((3,)), dma((3, 5)), dma((2,)), dma((2, 3, 3)), dma((6,)), dma((13,)), dma((1,)), dma((1,)), dma((1,)), dma((3,)),
+            pltpu.VMEM((8, TOK), F32), pltpu.VMEM((2 * SHARDS, 8, TOK), F32),
+            dma((8,)), dma((3,)), dma((3,)), dma((3, 5)), dma((2,)), dma((2, 3, 3)), dma((6,)), dma((14,)), dma((1,)), dma((1,)), dma((1,)), dma((3,)),
         ],
-        compiler_params=pltpu.CompilerParams(collective_id=0, has_side_effects=True, vmem_limit_bytes=60 << 20),
+        compiler_params=pltpu.CompilerParams(collective_id=0, has_side_effects=True, vmem_limit_bytes=40 << 20),
         name="moe_layer",
     )(x_in, y_grad, prim, alt, wr_t, exp_gate, exp_up, exp_down, sh_gate, sh_up, sh_down)
 
 
-def grads_kernel(xs_hbm, us_hbm, h_hbm, dab_hbm, n_hbm, dy_hbm, sh_hbm, sdab_hbm, gr_hbm, y_hbm, g_gate_hbm, g_up_hbm, g_down_hbm, gs_gate_hbm, gs_up_hbm, gs_down_hbm, g_router_hbm, y_out_hbm,
-                 xs, us, hid, dab, n_all, dy_all, hid_s, dab_s, g_router, y_out, g_gate, g_up, g_down, gs_gate, gs_up, gs_down, in_sem, out_sem, sh_sem):
-    loads = [pltpu.make_async_copy(src, dst, in_sem.at[k]) for k, (src, dst) in enumerate((
-        (h_hbm, hid), (us_hbm, us), (xs_hbm, xs), (dab_hbm, dab), (n_hbm, n_all), (sdab_hbm, dab_s), (sh_hbm, hid_s), (dy_hbm, dy_all), (gr_hbm, g_router), (y_hbm, y_out)))]
-    for load in loads:
-        load.start()
-
+def grads_kernel(xs, us, hid, dab, n_all, dy_all, hid_s, dab_s, g_router, y_out, g_gate_hbm, g_up_hbm, g_down_hbm, gs_gate_hbm, gs_up_hbm, gs_down_hbm, g_router_hbm, y_out_hbm,
+                 g_gate, g_up, g_down, gs_gate, gs_up, gs_down, out_sem, sh_sem):
     def write(src, dst, sem):
         copy = pltpu.make_async_copy(src, dst, sem)
         copy.start()
         return copy
 
-    for load in loads[:2]:
-        load.wait()
     for e in range(OWN):
         rows = slice(e * PAD, (e + 1) * PAD)
         g_down[e] = mm(hid[rows, :], us[rows, :], TN)
         write(g_down.at[e], g_down_hbm.at[e], out_sem.at[0])
-        if e == 0:
-            for load in loads[2:4]:
-                load.wait()
         both = mm(xs[rows, :], dab[rows, :], TN)
         g_gate[e] = both[:, :WIDTH]
         g_up[e] = both[:, WIDTH:]
         write(g_gate.at[e], g_gate_hbm.at[e], out_sem.at[1])
         write(g_up.at[e], g_up_hbm.at[e], out_sem.at[2])
-    for load in loads[4:]:
-        load.wait()
     both = mm(n_all[...], dab_s[...], TN)
     gs_gate[...] = both[:, :WIDTH]
     gs_up[...] = both[:, WIDTH:]
@@ -432,10 +408,10 @@
     return pl.pallas_call(
         grads_kernel,
         out_shape=tuple(shape(dims, F32) for dims in outs) + (shape((TOK, DIM), BF16),),
-        in_specs=[ANY] * 10,
+        in_specs=[VMEM] * 10,
         out_specs=(ANY,) * 8,
-        scratch_shapes=[pltpu.VMEM(a.shape, a.dtype) for a in saved] + [pltpu.VMEM(dims, F32) for dims in outs[:-1]] + [pltpu.SemaphoreType.DMA((10,)), pltpu.SemaphoreType.DMA((3,)), pltpu.SemaphoreType.DMA((5,))],
-        compiler_params=pltpu.CompilerParams(vmem_limit_bytes=63 << 20),
+        scratch_shapes=[pltpu.VMEM(dims, F32) for dims in outs[:-1]] + [pltpu.SemaphoreType.DMA((3,)), pltpu.SemaphoreType.DMA((5,))],
+        compiler_params=pltpu.CompilerParams(vmem_limit_bytes=44 << 20),
         cost_estimate=pl.CostEstimate(flops=8 << 30, bytes_accessed=32 << 20, transcendentals=0),
         name="weight_grads",
     )(*saved)
@@ -471,7 +447,7 @@
     out_specs = (tok_spec, tok_spec, P(("dp", "ep"), None, "etp"), P(("dp", "ep"), None, "etp"), P(("dp", "ep"), "etp", None), P("dp", "etp"), P("dp", "etp"), P(("dp", "etp"), None), P("dp", None))
 
     def local_step(x_in, y_grad, prim_exp, alt_exp, w_router, exp_gate, exp_up, exp_down, sh_gate, sh_up, sh_down):
-        y_full, dn_half, gr, xs, us, hid, dab, n_all, dy_all, hid_s, dab_s = layer_call(x_in, y_grad, prim_exp.reshape(1, TOK), alt_exp.reshape(1, TOK), w_router.T, exp_gate, exp_up, exp_down, sh_gate, sh_up, sh_down)
+        y_full, dn_half, gr, xs, us, hid, dab, n_all, dy_all, hid_s, dab_s = layer_call(*[pltpu.with_memory_space_constraint(a, pltpu.HBM) for a in (x_in, y_grad, prim_exp.reshape(1, TOK), alt_exp.reshape(1, TOK), w_router.T, exp_gate, exp_up, exp_down, sh_gate, sh_up, sh_down)])
         dn_other = lax.ppermute(dn_half, "etp", [(0, 1), (1, 0)])
         g_gate, g_up, g_down, gs_gate, gs_up, gs_down, g_router, y_out = grads_call(xs, us, hid, dab, n_all, dy_all.reshape(SHARDS * TOK, DIM), hid_s, dab_s, gr, y_full)
         x_grad = finish_call(x_in, y_grad, dn_half, dn_other)

time: 51 us -> 47.7 us (0.935)
  Pallas kernels: 49 us -> 45.5 us
    pallas_call x1, Pallas kernels: 11.1 us -> 9.76 us  [grads_call(): pl.pallas_call(grads_kernel, out_shape=tuple((shape(dims, F32) for dims i...]
    pallas_call x1, Pallas kernels: 35.9 us -> 34.8 us  [layer_call(): pl.pallas_call(layer_kernel, out_shape=(shape((TOK, DIM), BF16), shape((T...]
    pallas_call x1, Pallas kernels: 1.91 us -> 0.96 us  [finish_call(): pl.pallas_call(finish_kernel, out_shape=jax.ShapeDtypeStruct((TOK, DIM),...]
  transfers between devices with their start and end apart: 1 -> 1, of which waited for: 0 -> 0; matrix products, arithmetic and copies ran while one was open for 0% -> 0% of each run, Pallas kernels for 22% -> 21%
where the time goes in v5:
time: 47.7 us; the launch traced here: 47.6 us
  Pallas kernels  45.5 us (95%)
  starting transfers between devices  1.39 us (3%)
  between operations  0.69 us (1%)
    pallas_call x1, Pallas kernels, layer_call(): pl.pallas_call(layer_kernel, out_shape=(shape((TOK, DIM), BF16), shape((T...  34.8 us
    pallas_call x1, Pallas kernels, grads_call(): pl.pallas_call(grads_kernel, out_shape=tuple((shape(dims, F32) for dims i...  9.76 us
    ppermute x1, starting transfers between devices, local_step(): dn_other = lax.ppermute(dn_half, 'etp', [(0, 1), (1, 0)])  1.39 us
    pallas_call x1, Pallas kernels, finish_call(): pl.pallas_call(finish_kernel, out_shape=jax.ShapeDtypeStruct((TOK, DIM),...  0.96 us
  transfers between devices with their start and end apart: 1, of which 0 were waited for; matrix products, arithmetic and copies ran while one was open for 0% of the time, Pallas kernels for 21%

profile of v5, /device:TPU:0, one launch (start us, length us, event | category | flops | bytes accessed | tf_op | source)
XLA Modules:
  0.0 47.6 jit_solution(14684043905256593622)
XLA Ops:
  0.6 34.8 %moe_layer.1 = (bf16[128,1024]{1,0:T(8,128)(2,1)S(1)}, f32[128,512]{1,0:T(8,128)S(1)}, f32[32,1024]{1,0:T(8,128)S(1)}, bf16[256,1024]{1,0:T(8,128)(2,1)S(1)}, bf...) custom-call(bf16[128,1024]{1,0:T(8,128)(2,1)} %x_ref.1, ...), custom_call_target="tpu_custom_call" | custom-call | tf_op jit(solution)/shard_map/moe_layer/pallas_call | solution.py:350
  35.4 1.4 %collective-permute-start = (f32[128,512]{1,0:T(8,128)S(1)}, f32[128,512]{1,0:T(8,128)S(1)}, u32[]{:S(2)}, u32[]{:S(2)}) collective-permute-start(f32[128,512]{1,0:T(8,128)S(1)} %get-tuple-element.39.dn_mine), channel_id=1, source_target_pairs={{0,4},{4,0},{1,5},{5,1},{2,6},{6,2},{3,7},{7,3}} | collective-permute-start | bytes 786440 | tf_op jit(solution)/shard_map/ppermute | solution.py:451
  36.8 0.0 copy-start
  36.8 0.0 copy-start.1
  36.8 9.8 %weight_grads.1 = (f32[8,1024,256]{2,1,0:T(8,128)}, f32[8,1024,256]{2,1,0:T(8,128)}, f32[8,256,1024]{2,1,0:T(8,128)}, f32[1024,256]{1,0:T(8,128)}, f32[1024,256]...) custom-call(bf16[256,1024]{1,0:T(8,128)(2,1)S(1)} %get-tuple-element.28.xs, ...), custom_call_target="tpu_custom_call" | custom-call | flops 8589934592 | bytes 33554432 | tf_op jit(solution)/shard_map/weight_grads/pallas_call | solution.py:408
  46.6 0.0 collective-permute-done.dn_recv
  46.6 0.0 copy-done
  46.6 0.0 copy-done.1
  46.6 1.0 %finish_tokens.1 = bf16[128,1024]{1,0:T(8,128)(2,1)} custom-call(bf16[128,1024]{1,0:T(8,128)(2,1)S(1)} %copy-done, bf16[128,1024]{1,0:T(8,128)(2,1)S(1)} %copy-done.1, f32[128,512]{1,0:T(8,128)S(1)} %get-tuple-element.39.dn_mine, f32[128,512]{1,0:T(8,128)S(1)} %collective-permute-done.dn_recv), custom_call_target="tpu_custom_call" | custom-call | tf_op jit(solution)/shard_map/finish_tokens/pallas_call | solution.py:433
Async XLA Ops:
  35.4 11.2 %collective-permute-start = (f32[128,512]{1,0:T(8,128)S(1)}, f32[128,512]{1,0:T(8,128)S(1)}, u32[]{:S(2)}, u32[]{:S(2)}) collective-permute-start(f32[128,512]{1,0:T(8,128)S(1)} %get-tuple-element.39.dn_mine), channel_id=1, source_target_pairs={{0,4},{4,0},{1,5},{5,1},{2,6},{6,2},{3,7},{7,3}} | collective-permute-start | bytes 786440 | tf_op jit(solution)/shard_map/ppermute | solution.py:451
  36.8 9.8 %copy-start = (bf16[128,1024]{1,0:T(8,128)(2,1)S(1)}, bf16[128,1024]{1,0:T(8,128)(2,1)}, u32[]{:S(2)}) copy-start(bf16[128,1024]{1,0:T(8,128)(2,1)} %x_ref.1) | copy-start | bytes 786436
  36.8 9.8 %copy-start.1 = (bf16[128,1024]{1,0:T(8,128)(2,1)S(1)}, bf16[128,1024]{1,0:T(8,128)(2,1)}, u32[]{:S(2)}) copy-start(bf16[128,1024]{1,0:T(8,128)(2,1)} %dy_ref.1) | copy-start | bytes 786436

commit v6 on v5

--- a/solution.py
+++ b/solution.py
@@ -61,7 +61,7 @@
 
 def layer_kernel(x_hbm, dy_hbm, prim_hbm, alt_hbm, wr_hbm, wg_hbm, wu_hbm, wd_hbm, sg_hbm, su_hbm, sd_hbm,
                  y_out, dn_half, gr_out, xs, us, hid, dab, n_all, dy_all, hid_s, dab_s,
-                 x_all, ids_all, wr, wg, wu, wd, sg, su, sd, pick_own, acts, acts_up,
+                 x_all, ids_all, wr, wg, wu, wd, sg, su, sd, pick_own, xs_sum, acts, acts_up,
                  probs, meta, hid_own, hid_twin, sd_twin, s_keep, n_send, n_recv, n_keep, o_send, o_recv, o_keep, d_send, d_recv, d_keep,
                  o_all, d_all, dg_mine, dg_all,
                  in_sem, w_sem, send_sem, recv_sem, r_send_sem, r_recv_sem, y_send_sem, y_recv_sem, g_send_sem, g_recv_sem, q_send_sem, q_recv_sem):
@@ -85,7 +85,7 @@
     barrier(others)
 
     def remote(view, lane, k, target):
-        return pltpu.make_async_remote_copy(src_ref=view, dst_ref=view, send_sem=send_sem.at[(k + 1) // 2], recv_sem=recv_sem.at[lane, k], device_id=target, device_id_type=MESH)
+        return pltpu.make_async_remote_copy(src_ref=view, dst_ref=view, send_sem=send_sem.at[(k + 1) // 2], recv_sem=recv_sem.at[k if lane == 0 else (4 + lane, 6 + lane, 9)[(k + 1) // 2]], device_id=target, device_id_type=MESH)
 
     def twin(src, dst, k, group):
         return pltpu.make_async_remote_copy(src_ref=src, dst_ref=dst, send_sem=y_send_sem.at[group], recv_sem=y_recv_sem.at[k], device_id=to_twin, device_id_type=MESH)
@@ -113,6 +113,9 @@
         out_mate[k].start()
     for load in w_loads:
         load.start()
+
+    def landed(ref, sem):
+        pltpu.make_async_remote_copy(src_ref=ref, dst_ref=ref, send_sem=sem, recv_sem=sem, device_id=to_twin, device_id_type=MESH).wait_recv()
 
     x_wide = x_all[me].astype(F32)
     normed = (x_wide * inv_rms_of(x_wide)).astype(BF16)
@@ -162,23 +165,29 @@
 
     sd_copy.wait_recv()
     view = sd_twin.at[quarter(me)]
-    sd_spread = [pltpu.make_async_remote_copy(src_ref=view, dst_ref=view, send_sem=q_send_sem.at[0], recv_sem=q_recv_sem.at[k - 1], device_id={"ep": jnp.bitwise_xor(me, k)}, device_id_type=MESH) for k in range(1, SHARDS)]
+    sd_spread = [pltpu.make_async_remote_copy(src_ref=view, dst_ref=view, send_sem=q_send_sem.at[0], recv_sem=q_recv_sem.at[0], device_id={"ep": jnp.bitwise_xor(me, k)}, device_id_type=MESH) for k in range(1, SHARDS)]
     for copy in sd_spread:
         copy.start()
-    for k in range(1, 3):
-        out_mate[k].wait_recv()
+    def picked(shard):
+        rows = pl.ds(pl.multiple_of(shard * TOK, TOK), TOK)
+        return mm(pick_own[:, rows], n_all[rows, :])
+
+    landed(x_all.at[0], recv_sem.at[7])
     norm(mate)
+    xs_sum[...] = picked(me) + picked(mate)
     for k in range(1, 3):
         out_across[k].wait_recv()
         forwards[k].start()
     norm(across)
-    for k in range(1, 3):
-        forwards[k].wait_recv()
+    xs_sum[...] += picked(across)
+    landed(x_all.at[0], recv_sem.at[8])
     norm(jnp.bitwise_xor(me, 3))
-    xs[...] = mm(pick_own[...], n_all[...]).astype(BF16)
-
-    O_PIECES = {0: (0, 16), 1: (16, 40), 3: (40, 80), 5: (80, 120), 7: (120, 160)}
-    o_copies, d_copies = [], []
+    xs[...] = (xs_sum[...] + picked(jnp.bitwise_xor(me, 3))).astype(BF16)
+
+    O_PIECES = {0: (0, 16, 0), 1: (16, 40, 0), 3: (40, 80, 0), 5: (80, 120, 1), 6: (120, 136, 1), 7: (136, 160, 2)}
+    D_PIECES = {1: (0, 40, 0), 3: (40, 80, 0), 5: (80, 120, 1), 6: (120, 136, 1), 7: (136, 160, 2)}
+    LANDED = ((0, 80), (80, 136), (136, 160))
+    CHUNKS = ((0, 80), (80, 128), (128, 160))
     for e in range(OWN):
         if e == 0:
             for load in w_loads:
@@ -194,30 +203,24 @@
         o_send[part, :] = mm(hidden, wd[e, :, theirs])[:CAP]
         o_keep[part, :] = mm(hidden, wd[e, :, mine])[:CAP]
         if e in O_PIECES:
-            chunk = slice(*O_PIECES[e])
-            o_copies.append(twin(o_send.at[chunk], o_recv.at[chunk], 13 if e == 0 else 3 + e // 2, 3))
-            o_copies[-1].start()
+            first, last, group = O_PIECES[e]
+            twin(o_send.at[first:last], o_recv.at[first:last], 3 + group, 3).start()
         if e == 5:
             out_across[3].wait_recv()
             forwards[3].start()
-    D_PIECES = {1: (0, 40), 3: (40, 80), 5: (80, 120), 6: (120, 136), 7: (136, 160)}
-    CHUNKS = (((0, 80), (80, 160)), ((0, 80), (80, 128), (128, 160)))
-    READY = ((3, 5), (2, 4, 5))
-    DIRECT = ((False, False), (False, False, True))
-
     def give_back(lane, chunk):
-        buf, keep, recv, copies = ((o_all, o_keep, o_recv, o_copies), (d_all, d_keep, d_recv, d_copies))[lane]
-        for copy in copies[READY[lane][chunk - 1] if chunk else 0 : READY[lane][chunk]]:
-            copy.wait_recv()
-        rows = slice(*CHUNKS[lane][chunk])
+        buf, keep, recv = ((o_all, o_keep, o_recv), (d_all, d_keep, d_recv))[lane]
+        landed(recv.at[slice(*LANDED[chunk])], y_recv_sem.at[3 + 3 * lane + chunk])
+        rows = slice(*CHUNKS[chunk])
         buf[me, rows] = (keep[rows, :] + recv[rows, :]).astype(BF16)
+        direct = chunk == 2
 
         def send(owner, k, j):
             view = buf.at[owner, rows]
             return pltpu.make_async_remote_copy(src_ref=view, dst_ref=view, send_sem=r_send_sem.at[lane], recv_sem=r_recv_sem.at[lane, chunk, j], device_id={"ep": jnp.bitwise_xor(me, k)}, device_id_type=MESH)
 
-        group = [send(me, 2, 0), send(me, 1, 1), send(me, 3, 2) if DIRECT[lane][chunk] else send(across, 1, 2)]
-        for copy in group if DIRECT[lane][chunk] else group[:2]:
+        group = [send(me, 2, 1 if direct else 0), send(me, 1, 1), send(me, 3, 1) if direct else send(across, 1, 1)]
+        for copy in group if direct else group[:2]:
             copy.start()
         return group
 
@@ -225,9 +228,10 @@
         group[0].wait_recv()
         group[2].start()
 
-    def arrived(group, forwarded):
-        for copy in group[1:] if forwarded else group:
-            copy.wait_recv()
+    def arrived(lane):
+        buf = (o_all, d_all)[lane]
+        for chunk, (first, last) in enumerate(CHUNKS):
+            landed(buf.at[: 3 if chunk == 2 else 2, first:last], r_recv_sem.at[lane, chunk, 1])
 
     @pl.when(me % 2 == 1)
     def forward_early():
@@ -251,9 +255,7 @@
         out_across[4].wait_recv()
         forwards[4].start()
 
-    for k in range(3, 5):
-        out_mate[k].wait_recv()
-        forwards[k].wait_recv()
+    landed(dy_all.at[:2], recv_sem.at[9])
     us[...] = (gate_slot * mm(pick_own[...], dy_all[...].reshape(total, DIM))).astype(BF16)
 
     for e in range(OWN):
@@ -265,13 +267,14 @@
         d_send[part, :] = (mm(d_gate, wg[e, theirs, :], NT) + mm(d_up, wu[e, theirs, :], NT))[:CAP]
         d_keep[part, :] = (mm(d_gate, wg[e, mine, :], NT) + mm(d_up, wu[e, mine, :], NT))[:CAP]
         if e in D_PIECES:
-            chunk = slice(*D_PIECES[e])
-            d_copies.append(twin(d_send.at[chunk], d_recv.at[chunk], 7 + len(d_copies), 4))
-            d_copies[-1].start()
+            first, last, group = D_PIECES[e]
+            twin(d_send.at[first:last], d_recv.at[first:last], 6 + group, 4).start()
         if e == 1:
             o_first = give_back(0, 0)
+        if e == 4:
+            o_second = give_back(0, 1)
         if e == 5:
-            o_second = give_back(0, 1)
+            give_back(0, 2)
 
 
     pass_on(o_first)
@@ -282,6 +285,9 @@
     dab_s[:, :WIDTH] = d_gate
     dab_s[:, WIDTH:] = d_up
 
+    h_copy.wait_recv()
+    landed(sd_twin.at[: 3 * (WIDTH // SHARDS)], q_recv_sem.at[0])
+    s_keep[...] += mm(hid_twin[...], sd_twin[...])
     x_half = x_all[me, :, mine].astype(F32)
     dy_half = dy_all[me, :, mine].astype(F32)
     gate_home = to_col(meta[2:3, home])
@@ -289,8 +295,7 @@
     pick = (lax.broadcasted_iota(jnp.int32, (TOK, SHARDS * SLOTS), 1) == flat_home).astype(F32).astype(BF16)
     d_first = give_back(1, 0)
     pass_on(o_second)
-    arrived(o_first, True)
-    arrived(o_second, True)
+    arrived(0)
     tok_out = mm(pick, o_all[...].reshape(SHARDS * SLOTS, HALF))
     dg_mine[...] = to_row(jnp.sum(dy_half * tok_out, axis=1, keepdims=True))
     place = side * SHARDS + me
@@ -298,14 +303,11 @@
     for copy in dg_copies:
         copy.start()
     dg_all[place] = dg_mine[...]
-    h_copy.wait_recv()
-    for copy in sd_spread:
-        copy.wait_recv()
-    y_out[:, mine] = (x_half + (s_keep[...] + mm(hid_twin[...], sd_twin[...])) + gate_home * tok_out).astype(BF16)
-    y_copy = twin(y_out.at[:, mine], y_out.at[:, mine], 12, 5)
+    y_out[:, mine] = (x_half + s_keep[...] + gate_home * tok_out).astype(BF16)
+    y_copy = twin(y_out.at[:, mine], y_out.at[:, mine], 9, 5)
     y_copy.start()
     d_second = give_back(1, 1)
-    d_third = give_back(1, 2)
+    give_back(1, 2)
     pass_on(d_first)
     pass_on(d_second)
     seven = pltpu.make_async_remote_copy(src_ref=dg_all.at[1:], dst_ref=dg_all.at[1:], send_sem=g_send_sem.at[0], recv_sem=g_recv_sem.at[0], device_id=to_twin, device_id_type=MESH)
@@ -319,9 +321,7 @@
     n_copy.wait_recv()
     d_normed = n_keep[...] + n_recv[...] + mm(d_logits_home, wr[:, mine], TN)
     gr_out[...] = mm(d_logits, n_all[...])
-    arrived(d_first, True)
-    arrived(d_second, True)
-    arrived(d_third, False)
+    arrived(1)
     dn_half[...] = d_normed + mm(pick, d_all[...].reshape(SHARDS * SLOTS, HALF))
     def sent(ref, sem):
         pltpu.make_async_remote_copy(src_ref=ref, dst_ref=ref, send_sem=sem, recv_sem=sem, device_id=to_twin, device_id_type=MESH).wait_send()
@@ -360,14 +360,14 @@
             pltpu.VMEM((SHARDS, TOK, DIM), BF16), pltpu.VMEM((SHARDS, 8, TOK), jnp.int32), pltpu.VMEM((EXPERTS, DIM), BF16),
             pltpu.VMEM((OWN, DIM, width), BF16), pltpu.VMEM((OWN, DIM, width), BF16), pltpu.VMEM((OWN, width, DIM), BF16),
             pltpu.VMEM((DIM, width), BF16), pltpu.VMEM((DIM, width), BF16), pltpu.VMEM((width, DIM), BF16),
-            pltpu.VMEM((rows, total), BF16),
+            pltpu.VMEM((rows, total), BF16), pltpu.VMEM((rows, DIM), F32),
             pltpu.VMEM((rows, width), F32), pltpu.VMEM((rows, width), F32),
             pltpu.VMEM((EXPERTS, total), F32), pltpu.VMEM((8, total), F32),
             pltpu.VMEM((TOK, width), BF16), pltpu.VMEM((TOK, width), BF16), pltpu.VMEM((width, HALF), BF16), half_f32, half_f32, half_f32, half_f32,
             slots_f32, slots_f32, slots_f32, slots_f32, slots_f32, slots_f32,
             pltpu.VMEM((SHARDS, SLOTS, HALF), BF16), pltpu.VMEM((SHARDS, SLOTS, HALF), BF16),
             pltpu.VMEM((8, TOK), F32), pltpu.VMEM((2 * SHARDS, 8, TOK), F32),
-            dma((8,)), dma((3,)), dma((3,)), dma((3, 5)), dma((2,)), dma((2, 3, 3)), dma((6,)), dma((14,)), dma((1,)), dma((1,)), dma((1,)), dma((3,)),
+            dma((8,)), dma((3,)), dma((3,)), dma((10,)), dma((2,)), dma((2, 3, 2)), dma((6,)), dma((10,)), dma((1,)), dma((1,)), dma((1,)), dma((1,)),
         ],
         compiler_params=pltpu.CompilerParams(collective_id=0, has_side_effects=True, vmem_limit_bytes=40 << 20),
         name="moe_layer",

time: 47.7 us -> 47.4 us (level)
  no operation moved by 1% of the time
where the time goes in v6:
time: 47.4 us; the launch traced here: 47.3 us
  Pallas kernels  45.1 us (95%)
  starting transfers between devices  1.45 us (3%)
  between operations  0.69 us (1%)
    pallas_call x1, Pallas kernels, layer_call(): pl.pallas_call(layer_kernel, out_shape=(shape((TOK, DIM), BF16), shape((T...  34.4 us
    pallas_call x1, Pallas kernels, grads_call(): pl.pallas_call(grads_kernel, out_shape=tuple((shape(dims, F32) for dims i...  9.77 us
    ppermute x1, starting transfers between devices, local_step(): dn_other = lax.ppermute(dn_half, 'etp', [(0, 1), (1, 0)])  1.45 us
    pallas_call x1, Pallas kernels, finish_call(): pl.pallas_call(finish_kernel, out_shape=jax.ShapeDtypeStruct((TOK, DIM),...  0.96 us
  transfers between devices with their start and end apart: 1, of which 0 were waited for; matrix products, arithmetic and copies ran while one was open for 0% of the time, Pallas kernels for 21%

profile of v6, /device:TPU:0, one launch (start us, length us, event | category | flops | bytes accessed | tf_op | source)
XLA Modules:
  0.0 47.3 jit_solution(15030244547620009015)
XLA Ops:
  0.6 34.4 %moe_layer.1 = (bf16[128,1024]{1,0:T(8,128)(2,1)S(1)}, f32[128,512]{1,0:T(8,128)S(1)}, f32[32,1024]{1,0:T(8,128)S(1)}, bf16[256,1024]{1,0:T(8,128)(2,1)S(1)}, bf...) custom-call(bf16[128,1024]{1,0:T(8,128)(2,1)} %x_ref.1, ...), custom_call_target="tpu_custom_call" | custom-call | tf_op jit(solution)/shard_map/moe_layer/pallas_call | solution.py:350
  35.1 1.4 %collective-permute-start = (f32[128,512]{1,0:T(8,128)S(1)}, f32[128,512]{1,0:T(8,128)S(1)}, u32[]{:S(2)}, u32[]{:S(2)}) collective-permute-start(f32[128,512]{1,0:T(8,128)S(1)} %get-tuple-element.39.dn_mine), channel_id=1, source_target_pairs={{0,4},{4,0},{1,5},{5,1},{2,6},{6,2},{3,7},{7,3}} | collective-permute-start | bytes 786440 | tf_op jit(solution)/shard_map/ppermute | solution.py:451
  36.5 0.0 copy-start
  36.5 0.0 copy-start.1
  36.5 9.8 %weight_grads.1 = (f32[8,1024,256]{2,1,0:T(8,128)}, f32[8,1024,256]{2,1,0:T(8,128)}, f32[8,256,1024]{2,1,0:T(8,128)}, f32[1024,256]{1,0:T(8,128)}, f32[1024,256]...) custom-call(bf16[256,1024]{1,0:T(8,128)(2,1)S(1)} %get-tuple-element.28.xs, ...), custom_call_target="tpu_custom_call" | custom-call | flops 8589934592 | bytes 33554432 | tf_op jit(solution)/shard_map/weight_grads/pallas_call | solution.py:408
  46.3 0.0 collective-permute-done.dn_recv
  46.3 0.0 copy-done
  46.3 0.0 copy-done.1
  46.3 1.0 %finish_tokens.1 = bf16[128,1024]{1,0:T(8,128)(2,1)} custom-call(bf16[128,1024]{1,0:T(8,128)(2,1)S(1)} %copy-done, bf16[128,1024]{1,0:T(8,128)(2,1)S(1)} %copy-done.1, f32[128,512]{1,0:T(8,128)S(1)} %get-tuple-element.39.dn_mine, f32[128,512]{1,0:T(8,128)S(1)} %collective-permute-done.dn_recv), custom_call_target="tpu_custom_call" | custom-call | tf_op jit(solution)/shard_map/finish_tokens/pallas_call | solution.py:433
Async XLA Ops:
  35.1 11.2 %collective-permute-start = (f32[128,512]{1,0:T(8,128)S(1)}, f32[128,512]{1,0:T(8,128)S(1)}, u32[]{:S(2)}, u32[]{:S(2)}) collective-permute-start(f32[128,512]{1,0:T(8,128)S(1)} %get-tuple-element.39.dn_mine), channel_id=1, source_target_pairs={{0,4},{4,0},{1,5},{5,1},{2,6},{6,2},{3,7},{7,3}} | collective-permute-start | bytes 786440 | tf_op jit(solution)/shard_map/ppermute | solution.py:451
  36.5 9.8 %copy-start = (bf16[128,1024]{1,0:T(8,128)(2,1)S(1)}, bf16[128,1024]{1,0:T(8,128)(2,1)}, u32[]{:S(2)}) copy-start(bf16[128,1024]{1,0:T(8,128)(2,1)} %x_ref.1) | copy-start | bytes 786436
  36.5 9.8 %copy-start.1 = (bf16[128,1024]{1,0:T(8,128)(2,1)S(1)}, bf16[128,1024]{1,0:T(8,128)(2,1)}, u32[]{:S(2)}) copy-start(bf16[128,1024]{1,0:T(8,128)(2,1)} %dy_ref.1) | copy-start | bytes 786436

commit v7 on v6

--- a/solution.py
+++ b/solution.py
@@ -64,7 +64,7 @@
                  x_all, ids_all, wr, wg, wu, wd, sg, su, sd, pick_own, xs_sum, acts, acts_up,
                  probs, meta, hid_own, hid_twin, sd_twin, s_keep, n_send, n_recv, n_keep, o_send, o_recv, o_keep, d_send, d_recv, d_keep,
                  o_all, d_all, dg_mine, dg_all,
-                 in_sem, w_sem, send_sem, recv_sem, r_send_sem, r_recv_sem, y_send_sem, y_recv_sem, g_send_sem, g_recv_sem, q_send_sem, q_recv_sem):
+                 in_sem, w_sem, send_sem, recv_sem, r_send_sem, r_recv_sem, y_send_sem, y_recv_sem, g_send_sem, g_recv_sem, q_send_sem, q_recv_sem, step_sem):
     me = lax.axis_index("ep")
     side = lax.axis_index("etp")
     total = SHARDS * TOK
@@ -82,7 +82,14 @@
     for load in loads:
         load.start()
     w_loads = [pltpu.make_async_copy(src, dst, w_sem.at[k]) for k, (src, dst) in enumerate(((wg_hbm, wg), (wu_hbm, wu), (wd_hbm, wd)))]
-    barrier(others)
+    near = (to_mate, to_across, to_twin)
+    barrier(near)
+
+    def relay(k):
+        for peer in near:
+            pl.semaphore_signal(step_sem.at[k], inc=1, device_id=peer, device_id_type=MESH)
+
+    relay(0)
 
     def remote(view, lane, k, target):
         return pltpu.make_async_remote_copy(src_ref=view, dst_ref=view, send_sem=send_sem.at[(k + 1) // 2], recv_sem=recv_sem.at[k if lane == 0 else (4 + lane, 6 + lane, 9)[(k + 1) // 2]], device_id=target, device_id_type=MESH)
@@ -163,6 +170,8 @@
     target = jnp.where(owned, local * PAD + slot, -1)
     pick_own[...] = (lax.broadcasted_iota(jnp.int32, (OWN * PAD, total), 0) == target).astype(F32).astype(BF16)
 
+    pl.semaphore_wait(step_sem.at[0], 3)
+    relay(1)
     sd_copy.wait_recv()
     view = sd_twin.at[quarter(me)]
     sd_spread = [pltpu.make_async_remote_copy(src_ref=view, dst_ref=view, send_sem=q_send_sem.at[0], recv_sem=q_recv_sem.at[0], device_id={"ep": jnp.bitwise_xor(me, k)}, device_id_type=MESH) for k in range(1, SHARDS)]
@@ -299,6 +308,7 @@
     tok_out = mm(pick, o_all[...].reshape(SHARDS * SLOTS, HALF))
     dg_mine[...] = to_row(jnp.sum(dy_half * tok_out, axis=1, keepdims=True))
     place = side * SHARDS + me
+    pl.semaphore_wait(step_sem.at[1], 3)
     dg_copies = [pltpu.make_async_remote_copy(src_ref=dg_mine, dst_ref=dg_all.at[place], send_sem=g_send_sem.at[0], recv_sem=g_recv_sem.at[0], device_id=other, device_id_type=MESH) for other in others]
     for copy in dg_copies:
         copy.start()
@@ -367,7 +377,7 @@
             slots_f32, slots_f32, slots_f32, slots_f32, slots_f32, slots_f32,
             pltpu.VMEM((SHARDS, SLOTS, HALF), BF16), pltpu.VMEM((SHARDS, SLOTS, HALF), BF16),
             pltpu.VMEM((8, TOK), F32), pltpu.VMEM((2 * SHARDS, 8, TOK), F32),
-            dma((8,)), dma((3,)), dma((3,)), dma((10,)), dma((2,)), dma((2, 3, 2)), dma((6,)), dma((10,)), dma((1,)), dma((1,)), dma((1,)), dma((1,)),
+            dma((8,)), dma((3,)), dma((3,)), dma((10,)), dma((2,)), dma((2, 3, 2)), dma((6,)), dma((10,)), dma((1,)), dma((1,)), dma((1,)), dma((1,)), pltpu.SemaphoreType.REGULAR((2,)),
         ],
         compiler_params=pltpu.CompilerParams(collective_id=0, has_side_effects=True, vmem_limit_bytes=40 << 20),
         name="moe_layer",

time: 47.4 us -> 46.7 us (0.985)
  starting transfers between devices: 1.45 us -> 0.73 us
    ppermute x1, starting transfers between devices: 1.45 us -> 0.73 us  [local_step(): dn_other = lax.ppermute(dn_half, 'etp', [(0, 1), (1, 0)])]
where the time goes in v7:
time: 46.7 us; the launch traced here: 46.6 us
  Pallas kernels  45.2 us (97%)
  starting transfers between devices  0.73 us (2%)
  between operations  0.69 us (1%)
    pallas_call x1, Pallas kernels, layer_call(): pl.pallas_call(layer_kernel, out_shape=(shape((TOK, DIM), BF16), shape((T...  34.5 us
    pallas_call x1, Pallas kernels, grads_call(): pl.pallas_call(grads_kernel, out_shape=tuple((shape(dims, F32) for dims i...  9.77 us
    pallas_call x1, Pallas kernels, finish_call(): pl.pallas_call(finish_kernel, out_shape=jax.ShapeDtypeStruct((TOK, DIM),...  0.96 us
  transfers between devices with their start and end apart: 1, of which 0 were waited for; matrix products, arithmetic and copies ran while one was open for 0% of the time, Pallas kernels for 21%

profile of v7, /device:TPU:0, one launch (start us, length us, event | category | flops | bytes accessed | tf_op | source)
XLA Modules:
  0.0 46.6 jit_solution(16263855935824670558)
XLA Ops:
  0.6 34.5 %moe_layer.1 = (bf16[128,1024]{1,0:T(8,128)(2,1)S(1)}, f32[128,512]{1,0:T(8,128)S(1)}, f32[32,1024]{1,0:T(8,128)S(1)}, bf16[256,1024]{1,0:T(8,128)(2,1)S(1)}, bf...) custom-call(bf16[128,1024]{1,0:T(8,128)(2,1)} %x_ref.1, ...), custom_call_target="tpu_custom_call" | custom-call | tf_op jit(solution)/shard_map/moe_layer/pallas_call | solution.py:360
  35.1 0.7 %collective-permute-start = (f32[128,512]{1,0:T(8,128)S(1)}, f32[128,512]{1,0:T(8,128)S(1)}, u32[]{:S(2)}, u32[]{:S(2)}) collective-permute-start(f32[128,512]{1,0:T(8,128)S(1)} %get-tuple-element.39.dn_mine), channel_id=1, source_target_pairs={{0,4},{4,0},{1,5},{5,1},{2,6},{6,2},{3,7},{7,3}} | collective-permute-start | bytes 786440 | tf_op jit(solution)/shard_map/ppermute | solution.py:461
  35.9 0.0 copy-start
  35.9 0.0 copy-start.1
  35.9 9.8 %weight_grads.1 = (f32[8,1024,256]{2,1,0:T(8,128)}, f32[8,1024,256]{2,1,0:T(8,128)}, f32[8,256,1024]{2,1,0:T(8,128)}, f32[1024,256]{1,0:T(8,128)}, f32[1024,256]...) custom-call(bf16[256,1024]{1,0:T(8,128)(2,1)S(1)} %get-tuple-element.28.xs, ...), custom_call_target="tpu_custom_call" | custom-call | flops 8589934592 | bytes 33554432 | tf_op jit(solution)/shard_map/weight_grads/pallas_call | solution.py:418
  45.6 0.0 collective-permute-done.dn_recv
  45.6 0.0 copy-done
  45.7 0.0 copy-done.1
  45.7 1.0 %finish_tokens.1 = bf16[128,1024]{1,0:T(8,128)(2,1)} custom-call(bf16[128,1024]{1,0:T(8,128)(2,1)S(1)} %copy-done, bf16[128,1024]{1,0:T(8,128)(2,1)S(1)} %copy-done.1, f32[128,512]{1,0:T(8,128)S(1)} %get-tuple-element.39.dn_mine, f32[128,512]{1,0:T(8,128)S(1)} %collective-permute-done.dn_recv), custom_call_target="tpu_custom_call" | custom-call | tf_op jit(solution)/shard_map/finish_tokens/pallas_call | solution.py:443
Async XLA Ops:
  35.1 10.5 %collective-permute-start = (f32[128,512]{1,0:T(8,128)S(1)}, f32[128,512]{1,0:T(8,128)S(1)}, u32[]{:S(2)}, u32[]{:S(2)}) collective-permute-start(f32[128,512]{1,0:T(8,128)S(1)} %get-tuple-element.39.dn_mine), channel_id=1, source_target_pairs={{0,4},{4,0},{1,5},{5,1},{2,6},{6,2},{3,7},{7,3}} | collective-permute-start | bytes 786440 | tf_op jit(solution)/shard_map/ppermute | solution.py:461
  35.9 9.8 %copy-start = (bf16[128,1024]{1,0:T(8,128)(2,1)S(1)}, bf16[128,1024]{1,0:T(8,128)(2,1)}, u32[]{:S(2)}) copy-start(bf16[128,1024]{1,0:T(8,128)(2,1)} %x_ref.1) | copy-start | bytes 786436
  35.9 9.8 %copy-start.1 = (bf16[128,1024]{1,0:T(8,128)(2,1)S(1)}, bf16[128,1024]{1,0:T(8,128)(2,1)}, u32[]{:S(2)}) copy-start(bf16[128,1024]{1,0:T(8,128)(2,1)} %dy_ref.1) | copy-start | bytes 786436
